TPU v7x, 32 devices: a whole 2x2x4 slice. The times are simulated.
32 devices in a mesh: etp: 4 (over z), ep: 8 (over y, x, core).
Axes of the slice: x: 2, y: 2, z: 4, core: 2. Of those that a mesh axis runs over, the one named last changes fastest.
Arguments:
- hidden: bfloat16 [16384, 1024], P(('ep', 'etp'))
- w_router: float32 [1024, 8], replicated
- expert_ids: int32 [16384, 2], P(('ep', 'etp'))
- d_out: bfloat16 [16384, 1024], P(('ep', 'etp'))
- w_gate: bfloat16 [8, 1024, 7168], P('ep', None, 'etp')
- w_up: bfloat16 [8, 1024, 7168], P('ep', None, 'etp')
- w_down: bfloat16 [8, 7168, 1024], P('ep', 'etp')
Outputs:
- output 1: bfloat16 [16384, 1024], P(('ep', 'etp'))
- output 2: bfloat16 [16384, 1024], P(('ep', 'etp'))
- output 3: float32 [1024, 8], replicated
- output 4: float32 [], replicated
- output 5: float32 [8, 1024, 7168], P('ep', None, 'etp')
- output 6: float32 [8, 1024, 7168], P('ep', None, 'etp')
- output 7: float32 [8, 7168, 1024], P('ep', 'etp')
All inputs are finite; a program needn't handle non-finite values.
Results may differ from a plain program's by a relative error of at most 0.00896172.
Values are sent between devices in bfloat16 or wider.
A program may use at most 1 GiB of HBM per device.

v0:
```python
import functools
import jax
import jax.numpy as jnp
from jax import lax
from jax.sharding import PartitionSpec as P

AUX_COEF = 0.01
OUT_SCALE = 2.0


def route_terms(logits, expert_ids):
    prob_vals = jax.nn.softmax(logits, axis=-1)
    picked = jnp.take_along_axis(prob_vals, expert_ids, axis=1)
    return picked / jnp.sum(picked, axis=1, keepdims=True), jnp.sum(prob_vals, axis=0)


def solution(mesh):
    ep_size = mesh.shape["ep"]
    etp_size = mesh.shape["etp"]
    n_dev = ep_size * etp_size
    all_axes = ("ep", "etp")
    tok_spec = P(all_axes, None)
    gate_spec = P("ep", None, "etp")
    down_spec = P("ep", "etp", None)

    def layer(hidden, w_router, expert_ids, d_out, w_gate, w_up, w_down):
        tok_rows, d_model = hidden.shape
        n_experts = w_router.shape[1]
        n_tokens = tok_rows * n_dev
        n_assign = 2 * tok_rows
        capacity = (5 * n_tokens + 2 * n_experts - 1) // (2 * n_experts)
        per_expert = 7 * tok_rows // (2 * n_experts)
        block_idx = lax.axis_index("ep") * etp_size + lax.axis_index("etp")

        hidden_f = hidden.astype(jnp.float32)
        logits = jnp.dot(hidden_f, w_router, preferred_element_type=jnp.float32)
        (gate_vals, prob_sum), route_vjp = jax.vjp(functools.partial(route_terms, expert_ids=expert_ids), logits)

        flat_ids = expert_ids.reshape(-1)
        one_hot = (flat_ids[:, None] == jnp.arange(n_experts, dtype=jnp.int32)[None, :]).astype(jnp.int32)
        local_pos = jnp.sum((jnp.cumsum(one_hot, axis=0) - one_hot) * one_hot, axis=1)
        count_table = lax.all_gather(jnp.sum(one_hot, axis=0), all_axes)
        earlier = (jnp.arange(n_dev) < block_idx)[:, None]
        prefix = jnp.sum(jnp.where(earlier, count_table, 0), axis=0)
        total_count = jnp.sum(count_table, axis=0)
        kept_mask = prefix[flat_ids] + local_pos < capacity
        dest_rows = jnp.where(kept_mask, flat_ids * per_expert + local_pos, n_experts * per_expert)
        source = jnp.full((n_experts * per_expert,), n_assign, jnp.int32).at[dest_rows].set(jnp.arange(n_assign, dtype=jnp.int32), mode="drop")

        def dispatch(values, row_index):
            send_buf = jnp.take(values, row_index, axis=0, mode="fill", fill_value=0).reshape(n_experts, per_expert, d_model)
            received = lax.all_to_all(send_buf, "ep", 0, 1, tiled=True)
            return lax.all_gather(received, "etp", axis=1, tiled=True)

        def combine(part_out):
            summed = lax.psum_scatter(part_out, "etp", scatter_dimension=1, tiled=True).astype(jnp.bfloat16)
            returned = lax.all_to_all(summed, "ep", 1, 0, tiled=True).reshape(n_experts * per_expert, d_model)
            return jnp.take(returned, dest_rows, axis=0, mode="fill", fill_value=0).reshape(tok_rows, 2, d_model)

        x_in = dispatch(hidden, source // 2)
        act_a = jnp.einsum("erd,edf->erf", x_in, w_gate, preferred_element_type=jnp.float32)
        act_b = jnp.einsum("erd,edf->erf", x_in, w_up, preferred_element_type=jnp.float32)
        sig_a = jax.nn.sigmoid(act_a)
        silu_a = act_a * sig_a
        inner_act = (silu_a * act_b).astype(jnp.bfloat16)
        y_pair = combine(jnp.einsum("erf,efd->erd", inner_act, w_down, preferred_element_type=jnp.float32))

        d_mix = OUT_SCALE * d_out.astype(jnp.float32)
        output = (hidden_f + OUT_SCALE * jnp.sum(gate_vals[:, :, None] * y_pair, axis=1)).astype(jnp.bfloat16)
        d_gates = jnp.sum(d_mix[:, None, :] * y_pair, axis=2)
        dy_assign = (gate_vals[:, :, None] * d_mix[:, None, :]).astype(jnp.bfloat16).reshape(n_assign, d_model)
        dy_in = dispatch(dy_assign, source)
        d_inner = jnp.einsum("erd,efd->erf", dy_in, w_down, preferred_element_type=jnp.float32)
        d_act_a = (d_inner * act_b * sig_a * (1.0 + act_a * (1.0 - sig_a))).astype(jnp.bfloat16)
        d_act_b = (d_inner * silu_a).astype(jnp.bfloat16)
        dx_part = jnp.einsum("erf,edf->erd", d_act_a, w_gate, preferred_element_type=jnp.float32) + jnp.einsum("erf,edf->erd", d_act_b, w_up, preferred_element_type=jnp.float32)
        dx_pair = combine(dx_part)
        g_gate = jnp.einsum("erd,erf->edf", x_in, d_act_a, preferred_element_type=jnp.float32)
        g_up = jnp.einsum("erd,erf->edf", x_in, d_act_b, preferred_element_type=jnp.float32)
        g_down = jnp.einsum("erf,erd->efd", inner_act, dy_in, preferred_element_type=jnp.float32)

        route_frac = total_count.astype(jnp.float32) / (2 * n_tokens)
        mean_prob = lax.psum(prob_sum, all_axes) / n_tokens
        aux_loss = AUX_COEF * n_experts * jnp.sum(route_frac * mean_prob)
        (d_logits,) = route_vjp((d_gates, (AUX_COEF * n_experts / n_tokens) * route_frac))
        d_router = lax.psum(jnp.einsum("td,te->de", hidden_f, d_logits, preferred_element_type=jnp.float32), all_axes)
        d_hidden = (d_out.astype(jnp.float32) + jnp.sum(dx_pair, axis=1, dtype=jnp.float32) + jnp.einsum("te,de->td", d_logits, w_router, preferred_element_type=jnp.float32)).astype(jnp.bfloat16)
        return output, d_hidden, d_router, aux_loss, g_gate, g_up, g_down

    return jax.shard_map(layer, mesh=mesh, in_specs=(tok_spec, P(), tok_spec, tok_spec, gate_spec, gate_spec, down_spec), out_specs=(tok_spec, tok_spec, P(), P(), gate_spec, gate_spec, down_spec), check_vma=False)
```

profile of v0, /device:TPU:0, one launch (start us, length us, event | category | flops | bytes accessed | tf_op | source)
XLA Modules:
  0.0 1946.6 jit_solution(9975734876032999823)
XLA Ops:
  13.8 41.9 %all-reduce = s32[256]{0:T(256)S(1)} all-reduce(s32[256]{0:T(256)S(1)} %dynamic-update-slice), channel_id=2, replica_groups=mesh['etp'=4,'ep'=8] {'ep','etp'}, use_global_device_ids=true, to_apply=%add | all-reduce | flops 256 | bytes 2048
  76.2 46.8 %all_to_all.42 = bf16[8,224,1024]{2,1,0:T(8,128)(2,1)} all-to-all(bf16[8,224,1024]{2,1,0:T(8,128)(2,1)S(1)} %broadcast_select_fusion.1), channel_id=1, replica_groups=mesh['etp'=4,'ep'=8] {'ep'}, dimensions={0} | all-to-all | bytes 7340032 | tf_op jit(solution)/shard_map/all_to_all | solution.py:52
  153.7 46.6 %all_to_all.43 = bf16[8,224,1024]{2,1,0:T(8,128)(2,1)} all-to-all(bf16[8,224,1024]{2,1,0:T(8,128)(2,1)S(1)} %broadcast_select_fusion), channel_id=1, replica_groups=mesh['etp'=4,'ep'=8] {'ep'}, dimensions={0} | all-to-all | bytes 7340032 | tf_op jit(solution)/shard_map/all_to_all | solution.py:52
  200.5 174.0 %all-gather.4.cloned.1.call-done = bf16[1,7168,1024]{2,1,0:T(8,128)(2,1)} async-done(((bf16[1,1792,1024]{2,1,0:T(8,128)(2,1)}), bf16[1,7168,1024]{2,1,0:T(8,128)(2,1)}) %all-gather.4.cloned.1.call-update) | async-done | bytes 14680080 | tf_op jit(solution)/shard_map/all_gather | solution.py:53
  374.5 35.3 %fusion.11 = f32[7168,1792]{1,0:T(8,128)} fusion(bf16[1,7168,1024]{2,1,0:T(8,128)(2,1)} %all-gather.4.cloned.1.call-done, bf16[1,1024,1792]{2,1,0:T(8,128)(2,1)} %param.13), kind=kOutput, calls=%fused_computation.24 | convolution fusion | flops 26306674688 | bytes 69730304 | tf_op jit(solution)/shard_map/erd,edf->erf/dot_general | solution.py:61
  409.8 33.7 %fusion.9 = f32[7168,1792]{1,0:T(8,128)} fusion(bf16[1,7168,1024]{2,1,0:T(8,128)(2,1)S(1)} %copy-done.37, bf16[1,1024,1792]{2,1,0:T(8,128)(2,1)} %param.14), kind=kOutput, calls=%fused_computation.22 | convolution fusion | flops 26306674688 | bytes 69730304 | tf_op jit(solution)/shard_map/erd,edf->erf/dot_general | solution.py:62
  443.5 184.0 %all-gather.6.cloned.1.call-done = bf16[1,7168,1024]{2,1,0:T(8,128)(2,1)} async-done(((bf16[1,1792,1024]{2,1,0:T(8,128)(2,1)}), bf16[1,7168,1024]{2,1,0:T(8,128)(2,1)}) %all-gather.6.cloned.1.call-update) | async-done | bytes 14680080 | tf_op jit(solution)/shard_map/all_gather | solution.py:53
  627.5 77.6 %multiply_convert_fusion = (bf16[7168,1792]{1,0:T(8,128)(2,1)}, bf16[7168,1792]{1,0:T(8,128)(2,1)}, bf16[7168,1792]{1,0:T(8,128)(2,1)}) fusion(f32[7168,1792]{1,0:T(8,128)} %fusion.11, f32[7168,1792]{1,0:T(8,128)} %fusion.9, bf16[1,1792,1024]{2,1,0:T(8,128)(2,1)} %param.15, bf16[1,7168,1024]{2,1,0:T(8,128)(2,1)} %all-gather.6.cloned.1.call-done), kind=kOutput, calls=%fused_computation.7 | convolution fusion | flops 26499350528 | bytes 198180864 | tf_op jit(solution)/shard_map/erd,efd->erf/dot_general | solution.py:73
  705.1 33.7 %convolution_bitcast_fusion = f32[1,7168,1024]{2,1,0:T(8,128)} fusion(bf16[7168,1792]{1,0:T(8,128)(2,1)} %get-tuple-element.24, bf16[1,1792,1024]{2,1,0:T(8,128)(2,1)} %param.15), kind=kOutput, calls=%fused_computation.13 | convolution fusion | flops 26306674688 | bytes 58720256 | tf_op jit(solution)/shard_map/erf,efd->erd/dot_general | solution.py:66
  738.8 34.0 %fusion.26 = f32[7168,1024]{1,0:T(8,128)} fusion(bf16[7168,1792]{1,0:T(8,128)(2,1)} %get-tuple-element.23, bf16[1,1024,1792]{2,1,0:T(8,128)(2,1)} %param.13), kind=kOutput, calls=%fused_computation.38 | convolution fusion | flops 26306674688 | bytes 58720256 | tf_op jit(solution)/shard_map/erf,edf->erd/dot_general | solution.py:76
  772.8 37.4 %add_bitcast_fusion = f32[1,7168,1024]{2,1,0:T(8,128)} fusion(f32[7168,1024]{1,0:T(8,128)} %fusion.26, bf16[7168,1792]{1,0:T(8,128)(2,1)} %get-tuple-element.22, bf16[1,1024,1792]{2,1,0:T(8,128)(2,1)} %param.14), kind=kOutput, calls=%fused_computation.12 | convolution fusion | flops 26314014720 | bytes 88080384 | tf_op jit(solution)/shard_map/erf,edf->erd/dot_general | solution.py:76
  812.2 34.7 %fusion.19 = f32[1,1792,1024]{2,1,0:T(8,128)} fusion(bf16[7168,1792]{1,0:T(8,128)(2,1)} %get-tuple-element.24, bf16[1,7168,1024]{2,1,0:T(8,128)(2,1)} %all-gather.6.cloned.1.call-done), kind=kOutput, calls=%fused_computation.28 | convolution fusion | flops 26306674688 | bytes 47710208 | tf_op jit(solution)/shard_map/erf,erd->efd/dot_general | solution.py:80
  846.9 371.5 %reduce-scatter.3.cloned.1.call-done = f32[1,1792,1024]{2,1,0:T(8,128)} async-done(((f32[1,7168,1024]{2,1,0:T(8,128)}), f32[1,1792,1024]{2,1,0:T(8,128)}) %reduce-scatter.3.cloned.1.call-update) | async-done | bytes 7340048 | tf_op jit(solution)/shard_map/reduce_scatter | solution.py:56
  1222.1 25.2 %copy.87 = bf16[1,1792,1024]{2,0,1:T(2,128)(2,1)} copy(bf16[1,1792,1024]{2,1,0:T(8,128)(2,1)S(1)} %convert_element_type.65) | data formatting | bytes 7340032 | tf_op jit(solution)/shard_map/convert_element_type | solution.py:56
  1247.9 23.1 %reduce.10 = bf16[1792,1024]{1,0:T(8,128)(2,1)} reduce(bf16[1792,1,1024]{2,1,0:T(2,128)(2,1)} %bitcast.123, bf16[]{:T(256)} %broadcast.297), dimensions={1}, to_apply=%bitcast.118.reduce_sub_computation | reduce | bytes 7340034
  1283.4 34.8 %fusion.13 = f32[1,1024,1792]{2,1,0:T(8,128)} fusion(bf16[7168,1792]{1,0:T(8,128)(2,1)} %get-tuple-element.23, bf16[1,7168,1024]{2,1,0:T(8,128)(2,1)} %all-gather.4.cloned.1.call-done), kind=kOutput, calls=%fused_computation.26 | convolution fusion | flops 26306674688 | bytes 47710208 | tf_op jit(solution)/shard_map/erd,erf->edf/dot_general | solution.py:78
  1318.1 385.3 %reduce-scatter.5.cloned.1.call-done = f32[1,1792,1024]{2,1,0:T(8,128)} async-done(((f32[1,7168,1024]{2,1,0:T(8,128)}), f32[1,1792,1024]{2,1,0:T(8,128)}) %reduce-scatter.5.cloned.1.call-update) | async-done | bytes 7340048 | tf_op jit(solution)/shard_map/reduce_scatter | solution.py:56
  1707.0 25.2 %copy.86 = bf16[1,1792,1024]{2,0,1:T(2,128)(2,1)} copy(bf16[1,1792,1024]{2,1,0:T(8,128)(2,1)S(1)} %convert_element_type.73) | data formatting | bytes 7340032 | tf_op jit(solution)/shard_map/convert_element_type | solution.py:56
  1732.3 23.0 %reduce.9 = bf16[1792,1024]{1,0:T(8,128)(2,1)} reduce(bf16[1792,1,1024]{2,1,0:T(2,128)(2,1)} %bitcast.124, bf16[]{:T(256)} %broadcast.297), dimensions={1}, to_apply=%bitcast.117.reduce_sub_computation | reduce | bytes 7340034
  1767.4 34.8 %fusion.16 = f32[1,1024,1792]{2,1,0:T(8,128)} fusion(bf16[7168,1792]{1,0:T(8,128)(2,1)} %get-tuple-element.22, bf16[1,7168,1024]{2,1,0:T(8,128)(2,1)} %all-gather.4.cloned.1.call-done), kind=kOutput, calls=%fused_computation.27 | convolution fusion | flops 26306674688 | bytes 47710208 | tf_op jit(solution)/shard_map/erd,erf->edf/dot_general | solution.py:79
  1802.2 8.3 reshape.401
  1835.5 42.2 %all-reduce.1 = (f32[1024,8]{0,1:T(8,128)}, f32[8]{0:T(128)S(1)}) all-reduce(f32[1024,8]{0,1:T(8,128)S(1)} %convolution_bitcast_fusion.1, f32[8]{0:T(128)S(1)} %copy-done.32), channel_id=1, replica_groups=mesh['etp'=4,'ep'=8] {'ep','etp'}, use_global_device_ids=true, to_apply=%region_18.20 | all-reduce | flops 8200 | bytes 65600 | tf_op jit(solution)/shard_map/psum | solution.py:86
  1878.3 8.3 reshape.403
  1893.1 8.7 gather_fusion.4
  (182 shorter events, 159.2 us)
Async XLA Ops:
  7.2 116.2 %copy-start = (f32[1024,8]{0,1:T(8,128)S(1)}, f32[1024,8]{0,1:T(8,128)}, u32[]{:S(2)}) copy-start(f32[1024,8]{0,1:T(8,128)} %param.10) | copy-start | bytes 98308
  7.2 60.0 %copy-start.1 = (bf16[512,1024]{1,0:T(8,128)(2,1)S(1)}, bf16[512,1024]{1,0:T(8,128)(2,1)}, u32[]{:S(2)}) copy-start(bf16[512,1024]{1,0:T(8,128)(2,1)} %param.9) | copy-start | bytes 3145732
  7.2 367.3 %all-gather.4.cloned.1.call-start = ((), (), s32[]{:S(2)}) async-start(), calls=%async_computation.6 | async-start | bytes 18350080 | tf_op jit(solution)/shard_map/all_gather | solution.py:53
  8.5 65.3 %copy-start.14 = (s32[1024]{0:T(1024)}, s32[1024]{0:T(1024)S(1)}, u32[]{:S(2)}) copy-start(s32[1024]{0:T(1024)S(1)} %eq.25) | copy-start | bytes 12292
  11.6 62.2 %copy-start.16 = (s32[1024]{0:T(1024)}, s32[1024]{0:T(1024)S(1)}, u32[]{:S(2)}) copy-start(s32[1024]{0:T(1024)S(1)} %get-tuple-element.11) | copy-start | bytes 12292
  62.7 11.1 copy-start.25
  76.1 46.9 %copy-start.12 = (s32[512,2]{0,1:T(2,128)S(1)}, s32[512,2]{0,1:T(2,128)}, u32[]{:S(2)}) copy-start(s32[512,2]{0,1:T(2,128)} %param.11) | copy-start | bytes 12292
  122.9 504.5 %all-gather.6.cloned.1.call-start = ((), (), s32[]{:S(2)}) async-start(), calls=%async_computation.8 | async-start | bytes 18350080 | tf_op jit(solution)/shard_map/all_gather | solution.py:53
  124.5 7.8 copy-start.5
  200.3 1018.2 %reduce-scatter.3.cloned.1.call-start = ((), (), s32[]{:S(2)}) async-start(), calls=%async_computation.7 | async-start | bytes 36700160 | tf_op jit(solution)/shard_map/reduce_scatter | solution.py:56
  374.5 35.3 %copy-start.37 = (bf16[1,7168,1024]{2,1,0:T(8,128)(2,1)S(1)}, bf16[1,7168,1024]{2,1,0:T(8,128)(2,1)}, u32[]{:S(2)}) copy-start(bf16[1,7168,1024]{2,1,0:T(8,128)(2,1)} %all-gather.4.cloned.1.call-done) | copy-start | bytes 44040196
  738.8 964.6 %reduce-scatter.5.cloned.1.call-start = ((), (), s32[]{:S(2)}) async-start(), calls=%async_computation.9 | async-start | bytes 36700160 | tf_op jit(solution)/shard_map/reduce_scatter | solution.py:56
  812.2 1004.6 %copy-start.21 = (s32[1024]{0:T(1024)}, s32[1024]{0:T(1024)S(1)}, u32[]{:S(2)}) copy-start(s32[1024]{0:T(1024)S(1)} %broadcast_clamp_fusion) | copy-start | bytes 12292
  1278.4 484.5 %all-to-all-start.1 = ((bf16[8,2,114688]{2,1,0:T(2,128)(2,1)}), bf16[8,2,114688]{2,1,0:T(2,128)(2,1)}, u32[]{:S(2)}, u32[]{:S(2)}) async-start(bf16[8,2,114688]{2,1,0:T(2,128)(2,1)} %reshape.400), calls=%async_computation.2 | async-start | bytes 7340032 | tf_op jit(solution)/shard_map/all_to_all | solution.py:57
  1762.9 115.4 %all-to-all-start.3 = ((bf16[8,2,114688]{2,1,0:T(2,128)(2,1)}), bf16[8,2,114688]{2,1,0:T(2,128)(2,1)}, u32[]{:S(2)}, u32[]{:S(2)}) async-start(bf16[8,2,114688]{2,1,0:T(2,128)(2,1)} %reshape.402), calls=%async_computation.5 | async-start | bytes 7340032 | tf_op jit(solution)/shard_map/all_to_all | solution.py:57
  1816.8 7.5 copy-start.29
  1828.8 6.4 copy-start.9
  1828.8 6.4 copy-start.2
  1828.8 6.4 copy-start.20
  1828.8 6.7 copy-start.32
  1828.8 48.9 %copy-start.34 = (s32[8]{0:T(128)S(1)}, s32[8]{0:T(128)}, u32[]{:S(2)}) copy-start(s32[8]{0:T(128)} %get-tuple-element.8) | copy-start | bytes 100
  1886.6 6.5 copy-start.22
  1893.1 8.7 copy-start.4
  1893.1 8.7 copy-start.30
  (20 other events, 46.1 us)
Sparse Core Ops, SparseCore 0:
  123.1 251.3 all-gather.3
  376.1 251.3 all-gather.5
  738.9 479.5 reduce-scatter.2
  1220.7 482.6 reduce-scatter.4
where the time goes:
time: 1960 us; the launch traced here: 1950 us
  waiting for transfers between devices  1110 us (57%)
  matrix products  359 us (18%)
  blocking collectives  177 us (9%)
  local copies, waits for them, and re-layouts  164 us (8%)
  other arithmetic  103 us (5%)
    reduce_scatter x2, waiting for transfers between devices, combine(): lax.psum_scatter(part_out, 'etp', scatter_dimension=1, tiled=True)  757 us
    all_gather x2, waiting for transfers between devices, dispatch(): return lax.all_gather(received, 'etp', axis=1, tiled=True)  358 us
    all_to_all x2, blocking collectives, dispatch(): received = lax.all_to_all(send_buf, 'ep', 0, 1, tiled=True)  93.3 us
    dot_general x1, matrix products, layer(): jnp.einsum('erd,efd->erf', dy_in, w_down, preferred_element_type=jnp.floa...  77.6 us
    unnamed x7, other arithmetic  52.6 us
    convert_element_type x2, local copies, waits for them, and re-layouts, combine(): lax.psum_scatter(part_out, 'etp', scatter_dimension=1, tiled=True)  50.4 us
    unnamed x91, local copies, waits for them, and re-layouts  49.1 us
    psum x1, blocking collectives, layer(): lax.psum(jnp.einsum('td,te->de', hidden_f, d_logits, preferred_element_ty...  42.2 us
  transfers between devices with their start and end apart: 6, of which 4 were waited for; matrix products, arithmetic and copies ran while one was open for 22% of the time, Pallas kernels for 0%

commit v1 on v0

v1 whole, which is shorter than its diff:
```python
import functools
import jax
import jax.numpy as jnp
from jax import lax
from jax.experimental import pallas as pl
from jax.experimental.pallas import tpu as pltpu
from jax.sharding import PartitionSpec as P


AUX_COEF = 0.01
OUT_SCALE = 2.0
ALL_AXES = ("ep", "etp")
BF16 = jnp.bfloat16
F32 = jnp.float32
MIB = 1 << 20
FF_STEP = 256

NEXT_PAIRS = (1, 0, 3, 2)
ENDS_PAIRS = (3, 2, 1, 0)


def mm(lhs, rhs):
    return jnp.dot(lhs, rhs, preferred_element_type=F32)


def mm_nt(lhs, rhs):
    return lax.dot_general(lhs, rhs, (((1,), (1,)), ((), ())), preferred_element_type=F32)


def mm_tn(lhs, rhs):
    return lax.dot_general(lhs, rhs, (((0,), (0,)), ((), ())), preferred_element_type=F32)


def params(vmem_mib, dims=1):
    return pltpu.CompilerParams(dimension_semantics=("arbitrary",) * dims, vmem_limit_bytes=vmem_mib * MIB)


def pick_kernel(scaled, win, planes_ref, slots_ref, base_ref, src_ref, pos_ref, *rest):
    if scaled:
        gate_ref, out_ref, acc_ref = rest
    else:
        out_ref, acc_ref = rest
    grp = pl.program_id(0)
    blk = pl.program_id(1)

    @pl.when(blk == 0)
    def _():
        acc_ref[...] = jnp.zeros_like(acc_ref)

    base = pl.multiple_of(base_ref[grp, blk], 8)
    pos_row = pos_ref[0]
    want = base + lax.broadcasted_iota(jnp.int32, (win, pos_row.shape[1]), 0)
    hit = want == pos_row
    part = mm(hit.astype(F32).astype(BF16), src_ref[0])
    if scaled:
        part = part * jnp.sum(jnp.where(hit, gate_ref[0], 0.0), axis=1, keepdims=True)
    acc_ref[pl.ds(base, win), :] += part

    @pl.when(blk == pl.num_programs(1) - 1)
    def _():
        out_ref[...] = acc_ref[: out_ref.shape[0], :].astype(out_ref.dtype)


def pick_rows(source, pos, gates, planes, slots, base, n_rows, win, n_src, n_etp):
    blk_rows = pos.shape[-1]
    d_model = source.shape[2]
    n_grp = planes.shape[0]
    src_map = lambda g, o, planes, slots, base: (o * n_etp + slots[g], 0, 0)
    tab_map = lambda g, o, planes, slots, base: (o * n_etp + planes[g], 0, 0)
    in_specs = [pl.BlockSpec((1, blk_rows, d_model), src_map), pl.BlockSpec((1, 1, blk_rows), tab_map)]
    operands = [source, pos[:, None, :]]
    if gates is not None:
        in_specs.append(pl.BlockSpec((1, 1, blk_rows), tab_map))
        operands.append(gates[:, None, :])
    flops = 2 * n_grp * n_src * win * blk_rows * d_model
    return pl.pallas_call(
        functools.partial(pick_kernel, gates is not None, win),
        grid_spec=pltpu.PrefetchScalarGridSpec(
            num_scalar_prefetch=3,
            grid=(n_grp, n_src),
            in_specs=in_specs,
            out_specs=pl.BlockSpec((n_rows, d_model), lambda g, o, planes, slots, base: (g, 0)),
            scratch_shapes=[pltpu.VMEM((n_rows + win, d_model), F32)],
        ),
        out_shape=jax.ShapeDtypeStruct((n_grp * n_rows, d_model), BF16),
        compiler_params=params(32, 2),
        cost_estimate=pl.CostEstimate(flops=flops, bytes_accessed=2 * source.size * 2, transcendentals=0),
        name="pick_rows",
    )(planes, slots, base, *operands)


def whole(array):
    return pl.BlockSpec(array.shape, lambda i: (0, 0), pipeline_mode=pl.Buffered(1))


def fwd_kernel(n_sets, x_ref, *refs):
    weights, (*base_ref, y_ref, u_ref) = refs[: 3 * n_sets], refs[3 * n_sets :]
    for s in range(n_sets):
        w1, w3, w2 = weights[3 * s : 3 * s + 3]

        def step(i, _):
            cols = pl.ds(pl.multiple_of(i * FF_STEP, FF_STEP), FF_STEP)
            act_a = mm(x_ref[...], w1[:, cols])
            act_b = mm(x_ref[...], w3[:, cols])
            u_ref[:, cols] = (act_a * jax.nn.sigmoid(act_a) * act_b).astype(BF16)
            return 0

        lax.fori_loop(0, w1.shape[1] // FF_STEP, step, 0)
        part = mm(u_ref[...], w2[...])
        if s > 0:
            y_ref[...] += part
        elif base_ref:
            y_ref[...] = base_ref[0][...] + part
        else:
            y_ref[...] = part


def ffn_fwd(x, sets, tile, first, n_tiles, base=()):
    d_model, d_ff = sets[0].shape
    rows = n_tiles * tile
    n_sets = len(sets) // 3
    return pl.pallas_call(
        functools.partial(fwd_kernel, n_sets),
        grid=(n_tiles,),
        in_specs=[pl.BlockSpec((tile, d_model), lambda i: (i + first, 0))] + [whole(w) for w in sets] + [pl.BlockSpec((tile, d_model), lambda i: (i + first, 0))] * len(base),
        out_specs=pl.BlockSpec((tile, d_model), lambda i: (i, 0)),
        out_shape=jax.ShapeDtypeStruct((rows, d_model), F32),
        scratch_shapes=[pltpu.VMEM((tile, d_ff), BF16)],
        compiler_params=params(56),
        cost_estimate=pl.CostEstimate(flops=6 * rows * d_model * d_ff * n_sets, bytes_accessed=6 * d_model * d_ff * n_sets + 6 * rows * d_model, transcendentals=rows * d_ff * n_sets),
        name="ffn_fwd",
    )(x, *sets, *base)


def bwd_kernel(n_sets, with_dx, with_y, n_alias, x_ref, c_ref, *refs):
    weights, refs = refs[: 3 * n_sets], list(refs[3 * n_sets + n_alias :])
    u_ref, da_ref, db_ref = refs[:3]
    dx_ref = refs.pop(3) if with_dx else None
    y_ref = refs.pop(3) if with_y else None
    tmp = refs[3:]
    for s in range(n_sets):
        w1, w3, w2 = weights[3 * s : 3 * s + 3]
        da, db, u = (da_ref, db_ref, u_ref) if s == 0 else (tmp[0], tmp[1], tmp[-1])
        with_u = s == 0 or with_y

        def step(i, _):
            cols = pl.ds(pl.multiple_of(i * FF_STEP, FF_STEP), FF_STEP)
            act_a = mm(x_ref[...], w1[:, cols])
            act_b = mm(x_ref[...], w3[:, cols])
            d_inner = mm_nt(c_ref[...], w2[cols, :])
            sig_a = jax.nn.sigmoid(act_a)
            silu_a = act_a * sig_a
            if with_u:
                u[:, cols] = (silu_a * act_b).astype(BF16)
            da[:, cols] = (d_inner * act_b * sig_a * (1.0 + act_a * (1.0 - sig_a))).astype(BF16)
            db[:, cols] = (d_inner * silu_a).astype(BF16)
            return 0

        lax.fori_loop(0, w1.shape[1] // FF_STEP, step, 0)
        if with_dx:
            part = mm_nt(da[...], w1[...]) + mm_nt(db[...], w3[...])
            if s == 0:
                dx_ref[...] = part
            else:
                dx_ref[...] += part
        if with_y:
            part = mm(u[...], w2[...])
            if s == 0:
                y_ref[...] = part
            else:
                y_ref[...] += part


def ffn_bwd(x, c, sets, tile, first, n_tiles, kept, with_dx=True, with_y=False):
    d_model, d_ff = sets[0].shape
    rows = n_tiles * tile
    n_sets = len(sets) // 3
    row_in = pl.BlockSpec((tile, d_model), lambda i: (i + first, 0))
    out_specs = [pl.BlockSpec((tile, d_ff), lambda i: (i + first, 0))] * 3
    out_shape = [jax.ShapeDtypeStruct((x.shape[0], d_ff), BF16)] * 3
    n_sums = int(with_dx) + int(with_y)
    out_specs += [pl.BlockSpec((tile, d_model), lambda i: (i, 0))] * n_sums
    out_shape += [jax.ShapeDtypeStruct((rows, d_model), F32)] * n_sums
    scratch = [pltpu.VMEM((tile, d_ff), BF16)] * (3 if with_y else 2) if n_sets > 1 else []
    n_in = 2 + len(sets)
    return pl.pallas_call(
        functools.partial(bwd_kernel, n_sets, with_dx, with_y, len(kept)),
        grid=(n_tiles,),
        in_specs=[row_in, row_in] + [whole(w) for w in sets] + [pl.BlockSpec(memory_space=pl.ANY)] * len(kept),
        out_specs=out_specs,
        out_shape=out_shape,
        scratch_shapes=scratch,
        input_output_aliases={n_in + i: i for i in range(len(kept))},
        compiler_params=params(60),
        cost_estimate=pl.CostEstimate(flops=(6 + 4 * with_dx + 2 * with_y) * rows * d_model * d_ff * n_sets, bytes_accessed=6 * d_model * d_ff * n_sets + 8 * rows * (d_model + d_ff), transcendentals=rows * d_ff * n_sets),
        name="ffn_bwd",
    )(x, c, *sets, *kept)


def home_kernel(win, n_far, start_ref, near_ref, *refs):
    fars, (more_ref, out_ref, sum_ref) = refs[:n_far], refs[n_far:]
    row = 0
    for far in fars:
        rows = far.shape[0]
        sum_ref[row : row + rows, :] = (near_ref[row : row + rows, :] + far[...]).astype(BF16).astype(F32)
        row += rows
    sum_ref[row : row + more_ref.shape[0], :] = more_ref[...].astype(F32)
    row += more_ref.shape[0]
    sum_ref[row:, :] = jnp.zeros((sum_ref.shape[0] - row, sum_ref.shape[1]), F32)
    out_rows = out_ref.shape[1]
    to = lax.broadcasted_iota(jnp.int32, (out_rows, win), 0)
    frm = lax.broadcasted_iota(jnp.int32, (out_rows, win), 1)
    for o in range(out_ref.shape[0]):
        start = start_ref[o]
        base = pl.multiple_of(start // 8 * 8, 8)
        rows = sum_ref[pl.ds(base, win), :].astype(BF16)
        move = (frm == to + (start - base)).astype(F32).astype(BF16)
        out_ref[o] = mm(move, rows).astype(BF16)


def home_blocks(starts, near, fars, more, out_rows):
    n_out = starts.shape[0]
    d_model = near.shape[1]
    win = out_rows + 8
    vmem = pl.BlockSpec(memory_space=pltpu.VMEM)
    return pl.pallas_call(
        functools.partial(home_kernel, win, len(fars)),
        in_specs=[pl.BlockSpec(memory_space=pltpu.SMEM)] + [vmem] * (2 + len(fars)),
        out_specs=vmem,
        out_shape=jax.ShapeDtypeStruct((n_out, out_rows, d_model), BF16),
        scratch_shapes=[pltpu.VMEM((near.shape[0] + more.shape[0] + win, d_model), F32)],
        compiler_params=pltpu.CompilerParams(vmem_limit_bytes=40 * MIB),
        cost_estimate=pl.CostEstimate(flops=2 * n_out * out_rows * win * d_model, bytes_accessed=12 * near.size, transcendentals=0),
        name="home_blocks",
    )(starts, near, *fars, more)


def split3(value):
    high = lax.reduce_precision(value, 8, 7)
    rest = value - high
    mid = lax.reduce_precision(rest, 8, 7)
    return high.astype(BF16), mid.astype(BF16), (rest - mid).astype(BF16)


def solution(mesh):
    ep_size = mesh.shape["ep"]
    etp_size = mesh.shape["etp"]
    n_dev = ep_size * etp_size
    tok_spec = P(ALL_AXES, None)
    gate_spec = P("ep", None, "etp")
    down_spec = P("ep", "etp", None)

    def layer(hidden, w_router, expert_ids, d_out, w_gate, w_up, w_down):
        tok_rows, d_model = hidden.shape
        n_experts = w_router.shape[1]
        n_tokens = tok_rows * n_dev
        capacity = (5 * n_tokens + 2 * n_experts - 1) // (2 * n_experts)
        per_expert = 7 * tok_rows // (2 * n_experts)
        list_max = ep_size * per_expert
        main_rows = 23 * tok_rows // 8
        more_rows = list_max - main_rows
        tile = main_rows // 2
        win = per_expert + 8
        ep_i = lax.axis_index("ep")
        etp_i = lax.axis_index("etp")
        block_idx = ep_i * etp_size + etp_i
        w1, w3, w2 = w_gate[0], w_up[0], w_down[0]

        def swap(array, even, odd):
            pairs = [(t * ep_size + o, (odd if o % 2 else even)[t] * ep_size + o) for t in range(etp_size) for o in range(ep_size)]
            return lax.ppermute(array, ("etp", "ep"), pairs)

        def spread(array):
            shifts = range(1, etp_size)
            moved = [lax.ppermute(array, "etp", [(t, (t + k) % etp_size) for t in range(etp_size)]) for k in shifts]
            return [array] + moved

        ids_row = expert_ids.T.astype(BF16).reshape(1, 2 * tok_rows)
        ids_row = jnp.concatenate([ids_row, jnp.zeros((7, 2 * tok_rows), BF16)])
        h_col = lax.all_gather(jnp.concatenate([hidden, ids_row]), "etp")
        w1_b, w3_b, w2_b, dy_b, h_col = lax.optimization_barrier((w1, w3, w2, d_out, h_col))
        dy_parts = spread(dy_b)
        w1p, w3p, w2p = [swap(w, NEXT_PAIRS, ENDS_PAIRS) for w in (w1_b, w3_b, w2_b)]
        h_all = lax.all_gather(h_col, "ep").reshape(n_dev, tok_rows + 8, d_model)
        *dy_parts, h_all = lax.optimization_barrier((*dy_parts, h_all))
        dy_col = jnp.stack(dy_parts)
        dy_all = lax.all_gather(dy_col, "ep").reshape(n_dev, tok_rows, d_model)

        ids_all = h_all[:, tok_rows, :].astype(jnp.int32).reshape(n_dev, 2, tok_rows)
        id0, id1 = ids_all[:, 0], ids_all[:, 1]
        experts = jnp.arange(n_experts, dtype=jnp.int32)[None, :, None]
        count = jnp.sum(((id0[:, None, :] == experts) | (id1[:, None, :] == experts)).astype(F32), axis=2)
        before = jnp.cumsum(count, axis=0) - count
        kept = jnp.clip(capacity - before, 0, count).astype(jnp.int32)
        kept_lists = kept.reshape(ep_size, etp_size, n_experts)
        list_start = jnp.cumsum(kept_lists, axis=0) - kept_lists
        list_len = jnp.sum(kept_lists, axis=0)
        earlier = (jnp.arange(tok_rows)[:, None] < jnp.arange(tok_rows)[None, :]).astype(BF16)

        my_member = (id0 == ep_i) | (id1 == ep_i)
        my_rank = mm(my_member.astype(BF16), earlier).astype(jnp.int32)
        my_start = lax.dynamic_index_in_dim(list_start, ep_i, 2, keepdims=False)
        my_kept = lax.dynamic_index_in_dim(kept, ep_i, 1, keepdims=True)
        my_pos = jnp.where(my_member & (my_rank < my_kept), my_start.reshape(n_dev, 1) + my_rank, -1)
        odd = ep_i % 2
        far = jnp.where(odd == 1, etp_i ^ 1, etp_size - 1 - etp_i)
        planes = jnp.stack([far, etp_i, far ^ 2, etp_i ^ 2]).astype(jnp.int32)
        my_base = jnp.minimum(my_start, main_rows) // 8 * 8
        pick = functools.partial(pick_rows, win=win, n_src=ep_size, n_etp=etp_size)
        main_pos = jnp.where(my_pos < main_rows, my_pos, -1)
        main_base = my_base.T[planes]
        dy_slots = (etp_i - planes) % etp_size
        x_main = pick(h_all, main_pos, None, planes, planes, main_base, main_rows)

        route_w = jnp.concatenate(split3(w_router), axis=1)
        logit_parts = lax.dot_general(route_w, h_all, (((0,), (2,)), ((), ())), preferred_element_type=F32)[:, :, :tok_rows].reshape(-1, n_tokens)
        logits = logit_parts[:n_experts] + logit_parts[n_experts : 2 * n_experts] + logit_parts[2 * n_experts :]
        probs_all = jax.nn.softmax(logits, axis=0)
        expert_col = jnp.arange(n_experts, dtype=jnp.int32)[:, None]
        picked_all = jnp.where((id0.reshape(1, -1) == expert_col) | (id1.reshape(1, -1) == expert_col), probs_all, 0.0)
        my_gate = lax.dynamic_index_in_dim(picked_all, ep_i, 0, keepdims=False) / jnp.sum(picked_all, axis=0)
        mean_prob = jnp.sum(probs_all, axis=1) / n_tokens
        my_scale = OUT_SCALE * my_gate.reshape(n_dev, tok_rows)
        c_main = pick(dy_all, main_pos, my_scale, planes, dy_slots, main_base, main_rows)

        own, pair = (w1, w3, w2), (w1p, w3p, w2p)
        y_base = ffn_fwd(x_main, own, tile, 0, 2)
        y_far = []
        for i in range(2):
            y_part = ffn_fwd(x_main, pair, tile, i, 1, (y_base,))
            y_far.append(swap(y_part, ENDS_PAIRS, NEXT_PAIRS))
        dx_far, acts = [], ()
        for i in range(2):
            *acts, dx_part = ffn_bwd(x_main, c_main, own + pair, tile, i, 1, acts)
            dx_far.append(swap(dx_part, ENDS_PAIRS, NEXT_PAIRS))
        *acts, dx_near, y_near = ffn_bwd(x_main, c_main, own + pair, tile // 2, 4, 4, acts, with_y=True)
        inner, d_a, d_b = ffn_bwd(x_main, c_main, own, tile, 4, 4, acts, with_dx=False)

        def more_work():
            more_pos = jnp.where(my_pos >= main_rows, my_pos - main_rows, -1)
            more_base = jnp.clip(my_start.T - main_rows, 0, more_rows) // 8 * 8
            order = jnp.arange(etp_size, dtype=jnp.int32)
            x_more = pick(h_all, more_pos, None, order, order, more_base, more_rows)
            c_more = pick(dy_all, more_pos, my_scale, order, (etp_i - order) % etp_size, more_base, more_rows)
            inner, d_a, d_b, dx_part, y_part = ffn_bwd(x_more, c_more, own, more_rows, 0, etp_size, (), with_y=True)
            y_more = lax.psum_scatter(y_part, "etp", scatter_dimension=0, tiled=True)
            dx_more = lax.psum_scatter(dx_part, "etp", scatter_dimension=0, tiled=True)
            return y_more.astype(BF16), dx_more.astype(BF16), x_more, c_more, inner, d_a, d_b

        def no_more_work():
            none = jnp.zeros((more_rows, d_model), BF16)
            rows = jnp.zeros((etp_size * more_rows, d_model), BF16)
            acts = jnp.zeros((etp_size * more_rows, w1.shape[1]), BF16)
            return none, none, rows, rows, acts, acts, acts

        any_more = jnp.max(list_len) > main_rows
        y_more, dx_more, *more = lax.cond(any_more, more_work, no_more_work)

        home_start = lax.dynamic_index_in_dim(my_start, etp_i, 1, keepdims=False)

        def send_home(near, fars, more):
            blocks = home_blocks(home_start, near, fars, more, per_expert)
            return lax.all_to_all(blocks, "ep", 0, 0, tiled=True).reshape(n_experts * per_expert, d_model)

        hot = [(expert_ids[:, k : k + 1] == experts[0].T).astype(F32) for k in range(2)]
        probs = lax.dynamic_slice_in_dim(probs_all, block_idx * tok_rows, tok_rows, 1).T
        picked = [jnp.sum(probs * hot[k], axis=1, keepdims=True) for k in range(2)]
        pick_sum = picked[0] + picked[1]
        gates = [picked[k] / pick_sum for k in range(2)]
        my_kept_row = lax.dynamic_index_in_dim(kept, block_idx, 0, keepdims=True).astype(F32)
        rank = mm_tn(earlier, (hot[0] + hot[1]).astype(BF16))
        slot_row = jnp.arange(n_experts * per_expert, dtype=jnp.int32)[None, :]
        chosen = []
        for k in range(2):
            rank_k = jnp.sum(rank * hot[k], axis=1, keepdims=True)
            kept_k = jnp.sum(my_kept_row * hot[k], axis=1, keepdims=True)
            slot_k = jnp.where(rank_k < kept_k, expert_ids[:, k : k + 1] * per_expert + rank_k.astype(jnp.int32), -1)
            chosen.append(slot_k == slot_row)

        y_back = send_home(y_near, y_far, y_more)
        y_pair = [mm(chosen[k].astype(BF16), y_back) for k in range(2)]
        hidden_f = hidden.astype(F32)
        output = (hidden_f + OUT_SCALE * (gates[0] * y_pair[0] + gates[1] * y_pair[1])).astype(BF16)
        d_out_f = d_out.astype(F32)
        d_gates = [jnp.sum(OUT_SCALE * d_out_f * y_pair[k], axis=1, keepdims=True) for k in range(2)]

        route_frac = jnp.sum(count, axis=0) / (2 * n_tokens)
        aux_loss = AUX_COEF * n_experts * jnp.sum(route_frac * mean_prob)
        mix = gates[0] * d_gates[0] + gates[1] * d_gates[1]
        d_probs = (AUX_COEF * n_experts / n_tokens) * route_frac[None, :]
        for k in range(2):
            d_probs = d_probs + hot[k] * ((d_gates[k] - mix) / pick_sum)
        d_logits = probs * (d_probs - jnp.sum(probs * d_probs, axis=1, keepdims=True))
        d_router_part = lax.dot_general(d_logits, hidden_f, (((0,), (0,)), ((), ())), precision=lax.Precision.HIGHEST, preferred_element_type=F32)
        x_main, c_main, inner, d_router_part = lax.optimization_barrier((x_main, c_main, inner, d_router_part))
        d_router = jnp.sum(lax.all_gather(d_router_part, ALL_AXES), axis=0).T
        dw1 = mm_tn(x_main, d_a)
        dw3 = mm_tn(x_main, d_b)
        dx_near, dw1, dw3 = lax.optimization_barrier((dx_near, dw1, dw3))
        dx_back = send_home(dx_near, dx_far, dx_more)
        dw2 = mm_tn(inner, c_main)

        def add_more(*grads):
            x_more, c_more, inner_more, d_a_more, d_b_more = more
            return grads[0] + mm_tn(x_more, d_a_more), grads[1] + mm_tn(x_more, d_b_more), grads[2] + mm_tn(inner_more, c_more)

        dw1, dw3, dw2 = lax.cond(any_more, add_more, lambda *grads: grads, dw1, dw3, dw2)
        d_route = lax.dot_general(d_logits, w_router, (((1,), (1,)), ((), ())), precision=lax.Precision.HIGHEST, preferred_element_type=F32)
        dx_sum = mm((chosen[0] | chosen[1]).astype(BF16), dx_back)
        d_hidden = (d_out_f + dx_sum + d_route).astype(BF16)
        return output, d_hidden, d_router, aux_loss, dw1[None], dw3[None], dw2[None]

    return jax.shard_map(layer, mesh=mesh, in_specs=(tok_spec, P(), tok_spec, tok_spec, gate_spec, gate_spec, down_spec), out_specs=(tok_spec, tok_spec, P(), P(), gate_spec, gate_spec, down_spec), check_vma=False)
```

time: 1960 us -> 993 us (0.51)
  waiting for transfers between devices: 1110 us -> 408 us
  Pallas kernels: 0 us -> 353 us
  matrix products: 359 us -> 129 us
  blocking collectives: 177 us -> 0 us
  local copies, waits for them, and re-layouts: 164 us -> 30.5 us
  other arithmetic: 103 us -> 20.6 us
    reduce_scatter x2 -> x0, waiting for transfers between devices: 757 us -> none  [combine(): lax.psum_scatter(part_out, 'etp', scatter_dimension=1, tiled=True)]
    pallas_call x0 -> x11, Pallas kernels: none -> 353 us  [the longest x4 217 us: ffn_bwd(): pl.pallas_call(functools.partial(bwd_kernel, n_sets, with_dx, with_y, len...]
    ppermute x0 -> x10, waiting for transfers between devices: none -> 242 us  [the longest x7 154 us: swap(): return lax.ppermute(array, ('etp', 'ep'), pairs)]
    dot_general x12 -> x11, matrix products: 359 us -> 129 us  [the longest x4 89 us: mm_tn(): lax.dot_general(lhs, rhs, (((0,), (0,)), ((), ())), preferred_element_typ...]
    all_gather x2 -> x4, waiting for transfers between devices: 358 us -> 160 us  [the longest x1 84.7 us: layer(): h_col = lax.all_gather(jnp.concatenate([hidden, ids_row]), 'etp')]
    all_to_all x2 -> x0, blocking collectives: 93.3 us -> none  [dispatch(): received = lax.all_to_all(send_buf, 'ep', 0, 1, tiled=True)]
    convert_element_type x4 -> x1, local copies, waits for them, and re-layouts: 62.3 us -> 0.11 us  [layer(): h_all[:, tok_rows, :].astype(jnp.int32).reshape(n_dev, 2, tok_rows)]
    unnamed x7 -> x1, other arithmetic: 52.6 us -> 0.69 us
  transfers between devices with their start and end apart: 6 -> 16, of which waited for: 4 -> 9; matrix products, arithmetic and copies ran while one was open for 22% -> 15% of each run, Pallas kernels for 0% -> 35%
where the time goes in v1:
time: 993 us; the launch traced here: 982 us
  waiting for transfers between devices  408 us (41%)
  Pallas kernels  353 us (36%)
  matrix products  129 us (13%)
  local copies, waits for them, and re-layouts  30.5 us (3%)
  starting transfers between devices  24 us (2%)
  other arithmetic  20.6 us (2%)
  between operations  17.2 us (2%)
    pallas_call x4, Pallas kernels, ffn_bwd(): pl.pallas_call(functools.partial(bwd_kernel, n_sets, with_dx, with_y, len...  217 us
    ppermute x7, waiting for transfers between devices, swap(): return lax.ppermute(array, ('etp', 'ep'), pairs)  154 us
    dot_general x4, matrix products, mm_tn(): lax.dot_general(lhs, rhs, (((0,), (0,)), ((), ())), preferred_element_typ...  89 us
    ppermute x3, waiting for transfers between devices, spread(): lax.ppermute(array, 'etp', [(t, (t + k) % etp_size) for t in range(etp_si...  88.4 us
    all_gather x1, waiting for transfers between devices, layer(): h_col = lax.all_gather(jnp.concatenate([hidden, ids_row]), 'etp')  84.7 us
    all_gather x1, waiting for transfers between devices, layer(): h_all = lax.all_gather(h_col, 'ep').reshape(n_dev, tok_rows + 8, d_model)  73.1 us
    pallas_call x2, Pallas kernels, pick_rows(): pl.pallas_call(functools.partial(pick_kernel, gates is not None, win), gr...  61.5 us
    pallas_call x3, Pallas kernels, ffn_fwd(): pl.pallas_call(functools.partial(fwd_kernel, n_sets), grid=(n_tiles,), in...  60.6 us
  transfers between devices with their start and end apart: 16, of which 9 were waited for; matrix products, arithmetic and copies ran while one was open for 15% of the time, Pallas kernels for 35%

profile of v1, /device:TPU:0, one launch (start us, length us, event | category | flops | bytes accessed | tf_op | source)
XLA Modules:
  0.0 981.9 jit_solution(12688409851176108900)
XLA Ops:
  10.6 84.7 %all-gather.9.cloned.1.call-done = bf16[2080,1024]{1,0:T(8,128)(2,1)} async-done(((bf16[520,1024]{1,0:T(8,128)(2,1)}), bf16[2080,1024]{1,0:T(8,128)(2,1)}) %all-gather.9.cloned.1.call-update) | async-done | bytes 4259856 | tf_op jit(solution)/shard_map/all_gather | solution.py:280
  98.3 22.8 %collective-permute-done.2 = bf16[512,1024]{1,0:T(8,128)(2,1)S(1)} collective-permute-done((bf16[512,1024]{1,0:T(8,128)(2,1)S(1)}, bf16[512,1024]{1,0:T(8,128)(2,1)S(1)}, u32[]{:S(2)}, u32[]{:S(2)}) %collective-permute-start.2) | collective-permute-done | bytes 1048608 | tf_op jit(solution)/shard_map/ppermute | solution.py:275
  121.1 65.6 %collective-permute-done.1 = bf16[512,1024]{1,0:T(8,128)(2,1)S(1)} collective-permute-done((bf16[512,1024]{1,0:T(8,128)(2,1)S(1)}, bf16[512,1024]{1,0:T(8,128)(2,1)S(1)}, u32[]{:S(2)}, u32[]{:S(2)}) %collective-permute-start.1) | collective-permute-done | bytes 1048608 | tf_op jit(solution)/shard_map/ppermute | solution.py:275
  186.7 73.1 %all-gather.11.cloned.1.call-done.src_ref = bf16[32,520,1024]{2,1,0:T(8,128)(2,1)} async-done(((bf16[4,520,1024]{2,1,0:T(8,128)(2,1)}), bf16[32,520,1024]{2,1,0:T(8,128)(2,1)}) %all-gather.11.cloned.1.call-update) | async-done | bytes 34078736 | tf_op jit(solution)/shard_map/all_gather | solution.py:284
  269.0 18.8 %fusion.32 = f32[24,32,520]{2,0,1:T(8,128)S(1)} fusion(bf16[32,520,1024]{2,1,0:T(8,128)(2,1)} %all-gather.11.cloned.1.call-done.src_ref, bf16[1024,8]{0,1:T(8,128)(2,1)S(1)} %get-tuple-element.214, bf16[1024,8]{0,1:T(8,128)(2,1)S(1)} %get-tuple-element.215, bf16[1024,8]{0,1:T(8,128)(2,1)S(1)} %get-tuple-element.213), kind=kOutput, calls=%fused_computation.74 | convolution fusion | flops 818036736 | bytes 35725312 | tf_op jit(solution)/shard_map/dot_general | solution.py:316
  295.4 30.8 %pick_rows.6.x_ref = bf16[5888,1024]{1,0:T(8,128)(2,1)S(1)} custom-call(s32[4]{0:T(128)S(1)} %get-tuple-element.210.planes_ref.slots_ref, s32[4]{0:T(128)S(1)} %get-tuple-element.210.planes_ref.slots_ref, s32[4,8]{1,0:T(4,128)S(1)} %gather_fusion, bf16[32,520,1024]{2,1,0:T(8,128)(2,1)} %all-gather.11.cloned.1.call-done.src_ref, ...), custom_call_target="tpu_custom_call" | custom-call | flops 7784628224 | bytes 68157440 | tf_op jit(solution)/shard_map/pick_rows/pallas_call | solution.py:76
  326.1 6.5 copy-done
  332.7 27.1 %ffn_fwd.3.refs_3_ = f32[1472,1024]{1,0:T(8,128)} custom-call(bf16[5888,1024]{1,0:T(8,128)(2,1)} %copy-done, bf16[1024,1792]{1,0:T(8,128)(2,1)S(1)} %bitcast.141, bf16[1024,1792]{1,0:T(8,128)(2,1)} %bitcast.143, bf16[1792,1024]{1,0:T(8,128)(2,1)} %bitcast.150), custom_call_target="tpu_custom_call" | custom-call | flops 16206790656 | bytes 20054016 | tf_op jit(solution)/shard_map/ffn_fwd/pallas_call | solution.py:122
  359.8 65.1 %collective-permute-done.4.refs_4_.refs_1_ = bf16[1024,1792]{1,0:T(8,128)(2,1)} collective-permute-done((bf16[1024,1792]{1,0:T(8,128)(2,1)}, bf16[1024,1792]{1,0:T(8,128)(2,1)}, u32[]{:S(2)}, u32[]{:S(2)}) %collective-permute-start.4) | collective-permute-done | bytes 3670048 | tf_op jit(solution)/shard_map/ppermute | solution.py:271
  424.8 78.6 %collective-permute-done.5.refs_5_.refs_2_ = bf16[1792,1024]{1,0:T(8,128)(2,1)} collective-permute-done((bf16[1792,1024]{1,0:T(8,128)(2,1)}, bf16[1792,1024]{1,0:T(8,128)(2,1)}, u32[]{:S(2)}, u32[]{:S(2)}) %collective-permute-start.5) | collective-permute-done | bytes 3670048 | tf_op jit(solution)/shard_map/ppermute | solution.py:271
  503.5 16.7 %ffn_fwd.4 = f32[736,1024]{1,0:T(8,128)} custom-call(bf16[5888,1024]{1,0:T(8,128)(2,1)} %copy-done, bf16[1024,1792]{1,0:T(8,128)(2,1)} %collective-permute-done.3.refs_3_.refs_0_, bf16[1024,1792]{1,0:T(8,128)(2,1)} %collective-permute-done.4.refs_4_.refs_1_, bf16[1792,1024]{1,0:T(8,128)(2,1)} %collective-permute-done.5.refs_5_.refs_2_, ...), custom_call_target="tpu_custom_call" | custom-call | flops 8103395328 | bytes 15532032 | tf_op jit(solution)/shard_map/ffn_fwd/pallas_call | solution.py:122
  523.8 16.9 %ffn_fwd.5 = f32[736,1024]{1,0:T(8,128)} custom-call(bf16[5888,1024]{1,0:T(8,128)(2,1)} %copy-done, bf16[1024,1792]{1,0:T(8,128)(2,1)} %collective-permute-done.3.refs_3_.refs_0_, bf16[1024,1792]{1,0:T(8,128)(2,1)} %collective-permute-done.4.refs_4_.refs_1_, bf16[1792,1024]{1,0:T(8,128)(2,1)} %collective-permute-done.5.refs_5_.refs_2_, ...), custom_call_target="tpu_custom_call" | custom-call | flops 8103395328 | bytes 15532032 | tf_op jit(solution)/shard_map/ffn_fwd/pallas_call | solution.py:122
  543.5 30.7 %pick_rows.7.c_ref = bf16[5888,1024]{1,0:T(8,128)(2,1)S(1)} custom-call(s32[4]{0:T(128)S(1)} %get-tuple-element.210.planes_ref.slots_ref, s32[4]{0:T(128)S(1)} %get-tuple-element.209.slots_ref, s32[4,8]{1,0:T(4,128)S(1)} %gather_fusion, bf16[32,512,1024]{2,1,0:T(8,128)(2,1)} %all-gather.13.cloned.1.call-done.src_ref, ...), custom_call_target="tpu_custom_call" | custom-call | flops 7784628224 | bytes 67108864 | tf_op jit(solution)/shard_map/pick_rows/pallas_call | solution.py:76
  578.6 41.1 %ffn_bwd.6 = (bf16[5888,1792]{1,0:T(8,128)(2,1)}, bf16[5888,1792]{1,0:T(8,128)(2,1)}, bf16[5888,1792]{1,0:T(8,128)(2,1)}, f32[736,1024]{1,0:T(8,128)}) custom-call(bf16[5888,1024]{1,0:T(8,128)(2,1)} %copy-done, bf16[5888,1024]{1,0:T(8,128)(2,1)} %copy-done.1, bf16[1024,1792]{1,0:T(8,128)(2,1)} %bitcast.136, bf16[1024,1792]{1,0:T(8,128)(2,1)} %bitcast.144, ...), custom_call_target="tpu_custom_call" | custom-call | flops 27011317760 | bytes 38600704 | tf_op jit(solution)/shard_map/ffn_bwd/pallas_call | solution.py:186
  619.7 40.9 %ffn_bwd.7 = (bf16[5888,1792]{1,0:T(8,128)(2,1)}, bf16[5888,1792]{1,0:T(8,128)(2,1)}, bf16[5888,1792]{1,0:T(8,128)(2,1)}, f32[736,1024]{1,0:T(8,128)}) custom-call(bf16[5888,1024]{1,0:T(8,128)(2,1)} %copy-done, bf16[5888,1024]{1,0:T(8,128)(2,1)} %copy-done.1, ...), custom_call_target="tpu_custom_call", output_to_operand_aliasing={{0}: (8, {}), {1}: (9, {}), {2}: (10, {})} | custom-call | flops 27011317760 | bytes 38600704 | tf_op jit(solution)/shard_map/ffn_bwd/pallas_call | solution.py:186
  660.6 87.7 %ffn_bwd.8 = (bf16[5888,1792]{1,0:T(8,128)(2,1)}, bf16[5888,1792]{1,0:T(8,128)(2,1)}, bf16[5888,1792]{1,0:T(8,128)(2,1)}, f32[1472,1024]{1,0:T(8,128)}, f32[1472,1024]{1,0:T(8,128)}) custom-call(bf16[5888,1024]{1,0:T(8,128)(2,1)} %copy-done, bf16[5888,1024]{1,0:T(8,128)(2,1)} %copy-done.1, ...), custom_call_target="tpu_custom_call", output_to_operand_aliasing={{0}: (8, {}), {1}: (9, {}), {2}: (10, {})} | custom-call | flops 64827162624 | bytes 55181312 | tf_op jit(solution)/shard_map/ffn_bwd/pallas_call | solution.py:186
  748.2 12.1 %conditional.2 = (bf16[320,1024]{1,0:T(8,128)(2,1)}, bf16[320,1024]{1,0:T(8,128)(2,1)S(1)}, bf16[1280,1024]{1,0:T(8,128)(2,1)}, bf16[1280,1024]{1,0:T(8,128)(2,1...) conditional(s32[]{:T(128)} %convert_element_type.121, () %tuple.47, ...), branch_computations={%region_12.13_spmd, %region_13.16_spmd} | conditional | flops 43755716608 | bytes 229704160 | solution.py:357
  761.2 7.2 home_blocks.2
  779.2 47.5 %ffn_bwd.9 = (bf16[5888,1792]{1,0:T(8,128)(2,1)}, bf16[5888,1792]{1,0:T(8,128)(2,1)}, bf16[5888,1792]{1,0:T(8,128)(2,1)}) custom-call(bf16[5888,1024]{1,0:T(8,128)(2,1)} %copy-done, bf16[5888,1024]{1,0:T(8,128)(2,1)} %copy-done.1, bf16[1024,1792]{1,0:T(8,128)(2,1)} %bitcast.140, ...), custom_call_target="tpu_custom_call", output_to_operand_aliasing={{0}: (5, {}), {1}: (6, {}), {2}: (7, {})} | custom-call | flops 32413581312 | bytes 77332480 | tf_op jit(solution)/shard_map/ffn_bwd/pallas_call | solution.py:186
  831.1 6.3 fusion.12
  840.2 29.6 %fusion.60 = f32[1024,1792]{1,0:T(8,128)} fusion(bf16[5888,1024]{1,0:T(8,128)(2,1)} %copy-done, bf16[5888,1792]{1,0:T(8,128)(2,1)} %get-tuple-element.163), kind=kOutput, calls=%fused_computation.143 | convolution fusion | flops 21609054208 | bytes 40501248 | tf_op jit(solution)/shard_map/dot_general | solution.py:31
  869.7 29.7 %fusion.59 = f32[1024,1792]{1,0:T(8,128)} fusion(bf16[5888,1024]{1,0:T(8,128)(2,1)} %copy-done, bf16[5888,1792]{1,0:T(8,128)(2,1)} %get-tuple-element.162), kind=kOutput, calls=%fused_computation.142 | convolution fusion | flops 21609054208 | bytes 40501248 | tf_op jit(solution)/shard_map/dot_general | solution.py:31
  899.5 10.3 %collective-permute-done.8.refs_0_ = f32[736,1024]{1,0:T(8,128)} collective-permute-done((f32[736,1024]{1,0:T(8,128)}, f32[736,1024]{1,0:T(8,128)}, u32[]{:S(2)}, u32[]{:S(2)}) %collective-permute-start.8) | collective-permute-done | bytes 3014688 | tf_op jit(solution)/shard_map/ppermute | solution.py:271
  922.4 29.1 %fusion.61 = f32[1792,1024]{1,0:T(8,128)S(1)} fusion(bf16[5888,1792]{1,0:T(8,128)(2,1)} %get-tuple-element.171, bf16[5888,1024]{1,0:T(8,128)(2,1)} %copy-done.1), kind=kOutput, calls=%fused_computation.144 | convolution fusion | flops 21609054208 | bytes 40501248 | tf_op jit(solution)/shard_map/dot_general | solution.py:31
  (159 shorter events, 97.9 us)
Async XLA Ops:
  7.2 88.1 %all-gather.9.cloned.1.call-start = ((), (), s32[]{:S(2)}) async-start(), calls=%async_computation.6 | async-start | bytes 5324800 | tf_op jit(solution)/shard_map/all_gather | solution.py:280
  8.0 87.3 %copy-start.12 = (bf16[512,1024]{1,0:T(8,128)(2,1)S(1)}, bf16[512,1024]{1,0:T(8,128)(2,1)}, u32[]{:S(2)}) copy-start(bf16[512,1024]{1,0:T(8,128)(2,1)} %param.14) | copy-start | bytes 3145732
  10.6 249.2 %all-gather.11.cloned.1.call-start = ((), (), s32[]{:S(2)}) async-start(), calls=%async_computation.7 | async-start | bytes 38338560 | tf_op jit(solution)/shard_map/all_gather | solution.py:284
  95.3 448.2 %all-gather.13.cloned.1.call-start = ((), (), s32[]{:S(2)}) async-start(), calls=%async_computation.8 | async-start | bytes 37748736 | tf_op jit(solution)/shard_map/all_gather | solution.py:287
  95.3 25.7 %collective-permute-start.2 = (bf16[512,1024]{1,0:T(8,128)(2,1)S(1)}, bf16[512,1024]{1,0:T(8,128)(2,1)S(1)}, u32[]{:S(2)}, u32[]{:S(2)}) collective-permute-start(bf16[512,1024]{1,0:T(8,128)(2,1)S(1)} %copy-done.12), channel_id=1, source_target_pairs={{0,24},{8,0},{16,8},{24,16},{1,25},{9,1},{17,9},{25,17},{2,26},{10... | collective-permute-start | bytes 3145736 | tf_op jit(solution)/shard_map/ppermute | solution.py:275
  96.0 90.7 %collective-permute-start.1 = (bf16[512,1024]{1,0:T(8,128)(2,1)S(1)}, bf16[512,1024]{1,0:T(8,128)(2,1)S(1)}, u32[]{:S(2)}, u32[]{:S(2)}) collective-permute-start(bf16[512,1024]{1,0:T(8,128)(2,1)S(1)} %copy-done.12), channel_id=1, source_target_pairs={{0,16},{8,24},{16,0},{24,8},{1,17},{9,25},{17,1},{25,9},{2,18},{10... | collective-permute-start | bytes 3145736 | tf_op jit(solution)/shard_map/ppermute | solution.py:275
  96.4 90.3 %collective-permute-start = (bf16[512,1024]{1,0:T(8,128)(2,1)S(1)}, bf16[512,1024]{1,0:T(8,128)(2,1)}, u32[]{:S(2)}, u32[]{:S(2)}) collective-permute-start(bf16[512,1024]{1,0:T(8,128)(2,1)S(1)} %copy-done.12), channel_id=1, source_target_pairs={{0,8},{8,16},{16,24},{24,0},{1,9},{9,17},{17,25},{25,1},{2,10},{10... | collective-permute-start | bytes 3145736 | tf_op jit(solution)/shard_map/ppermute | solution.py:275
  263.9 28.0 %copy-start.23 = (s32[512,1]{0,1:T(1,128)}, s32[512,1]{0,1:T(1,128)S(1)}, u32[]{:S(2)}) copy-start(s32[512,1]{0,1:T(1,128)S(1)} %get-tuple-element.219) | copy-start | bytes 6148
  263.9 95.9 %collective-permute-start.3 = (bf16[1024,1792]{1,0:T(8,128)(2,1)}, bf16[1024,1792]{1,0:T(8,128)(2,1)}, u32[]{:S(2)}, u32[]{:S(2)}) collective-permute-start(bf16[1024,1792]{1,0:T(8,128)(2,1)} %bitcast.135), channel_id=1, source_target_pairs={{0,8},{1,25},{2,10},{3,27},{4,12},{5,29},{6,14},{7,31},{8,0},{9,17... | collective-permute-start | bytes 11010056 | tf_op jit(solution)/shard_map/ppermute | solution.py:271
  265.5 159.4 %collective-permute-start.4 = (bf16[1024,1792]{1,0:T(8,128)(2,1)}, bf16[1024,1792]{1,0:T(8,128)(2,1)}, u32[]{:S(2)}, u32[]{:S(2)}) collective-permute-start(bf16[1024,1792]{1,0:T(8,128)(2,1)} %bitcast.142), channel_id=1, source_target_pairs={{0,8},{1,25},{2,10},{3,27},{4,12},{5,29},{6,14},{7,31},{8,0},{9,17... | collective-permute-start | bytes 11010056 | tf_op jit(solution)/shard_map/ppermute | solution.py:271
  266.0 237.5 %collective-permute-start.5 = (bf16[1792,1024]{1,0:T(8,128)(2,1)}, bf16[1792,1024]{1,0:T(8,128)(2,1)}, u32[]{:S(2)}, u32[]{:S(2)}) collective-permute-start(bf16[1792,1024]{1,0:T(8,128)(2,1)} %bitcast.149), channel_id=1, source_target_pairs={{0,8},{1,25},{2,10},{3,27},{4,12},{5,29},{6,14},{7,31},{8,0},{9,17... | collective-permute-start | bytes 11010056 | tf_op jit(solution)/shard_map/ppermute | solution.py:271
  288.6 254.7 %copy-start.15 = (f32[8,16384]{1,0:T(8,128)}, f32[8,16384]{1,0:T(8,128)S(1)}, u32[]{:S(2)}) copy-start(f32[8,16384]{1,0:T(8,128)S(1)} %exponential_divide_fusion) | copy-start | bytes 1572868
  289.5 36.7 %copy-start.25 = (s32[8,4,1]{0,1,2:T(4,128)}, s32[8,4,1]{0,1,2:T(4,128)S(1)}, u32[]{:S(2)}) copy-start(s32[8,4,1]{0,1,2:T(4,128)S(1)} %copy.44) | copy-start | bytes 388
  295.3 37.3 %copy-start.9 = (bf16[1,1024,1792]{2,1,0:T(8,128)(2,1)S(1)}, bf16[1,1024,1792]{2,1,0:T(8,128)(2,1)}, u32[]{:S(2)}) copy-start(bf16[1,1024,1792]{2,1,0:T(8,128)(2,1)} %param.15) | copy-start | bytes 11010052
  520.2 240.2 %collective-permute-start.6 = (f32[736,1024]{1,0:T(8,128)}, f32[736,1024]{1,0:T(8,128)}, u32[]{:S(2)}, u32[]{:S(2)}) collective-permute-start(f32[736,1024]{1,0:T(8,128)} %ffn_fwd.4), channel_id=1, source_target_pairs={{0,24},{1,9},{2,26},{3,11},{4,28},{5,13},{6,30},{7,15},{8,16},{9,1... | collective-permute-start | bytes 9043976 | tf_op jit(solution)/shard_map/ppermute | solution.py:271
  540.7 219.7 %collective-permute-start.7 = (f32[736,1024]{1,0:T(8,128)}, f32[736,1024]{1,0:T(8,128)}, u32[]{:S(2)}, u32[]{:S(2)}) collective-permute-start(f32[736,1024]{1,0:T(8,128)} %ffn_fwd.5), channel_id=1, source_target_pairs={{0,24},{1,9},{2,26},{3,11},{4,28},{5,13},{6,30},{7,15},{8,16},{9,1... | collective-permute-start | bytes 9043976 | tf_op jit(solution)/shard_map/ppermute | solution.py:271
  660.6 87.7 %copy-start.18 = (s32[32,512]{1,0:T(8,128)S(1)}, s32[32,512]{1,0:T(8,128)}, u32[]{:S(2)}) copy-start(s32[32,512]{1,0:T(8,128)} %get-tuple-element.223) | copy-start | bytes 196612
  660.6 87.7 %copy-start.26 = (s32[8,4,1]{0,1,2:T(4,128)S(1)}, s32[8,4,1]{0,1,2:T(4,128)}, u32[]{:S(2)}) copy-start(s32[8,4,1]{0,1,2:T(4,128)} %copy-done.25) | copy-start | bytes 388
  770.2 56.5 %all-to-all-start = ((bf16[8,224,1024]{2,1,0:T(8,128)(2,1)}), bf16[8,224,1024]{2,1,0:T(8,128)(2,1)}, u32[]{:S(2)}, u32[]{:S(2)}) async-start(bf16[8,224,1024]{2,1,0:T(8,128)(2,1)} %copy-done.3), calls=%async_computation.2 | async-start | bytes 7340032 | tf_op jit(solution)/shard_map/all_to_all | solution.py:363
  774.7 186.9 %all-gather.15.cloned.1.call-start = ((), (), s32[]{:S(2)}) async-start(), calls=%async_computation.9 | async-start | bytes 1081344 | tf_op jit(solution)/shard_map/all_gather | solution.py:396
  775.3 124.2 %collective-permute-start.9 = (f32[736,1024]{1,0:T(8,128)}, f32[736,1024]{1,0:T(8,128)S(1)}, u32[]{:S(2)}, u32[]{:S(2)}) collective-permute-start(f32[736,1024]{1,0:T(8,128)} %get-tuple-element.166), channel_id=1, source_target_pairs={{0,24},{1,9},{2,26},{3,11},{4,28},{5,13},{6,30},{7,15},{8,16},{9,1... | collective-permute-start | bytes 9043976 | tf_op jit(solution)/shard_map/ppermute | solution.py:271
  779.1 130.7 %collective-permute-start.8 = (f32[736,1024]{1,0:T(8,128)}, f32[736,1024]{1,0:T(8,128)}, u32[]{:S(2)}, u32[]{:S(2)}) collective-permute-start(f32[736,1024]{1,0:T(8,128)} %get-tuple-element.165), channel_id=1, source_target_pairs={{0,24},{1,9},{2,26},{3,11},{4,28},{5,13},{6,30},{7,15},{8,16},{9,1... | collective-permute-start | bytes 9043976 | tf_op jit(solution)/shard_map/ppermute | solution.py:271
  917.9 50.9 %all-to-all-start.1 = ((bf16[8,224,1024]{2,1,0:T(8,128)(2,1)}), bf16[8,224,1024]{2,1,0:T(8,128)(2,1)}, u32[]{:S(2)}, u32[]{:S(2)}) async-start(bf16[8,224,1024]{2,1,0:T(8,128)(2,1)} %copy-done.2), calls=%async_computation.3 | async-start | bytes 7340032 | tf_op jit(solution)/shard_map/all_to_all | solution.py:363
  922.4 29.1 %copy-start.5 = (bf16[1280,1024]{1,0:T(8,128)(2,1)S(1)}, bf16[1280,1024]{1,0:T(8,128)(2,1)}, u32[]{:S(2)}) copy-start(bf16[1280,1024]{1,0:T(8,128)(2,1)} %get-tuple-element.250) | copy-start | bytes 7864324
  (24 other events, 137.1 us)
Sparse Core Ops, SparseCore 0:
  10.7 84.5 all-gather.8
  97.2 162.5 all-gather.10
  263.3 160.6 all-gather.12
  899.6 62.0 all-gather.14

commit v2 on v1

--- a/solution.py
+++ b/solution.py
@@ -35,6 +35,155 @@
     return pltpu.CompilerParams(dimension_semantics=("arbitrary",) * dims, vmem_limit_bytes=vmem_mib * MIB)
 
 
+def spread_kernel(n_etp, h_ref, dy_ref, h_all, dy_col, h_recv, dy_recv, z_send, x_send, y_send, c_send, own_sem):
+    t = lax.axis_index("etp")
+    o = lax.axis_index("ep")
+    col_c = o + 1 - 2 * (o % 2)
+    col_x = o + 2 - 4 * ((o // 2) % 2)
+    col_y = o + 4 - 8 * (o // 4)
+    col_d = col_x + 4 - 8 * (o // 4)
+    order = [t, t + 1 - 2 * (t % 2), (t + 2) % 4, 3 - t]
+    has_left, has_right = t > 0, t < n_etp - 1
+
+    barrier = pltpu.get_barrier_semaphore()
+    for col in (col_c, col_x, col_y):
+        pl.semaphore_signal(barrier, inc=1, device_id={"ep": col}, device_id_type=pl.DeviceIdType.MESH)
+
+    @pl.when(has_left)
+    def _():
+        pl.semaphore_signal(barrier, inc=1, device_id={"etp": t - 1}, device_id_type=pl.DeviceIdType.MESH)
+
+    @pl.when(has_right)
+    def _():
+        pl.semaphore_signal(barrier, inc=1, device_id={"etp": t + 1}, device_id_type=pl.DeviceIdType.MESH)
+
+    pl.semaphore_wait(barrier, 3 + (t + n_etp - 1) // n_etp + (2 * n_etp - 2 - t) // n_etp)
+
+    keep = [pltpu.make_async_copy(h_ref, h_all.at[o * n_etp + t], own_sem.at[0]), pltpu.make_async_copy(dy_ref, dy_col.at[t], own_sem.at[1])]
+    for copy in keep:
+        copy.start()
+
+    def h_copy(col, s, send_sem, to):
+        slot = col * n_etp + s
+        return pltpu.make_async_remote_copy(src_ref=h_all.at[slot], dst_ref=h_all.at[slot], send_sem=send_sem, recv_sem=h_recv.at[slot], device_id=to, device_id_type=pl.DeviceIdType.MESH)
+
+    def own_copy(send_sem, to):
+        slot = o * n_etp + t
+        return pltpu.make_async_remote_copy(src_ref=h_ref, dst_ref=h_all.at[slot], send_sem=send_sem, recv_sem=h_recv.at[slot], device_id=to, device_id_type=pl.DeviceIdType.MESH)
+
+    def dy_copy(s, send_sem, to, own=False):
+        return pltpu.make_async_remote_copy(src_ref=dy_ref if own else dy_col.at[s], dst_ref=dy_col.at[s], send_sem=send_sem, recv_sem=dy_recv.at[s], device_id=to, device_id_type=pl.DeviceIdType.MESH)
+
+    def h_arrived(col, s):
+        h_copy(col, s, own_sem.at[0], {"ep": col_c}).wait_recv()
+
+    def dy_arrived(s):
+        dy_copy(s, own_sem.at[0], {"ep": col_c}).wait_recv()
+
+    right, left = {"etp": t + 1}, {"etp": t - 1}
+    to_x, to_y, to_c = {"ep": col_x}, {"ep": col_y}, {"ep": col_c}
+
+    def z_copy(k, data, go):
+        s, to, sem = (t - k, right, z_send.at[data, 0, k]) if go == 0 else (t + k, left, z_send.at[data, 1, k])
+        if data == 0:
+            return own_copy(sem, to) if k == 0 else h_copy(o, s, sem, to)
+        return dy_copy(s, sem, to, own=k == 0)
+
+    def z_goes(k, go):
+        return has_right & (t >= k) if go == 0 else has_left & (t <= n_etp - 1 - k)
+
+    def z_send_step(k, data):
+        for go in (0, 1):
+            pl.when(z_goes(k, go))(lambda: z_copy(k, data, go).start())
+
+    def z_arrive(k, data):
+        arrived = (lambda s: h_arrived(o, s)) if data == 0 else dy_arrived
+        pl.when(t >= k)(lambda: arrived(t - k))
+        pl.when(t <= n_etp - 1 - k)(lambda: arrived(t + k))
+
+    def a_step(k):
+        s = order[k]
+        for sem, to in ((x_send.at[k], to_x), (y_send.at[k], to_y), (c_send.at[0, k], to_c)):
+            (own_copy(sem, to) if k == 0 else h_copy(o, s, sem, to)).start()
+
+    def b_step(k):
+        s = order[k]
+        h_arrived(col_x, s)
+        if k % 2 == 0:
+            h_copy(col_x, s, y_send.at[4 + k // 2], to_y).start()
+        h_copy(col_x, s, c_send.at[1, k], to_c).start()
+        h_arrived(col_y, s)
+        if k % 2 == 1:
+            h_copy(col_y, s, x_send.at[4 + k // 2], to_x).start()
+        h_copy(col_y, s, c_send.at[2, k], to_c).start()
+
+    def c_step(k):
+        s = order[k]
+        h_arrived(col_d, s)
+        h_copy(col_d, s, c_send.at[3, k], to_c).start()
+
+    z_send_step(0, 0)
+    a_step(0)
+    z_arrive(1, 0)
+    z_send_step(1, 0)
+    a_step(1)
+    b_step(0)
+    z_arrive(2, 0)
+    z_send_step(2, 0)
+    z_send_step(0, 1)
+    a_step(2)
+    b_step(1)
+    z_arrive(3, 0)
+    a_step(3)
+    c_step(0)
+    b_step(2)
+    c_step(1)
+    z_arrive(1, 1)
+    z_send_step(1, 1)
+    b_step(3)
+    z_arrive(2, 1)
+    z_send_step(2, 1)
+    c_step(2)
+    c_step(3)
+    z_arrive(3, 1)
+
+    for k in range(n_etp):
+        for col in (col_x, col_y, col_d):
+            h_arrived(col + 1 - 2 * (o % 2), order[k])
+        h_arrived(col_c, order[k])
+    for copy in keep:
+        copy.wait()
+    for k in range(n_etp - 1):
+        for data in (0, 1):
+            for go in (0, 1):
+                pl.when(z_goes(k, go))(lambda: z_copy(k, data, go).wait_send())
+    for i in range(6):
+        h_copy(o, t, x_send.at[i], to_x).wait_send()
+        h_copy(o, t, y_send.at[i], to_y).wait_send()
+    for j in range(4):
+        for k in range(n_etp):
+            h_copy(o, t, c_send.at[j, k], to_c).wait_send()
+
+
+def spread_all(h, dy, n_etp, n_ep):
+    hbm = pl.BlockSpec(memory_space=pl.ANY)
+    vmem = pl.BlockSpec(memory_space=pltpu.VMEM)
+    dma = pltpu.SemaphoreType.DMA
+    return pl.pallas_call(
+        functools.partial(spread_kernel, n_etp),
+        in_specs=[vmem, vmem],
+        out_specs=[hbm, hbm],
+        out_shape=[jax.ShapeDtypeStruct((n_ep * n_etp, *h.shape), h.dtype), jax.ShapeDtypeStruct((n_etp, *dy.shape), dy.dtype)],
+        scratch_shapes=[dma((n_ep * n_etp,)), dma((n_etp,)), dma((2, 2, n_etp - 1)), dma((6,)), dma((6,)), dma((4, n_etp)), dma((2,))],
+        compiler_params=pltpu.CompilerParams(collective_id=0, has_side_effects=True, vmem_limit_bytes=16 * MIB),
+        cost_estimate=pl.CostEstimate(flops=10**11, bytes_accessed=2 * n_ep * n_etp * h.size, transcendentals=0),
+        name="spread_all",
+    )(h, dy)
+
+
+PICK_STEP = 8
+
+
 def pick_kernel(scaled, win, planes_ref, slots_ref, base_ref, src_ref, pos_ref, *rest):
     if scaled:
         gate_ref, out_ref, acc_ref = rest
@@ -47,14 +196,18 @@
     def _():
         acc_ref[...] = jnp.zeros_like(acc_ref)
 
-    base = pl.multiple_of(base_ref[grp, blk], 8)
-    pos_row = pos_ref[0]
-    want = base + lax.broadcasted_iota(jnp.int32, (win, pos_row.shape[1]), 0)
-    hit = want == pos_row
-    part = mm(hit.astype(F32).astype(BF16), src_ref[0])
-    if scaled:
-        part = part * jnp.sum(jnp.where(hit, gate_ref[0], 0.0), axis=1, keepdims=True)
-    acc_ref[pl.ds(base, win), :] += part
+    parts = []
+    for i in range(PICK_STEP):
+        base = pl.multiple_of(base_ref[grp, blk * PICK_STEP + i], 8)
+        pos_row = pos_ref[i, 0]
+        want = base + lax.broadcasted_iota(jnp.int32, (win, pos_row.shape[1]), 0)
+        hit = want == pos_row
+        part = mm(hit.astype(F32).astype(BF16), src_ref[i, 0])
+        if scaled:
+            part = part * jnp.sum(jnp.where(hit, gate_ref[i, 0], 0.0), axis=1, keepdims=True)
+        parts.append((base, part))
+    for base, part in parts:
+        acc_ref[pl.ds(base, win), :] += part
 
     @pl.when(blk == pl.num_programs(1) - 1)
     def _():
@@ -65,71 +218,149 @@
     blk_rows = pos.shape[-1]
     d_model = source.shape[2]
     n_grp = planes.shape[0]
-    src_map = lambda g, o, planes, slots, base: (o * n_etp + slots[g], 0, 0)
-    tab_map = lambda g, o, planes, slots, base: (o * n_etp + planes[g], 0, 0)
-    in_specs = [pl.BlockSpec((1, blk_rows, d_model), src_map), pl.BlockSpec((1, 1, blk_rows), tab_map)]
-    operands = [source, pos[:, None, :]]
-    if gates is not None:
-        in_specs.append(pl.BlockSpec((1, 1, blk_rows), tab_map))
-        operands.append(gates[:, None, :])
+    src_map = lambda g, o, planes, slots, base: (o, slots[g], 0, 0)
+    tab_map = lambda g, o, planes, slots, base: (o, planes[g], 0, 0)
+    tab_spec = pl.BlockSpec((PICK_STEP, 1, 1, blk_rows), tab_map)
+    tables = [table.reshape(n_src, n_etp, 1, blk_rows) for table in (pos, gates) if table is not None]
     flops = 2 * n_grp * n_src * win * blk_rows * d_model
     return pl.pallas_call(
         functools.partial(pick_kernel, gates is not None, win),
         grid_spec=pltpu.PrefetchScalarGridSpec(
             num_scalar_prefetch=3,
-            grid=(n_grp, n_src),
-            in_specs=in_specs,
+            grid=(n_grp, n_src // PICK_STEP),
+            in_specs=[pl.BlockSpec((PICK_STEP, 1, blk_rows, d_model), src_map)] + [tab_spec] * len(tables),
             out_specs=pl.BlockSpec((n_rows, d_model), lambda g, o, planes, slots, base: (g, 0)),
             scratch_shapes=[pltpu.VMEM((n_rows + win, d_model), F32)],
         ),
         out_shape=jax.ShapeDtypeStruct((n_grp * n_rows, d_model), BF16),
-        compiler_params=params(32, 2),
+        compiler_params=params(58, 2),
         cost_estimate=pl.CostEstimate(flops=flops, bytes_accessed=2 * source.size * 2, transcendentals=0),
         name="pick_rows",
-    )(planes, slots, base, *operands)
+    )(planes, slots, base, source.reshape(n_src, n_etp, *source.shape[1:]), *tables)
 
 
 def whole(array):
     return pl.BlockSpec(array.shape, lambda i: (0, 0), pipeline_mode=pl.Buffered(1))
 
 
-def fwd_kernel(n_sets, x_ref, *refs):
-    weights, (*base_ref, y_ref, u_ref) = refs[: 3 * n_sets], refs[3 * n_sets :]
-    for s in range(n_sets):
-        w1, w3, w2 = weights[3 * s : 3 * s + 3]
-
-        def step(i, _):
-            cols = pl.ds(pl.multiple_of(i * FF_STEP, FF_STEP), FF_STEP)
-            act_a = mm(x_ref[...], w1[:, cols])
-            act_b = mm(x_ref[...], w3[:, cols])
-            u_ref[:, cols] = (act_a * jax.nn.sigmoid(act_a) * act_b).astype(BF16)
-            return 0
-
-        lax.fori_loop(0, w1.shape[1] // FF_STEP, step, 0)
-        part = mm(u_ref[...], w2[...])
-        if s > 0:
-            y_ref[...] += part
-        elif base_ref:
-            y_ref[...] = base_ref[0][...] + part
+def sum_into(out_ref, base_ref, first, product):
+    def step(i, _):
+        cols = pl.ds(pl.multiple_of(i * FF_STEP, FF_STEP), FF_STEP)
+        if not first:
+            out_ref[:, cols] += product(cols)
+        elif base_ref is not None:
+            out_ref[:, cols] = base_ref[:, cols] + product(cols)
         else:
-            y_ref[...] = part
-
-
-def ffn_fwd(x, sets, tile, first, n_tiles, base=()):
-    d_model, d_ff = sets[0].shape
+            out_ref[:, cols] = product(cols)
+        return 0
+
+    lax.fori_loop(0, out_ref.shape[1] // FF_STEP, step, 0, unroll=True)
+
+
+def act_kernel(with_y, n_alias, x_ref, *refs):
+    (w1, w3, *w2), refs = refs[: 2 + with_y], refs[2 + with_y + n_alias :]
+    a_ref, b_ref, u_ref = refs[:3]
+
+    def step(i, _):
+        cols = pl.ds(pl.multiple_of(i * FF_STEP, FF_STEP), FF_STEP)
+        act_a = mm(x_ref[...], w1[:, cols])
+        act_b = mm(x_ref[...], w3[:, cols])
+        a_ref[:, cols] = act_a
+        b_ref[:, cols] = act_b
+        u_ref[:, cols] = (act_a * jax.nn.sigmoid(act_a) * act_b).astype(BF16)
+        return 0
+
+    lax.fori_loop(0, w1.shape[1] // FF_STEP, step, 0, unroll=True)
+    if with_y:
+        sum_into(refs[3], None, True, lambda cols: mm(u_ref[...], w2[0][:, cols]))
+
+
+def ffn_act(x, weights, tile, first, n_tiles, kept, total):
+    d_model, d_ff = weights[0].shape
+    with_y = len(weights) == 3
     rows = n_tiles * tile
-    n_sets = len(sets) // 3
-    return pl.pallas_call(
-        functools.partial(fwd_kernel, n_sets),
+    out_specs = [pl.BlockSpec((tile, d_ff), lambda i: (i + first, 0))] * 3
+    out_shape = [jax.ShapeDtypeStruct((total, d_ff), dtype) for dtype in (F32, F32, BF16)]
+    if with_y:
+        out_specs.append(pl.BlockSpec((tile, d_model), lambda i: (i, 0)))
+        out_shape.append(jax.ShapeDtypeStruct((rows, d_model), F32))
+    n_in = 1 + len(weights)
+    return pl.pallas_call(
+        functools.partial(act_kernel, with_y, len(kept)),
         grid=(n_tiles,),
-        in_specs=[pl.BlockSpec((tile, d_model), lambda i: (i + first, 0))] + [whole(w) for w in sets] + [pl.BlockSpec((tile, d_model), lambda i: (i + first, 0))] * len(base),
+        in_specs=[pl.BlockSpec((tile, d_model), lambda i: (i + first, 0))] + [whole(w) for w in weights] + [pl.BlockSpec(memory_space=pl.ANY)] * len(kept),
+        out_specs=out_specs,
+        out_shape=out_shape,
+        input_output_aliases={n_in + i: i for i in range(len(kept))},
+        compiler_params=params(60),
+        cost_estimate=pl.CostEstimate(flops=2 * len(weights) * rows * d_model * d_ff, bytes_accessed=6 * d_model * d_ff + 10 * rows * d_ff, transcendentals=rows * d_ff),
+        name="ffn_act",
+    )(x, *weights, *kept)
+
+
+def down_kernel(u_ref, w2, y_in, y_ref):
+    sum_into(y_ref, y_in, True, lambda cols: mm(u_ref[...], w2[:, cols]))
+
+
+def ffn_down(u, w2, y_in, tile, first):
+    d_ff, d_model = w2.shape
+    return pl.pallas_call(
+        down_kernel,
+        grid=(1,),
+        in_specs=[pl.BlockSpec((tile, d_ff), lambda i: (i + first, 0)), whole(w2), pl.BlockSpec((tile, d_model), lambda i: (i + first, 0))],
         out_specs=pl.BlockSpec((tile, d_model), lambda i: (i, 0)),
-        out_shape=jax.ShapeDtypeStruct((rows, d_model), F32),
-        scratch_shapes=[pltpu.VMEM((tile, d_ff), BF16)],
-        compiler_params=params(56),
-        cost_estimate=pl.CostEstimate(flops=6 * rows * d_model * d_ff * n_sets, bytes_accessed=6 * d_model * d_ff * n_sets + 6 * rows * d_model, transcendentals=rows * d_ff * n_sets),
-        name="ffn_fwd",
-    )(x, *sets, *base)
+        out_shape=jax.ShapeDtypeStruct((tile, d_model), F32),
+        compiler_params=params(48),
+        cost_estimate=pl.CostEstimate(flops=2 * tile * d_model * d_ff, bytes_accessed=2 * d_model * d_ff + 8 * tile * d_model, transcendentals=0),
+        name="ffn_down",
+    )(u, w2, y_in)
+
+
+def grad_kernel(with_dx, keeps, n_base, n_alias, c_ref, a_ref, b_ref, *refs):
+    n_w = 3 if with_dx else 1
+    (w2, *w13), base, refs = refs[:n_w], refs[n_w : n_w + n_base], list(refs[n_w + n_base + n_alias :])
+    dx_ref = refs.pop(2 if keeps else 0) if with_dx else None
+    da_ref, db_ref = refs
+
+    def step(i, _):
+        cols = pl.ds(pl.multiple_of(i * FF_STEP, FF_STEP), FF_STEP)
+        d_inner = mm_nt(c_ref[...], w2[cols, :])
+        act_a = a_ref[:, cols]
+        sig_a = jax.nn.sigmoid(act_a)
+        da_ref[:, cols] = (d_inner * b_ref[:, cols] * sig_a * (1.0 + act_a * (1.0 - sig_a))).astype(BF16)
+        db_ref[:, cols] = (d_inner * (act_a * sig_a)).astype(BF16)
+        return 0
+
+    lax.fori_loop(0, w2.shape[0] // FF_STEP, step, 0, unroll=True)
+    if with_dx:
+        w1, w3 = w13
+        sum_into(dx_ref, base[0] if base else None, True, lambda cols: mm_nt(da_ref[...], w1[cols, :]) + mm_nt(db_ref[...], w3[cols, :]))
+
+
+def ffn_grad(c, act_a, act_b, weights, tile, first, first_act, n_tiles, kept, total=0, base=()):
+    w2, *w13 = weights
+    d_ff, d_model = w2.shape
+    with_dx = bool(w13)
+    rows = n_tiles * tile
+    at = lambda width, start: pl.BlockSpec((tile, width), lambda i: (i + start, 0))
+    out_specs = [at(d_ff, first)] * 2 if total else []
+    out_shape = [jax.ShapeDtypeStruct((total, d_ff), BF16)] * 2 if total else []
+    if with_dx:
+        out_specs.append(at(d_model, 0))
+        out_shape.append(jax.ShapeDtypeStruct((rows, d_model), F32))
+    n_in = 3 + len(weights) + len(base)
+    return pl.pallas_call(
+        functools.partial(grad_kernel, with_dx, bool(total), len(base), len(kept)),
+        grid=(n_tiles,),
+        in_specs=[at(d_model, first), at(d_ff, first_act), at(d_ff, first_act)] + [whole(w) for w in weights] + [at(d_model, first)] * len(base) + [pl.BlockSpec(memory_space=pl.ANY)] * len(kept),
+        out_specs=out_specs,
+        out_shape=out_shape,
+        scratch_shapes=[] if total else [pltpu.VMEM((tile, d_ff), BF16)] * 2,
+        input_output_aliases={n_in + i: i for i in range(len(kept))},
+        compiler_params=params(62),
+        cost_estimate=pl.CostEstimate(flops=2 * len(weights) * rows * d_model * d_ff, bytes_accessed=6 * d_model * d_ff + 12 * rows * d_ff, transcendentals=rows * d_ff),
+        name="ffn_grad",
+    )(c, act_a, act_b, *weights, *base, *kept)
 
 
 def bwd_kernel(n_sets, with_dx, with_y, n_alias, x_ref, c_ref, *refs):
@@ -156,19 +387,11 @@
             db[:, cols] = (d_inner * silu_a).astype(BF16)
             return 0
 
-        lax.fori_loop(0, w1.shape[1] // FF_STEP, step, 0)
+        lax.fori_loop(0, w1.shape[1] // FF_STEP, step, 0, unroll=True)
         if with_dx:
-            part = mm_nt(da[...], w1[...]) + mm_nt(db[...], w3[...])
-            if s == 0:
-                dx_ref[...] = part
-            else:
-                dx_ref[...] += part
+            sum_into(dx_ref, None, s == 0, lambda cols: mm_nt(da[...], w1[cols, :]) + mm_nt(db[...], w3[cols, :]))
         if with_y:
-            part = mm(u[...], w2[...])
-            if s == 0:
-                y_ref[...] = part
-            else:
-                y_ref[...] += part
+            sum_into(y_ref, None, s == 0, lambda cols: mm(u[...], w2[:, cols]))
 
 
 def ffn_bwd(x, c, sets, tile, first, n_tiles, kept, with_dx=True, with_y=False):
@@ -195,6 +418,50 @@
         cost_estimate=pl.CostEstimate(flops=(6 + 4 * with_dx + 2 * with_y) * rows * d_model * d_ff * n_sets, bytes_accessed=6 * d_model * d_ff * n_sets + 8 * rows * (d_model + d_ff), transcendentals=rows * d_ff * n_sets),
         name="ffn_bwd",
     )(x, c, *sets, *kept)
+
+
+def pair_kernel(x_ref, c_ref, y_in, dx_in, w1, w3, w2, y_ref, dx_ref, u_ref, da_ref, db_ref):
+    def step(i, _):
+        cols = pl.ds(pl.multiple_of(i * FF_STEP, FF_STEP), FF_STEP)
+        act_a = mm(x_ref[...], w1[:, cols])
+        act_b = mm(x_ref[...], w3[:, cols])
+        d_inner = mm_nt(c_ref[...], w2[cols, :])
+        sig_a = jax.nn.sigmoid(act_a)
+        silu_a = act_a * sig_a
+        u_ref[:, cols] = (silu_a * act_b).astype(BF16)
+        da_ref[:, cols] = (d_inner * act_b * sig_a * (1.0 + act_a * (1.0 - sig_a))).astype(BF16)
+        db_ref[:, cols] = (d_inner * silu_a).astype(BF16)
+        return 0
+
+    lax.fori_loop(0, w1.shape[1] // FF_STEP, step, 0, unroll=True)
+    sum_into(y_ref, y_in, True, lambda cols: mm(u_ref[...], w2[:, cols]))
+    sum_into(dx_ref, dx_in, True, lambda cols: mm_nt(da_ref[...], w1[cols, :]) + mm_nt(db_ref[...], w3[cols, :]))
+
+
+def ffn_pair(x, c, y_in, dx_in, weights, tile, first, n_tiles, first_dx):
+    d_model, d_ff = weights[0].shape
+    rows = n_tiles * tile
+    at = lambda start: pl.BlockSpec((tile, d_model), lambda i: (i + start, 0))
+    return pl.pallas_call(
+        pair_kernel,
+        grid=(n_tiles,),
+        in_specs=[at(first), at(first), at(first), at(first_dx)] + [whole(w) for w in weights],
+        out_specs=[at(0)] * 2,
+        out_shape=[jax.ShapeDtypeStruct((rows, d_model), F32)] * 2,
+        scratch_shapes=[pltpu.VMEM((tile, d_ff), BF16)] * 3,
+        compiler_params=params(60),
+        cost_estimate=pl.CostEstimate(flops=12 * rows * d_model * d_ff, bytes_accessed=6 * d_model * d_ff + 20 * rows * d_model, transcendentals=rows * d_ff),
+        name="ffn_pair",
+    )(x, c, y_in, dx_in, *weights)
+
+
+def unset(*shapes):
+    return pl.pallas_call(
+        lambda *refs: None,
+        out_specs=[pl.BlockSpec(memory_space=pl.ANY)] * len(shapes),
+        out_shape=[jax.ShapeDtypeStruct(shape, BF16) for shape in shapes],
+        name="unset",
+    )()
 
 
 def home_kernel(win, n_far, start_ref, near_ref, *refs):
@@ -210,12 +477,16 @@
     out_rows = out_ref.shape[1]
     to = lax.broadcasted_iota(jnp.int32, (out_rows, win), 0)
     frm = lax.broadcasted_iota(jnp.int32, (out_rows, win), 1)
-    for o in range(out_ref.shape[0]):
+
+    def block(o, _):
         start = start_ref[o]
         base = pl.multiple_of(start // 8 * 8, 8)
         rows = sum_ref[pl.ds(base, win), :].astype(BF16)
         move = (frm == to + (start - base)).astype(F32).astype(BF16)
         out_ref[o] = mm(move, rows).astype(BF16)
+        return 0
+
+    lax.fori_loop(0, out_ref.shape[0], block, 0)
 
 
 def home_blocks(starts, near, fars, more, out_rows):
@@ -259,7 +530,7 @@
         list_max = ep_size * per_expert
         main_rows = 23 * tok_rows // 8
         more_rows = list_max - main_rows
-        tile = main_rows // 2
+        tile = main_rows // 4
         win = per_expert + 8
         ep_i = lax.axis_index("ep")
         etp_i = lax.axis_index("etp")
@@ -270,20 +541,13 @@
             pairs = [(t * ep_size + o, (odd if o % 2 else even)[t] * ep_size + o) for t in range(etp_size) for o in range(ep_size)]
             return lax.ppermute(array, ("etp", "ep"), pairs)
 
-        def spread(array):
-            shifts = range(1, etp_size)
-            moved = [lax.ppermute(array, "etp", [(t, (t + k) % etp_size) for t in range(etp_size)]) for k in shifts]
-            return [array] + moved
-
         ids_row = expert_ids.T.astype(BF16).reshape(1, 2 * tok_rows)
         ids_row = jnp.concatenate([ids_row, jnp.zeros((7, 2 * tok_rows), BF16)])
-        h_col = lax.all_gather(jnp.concatenate([hidden, ids_row]), "etp")
-        w1_b, w3_b, w2_b, dy_b, h_col = lax.optimization_barrier((w1, w3, w2, d_out, h_col))
-        dy_parts = spread(dy_b)
-        w1p, w3p, w2p = [swap(w, NEXT_PAIRS, ENDS_PAIRS) for w in (w1_b, w3_b, w2_b)]
-        h_all = lax.all_gather(h_col, "ep").reshape(n_dev, tok_rows + 8, d_model)
-        *dy_parts, h_all = lax.optimization_barrier((*dy_parts, h_all))
-        dy_col = jnp.stack(dy_parts)
+        h_all, dy_col = spread_all(jnp.concatenate([hidden, ids_row]), d_out, etp_size, ep_size)
+        w1_b, w3_b, w2_b, h_all, dy_col = lax.optimization_barrier((w1, w3, w2, h_all, dy_col))
+        w1p = swap(w1_b, NEXT_PAIRS, ENDS_PAIRS)
+        w3p = swap(w3_b, NEXT_PAIRS, ENDS_PAIRS)
+        w2p = swap(w2_b, NEXT_PAIRS, ENDS_PAIRS)
         dy_all = lax.all_gather(dy_col, "ep").reshape(n_dev, tok_rows, d_model)
 
         ids_all = h_all[:, tok_rows, :].astype(jnp.int32).reshape(n_dev, 2, tok_rows)
@@ -309,7 +573,6 @@
         pick = functools.partial(pick_rows, win=win, n_src=ep_size, n_etp=etp_size)
         main_pos = jnp.where(my_pos < main_rows, my_pos, -1)
         main_base = my_base.T[planes]
-        dy_slots = (etp_i - planes) % etp_size
         x_main = pick(h_all, main_pos, None, planes, planes, main_base, main_rows)
 
         route_w = jnp.concatenate(split3(w_router), axis=1)
@@ -321,40 +584,44 @@
         my_gate = lax.dynamic_index_in_dim(picked_all, ep_i, 0, keepdims=False) / jnp.sum(picked_all, axis=0)
         mean_prob = jnp.sum(probs_all, axis=1) / n_tokens
         my_scale = OUT_SCALE * my_gate.reshape(n_dev, tok_rows)
-        c_main = pick(dy_all, main_pos, my_scale, planes, dy_slots, main_base, main_rows)
-
-        own, pair = (w1, w3, w2), (w1p, w3p, w2p)
-        y_base = ffn_fwd(x_main, own, tile, 0, 2)
-        y_far = []
+        c_main = pick(dy_all, main_pos, my_scale, planes, planes, main_base, main_rows)
+
+        n_rows = x_main.shape[0]
+        *acts, y_base = ffn_act(x_main, (w1, w3, w2), tile, 0, 8, (), n_rows)
+        act_a, act_b, inner = ffn_act(x_main, (w1, w3), tile, 8, 8, acts, n_rows)
+        far_a, far_b, far_u = ffn_act(x_main, (w1p, w3p), tile, 0, 4, (), main_rows)
+        *grads, dx_base = ffn_grad(c_main, act_a, act_b, (w2, w1, w3), tile, 0, 0, 4, (), n_rows)
+        y_far, dx_far = [], []
         for i in range(2):
-            y_part = ffn_fwd(x_main, pair, tile, i, 1, (y_base,))
+            y_part = ffn_down(far_u, w2p, y_base, 2 * tile, i)
             y_far.append(swap(y_part, ENDS_PAIRS, NEXT_PAIRS))
-        dx_far, acts = [], ()
         for i in range(2):
-            *acts, dx_part = ffn_bwd(x_main, c_main, own + pair, tile, i, 1, acts)
+            (dx_part,) = ffn_grad(c_main, far_a, far_b, (w2p, w1p, w3p), tile, 2 * i, 2 * i, 2, (), base=(dx_base,))
             dx_far.append(swap(dx_part, ENDS_PAIRS, NEXT_PAIRS))
-        *acts, dx_near, y_near = ffn_bwd(x_main, c_main, own + pair, tile // 2, 4, 4, acts, with_y=True)
-        inner, d_a, d_b = ffn_bwd(x_main, c_main, own, tile, 4, 4, acts, with_dx=False)
-
-        def more_work():
+        *grads, dx_base = ffn_grad(c_main, act_a, act_b, (w2, w1, w3), tile, 4, 4, 4, grads, n_rows)
+        y_near, dx_near = ffn_pair(x_main, c_main, y_base, dx_base, (w1p, w3p, w2p), tile, 4, 4, 0)
+        d_a, d_b = ffn_grad(c_main, act_a, act_b, (w2,), tile, 8, 8, 8, grads, n_rows)
+
+        def more_work(*_):
             more_pos = jnp.where(my_pos >= main_rows, my_pos - main_rows, -1)
             more_base = jnp.clip(my_start.T - main_rows, 0, more_rows) // 8 * 8
             order = jnp.arange(etp_size, dtype=jnp.int32)
             x_more = pick(h_all, more_pos, None, order, order, more_base, more_rows)
-            c_more = pick(dy_all, more_pos, my_scale, order, (etp_i - order) % etp_size, more_base, more_rows)
-            inner, d_a, d_b, dx_part, y_part = ffn_bwd(x_more, c_more, own, more_rows, 0, etp_size, (), with_y=True)
+            c_more = pick(dy_all, more_pos, my_scale, order, order, more_base, more_rows)
+            *acts, dx_part, y_part = ffn_bwd(x_more, c_more, (w1, w3, w2), more_rows, 0, etp_size, (), with_y=True)
             y_more = lax.psum_scatter(y_part, "etp", scatter_dimension=0, tiled=True)
             dx_more = lax.psum_scatter(dx_part, "etp", scatter_dimension=0, tiled=True)
-            return y_more.astype(BF16), dx_more.astype(BF16), x_more, c_more, inner, d_a, d_b
-
-        def no_more_work():
-            none = jnp.zeros((more_rows, d_model), BF16)
-            rows = jnp.zeros((etp_size * more_rows, d_model), BF16)
-            acts = jnp.zeros((etp_size * more_rows, w1.shape[1]), BF16)
-            return none, none, rows, rows, acts, acts, acts
-
+            return y_more.astype(BF16), dx_more.astype(BF16), x_more, c_more, *acts
+
+        n_more = etp_size * more_rows
+        none = jnp.zeros((more_rows, d_model), BF16)
+        spare = none, none, *unset(*[(n_more, d_model)] * 2, *[(n_more, w1.shape[1])] * 3)
         any_more = jnp.max(list_len) > main_rows
-        y_more, dx_more, *more = lax.cond(any_more, more_work, no_more_work)
+        y_more, dx_more, x_more, c_more, *more_acts = lax.cond(any_more, more_work, lambda *spare: spare, *spare)
+
+        def more_grads(*grads):
+            inner_more, d_a_more, d_b_more = more_acts
+            return grads[0] + mm_tn(x_more, d_a_more), grads[1] + mm_tn(x_more, d_b_more), grads[2] + mm_tn(inner_more, c_more)
 
         home_start = lax.dynamic_index_in_dim(my_start, etp_i, 1, keepdims=False)
 
@@ -377,7 +644,10 @@
             slot_k = jnp.where(rank_k < kept_k, expert_ids[:, k : k + 1] * per_expert + rank_k.astype(jnp.int32), -1)
             chosen.append(slot_k == slot_row)
 
+        dw1 = mm_tn(x_main, d_a)
+        y_near, dw1, x_main = lax.optimization_barrier((y_near, dw1, x_main))
         y_back = send_home(y_near, y_far, y_more)
+        dw3 = mm_tn(x_main, d_b)
         y_pair = [mm(chosen[k].astype(BF16), y_back) for k in range(2)]
         hidden_f = hidden.astype(F32)
         output = (hidden_f + OUT_SCALE * (gates[0] * y_pair[0] + gates[1] * y_pair[1])).astype(BF16)
@@ -392,19 +662,12 @@
             d_probs = d_probs + hot[k] * ((d_gates[k] - mix) / pick_sum)
         d_logits = probs * (d_probs - jnp.sum(probs * d_probs, axis=1, keepdims=True))
         d_router_part = lax.dot_general(d_logits, hidden_f, (((0,), (0,)), ((), ())), precision=lax.Precision.HIGHEST, preferred_element_type=F32)
-        x_main, c_main, inner, d_router_part = lax.optimization_barrier((x_main, c_main, inner, d_router_part))
+        dx_near, dw3, d_router_part = lax.optimization_barrier((dx_near, dw3, d_router_part))
         d_router = jnp.sum(lax.all_gather(d_router_part, ALL_AXES), axis=0).T
-        dw1 = mm_tn(x_main, d_a)
-        dw3 = mm_tn(x_main, d_b)
-        dx_near, dw1, dw3 = lax.optimization_barrier((dx_near, dw1, dw3))
         dx_back = send_home(dx_near, dx_far, dx_more)
         dw2 = mm_tn(inner, c_main)
 
-        def add_more(*grads):
-            x_more, c_more, inner_more, d_a_more, d_b_more = more
-            return grads[0] + mm_tn(x_more, d_a_more), grads[1] + mm_tn(x_more, d_b_more), grads[2] + mm_tn(inner_more, c_more)
-
-        dw1, dw3, dw2 = lax.cond(any_more, add_more, lambda *grads: grads, dw1, dw3, dw2)
+        dw1, dw3, dw2 = lax.cond(any_more, more_grads, lambda *grads: grads, dw1, dw3, dw2)
         d_route = lax.dot_general(d_logits, w_router, (((1,), (1,)), ((), ())), precision=lax.Precision.HIGHEST, preferred_element_type=F32)
         dx_sum = mm((chosen[0] | chosen[1]).astype(BF16), dx_back)
         d_hidden = (d_out_f + dx_sum + d_route).astype(BF16)

time: 993 us -> 800 us (0.81)
  waiting for transfers between devices: 408 us -> 121 us
  Pallas kernels: 353 us -> 468 us
  local copies, waits for them, and re-layouts: 30.5 us -> 15.6 us
    all_gather x2 -> x0, waiting for transfers between devices: 158 us -> none  [the longest x1 84.7 us: layer(): h_col = lax.all_gather(jnp.concatenate([hidden, ids_row]), 'etp')]
    pallas_call x7 -> x13, Pallas kernels: 278 us -> 413 us  [the longest x1 149 us: spread_all(): pl.pallas_call(functools.partial(spread_kernel, n_etp), in_specs=[vmem, v...]
    ppermute x3 -> x0, waiting for transfers between devices: 88.4 us -> none  [spread(): lax.ppermute(array, 'etp', [(t, (t + k) % etp_size) for t in range(etp_si...]
    ppermute x7, waiting for transfers between devices: 154 us -> 114 us  [swap(): return lax.ppermute(array, ('etp', 'ep'), pairs)]
    pallas_call x2, Pallas kernels: 61.5 us -> 41.3 us  [pick_rows(): pl.pallas_call(functools.partial(pick_kernel, gates is not None, win), gr...]
    another operation x7 -> x0, local copies, waits for them, and re-layouts: 11.9 us -> none
  transfers between devices with their start and end apart: 16 -> 11, of which waited for: 9 -> 4; matrix products, arithmetic and copies ran while one was open for 15% -> 18% of each run, Pallas kernels for 35% -> 40%
where the time goes in v2:
time: 800 us; the launch traced here: 790 us
  Pallas kernels  468 us (58%)
  matrix products  128 us (16%)
  waiting for transfers between devices  121 us (15%)
  starting transfers between devices  20.5 us (3%)
  other arithmetic  18.4 us (2%)
  between operations  17.3 us (2%)
  local copies, waits for them, and re-layouts  15.6 us (2%)
    pallas_call x1, Pallas kernels, spread_all(): pl.pallas_call(functools.partial(spread_kernel, n_etp), in_specs=[vmem, v...  149 us
    pallas_call x5, Pallas kernels, ffn_grad(): pl.pallas_call(functools.partial(grad_kernel, with_dx, bool(total), len(b...  119 us
    ppermute x7, waiting for transfers between devices, swap(): return lax.ppermute(array, ('etp', 'ep'), pairs)  114 us
    dot_general x4, matrix products, mm_tn(): lax.dot_general(lhs, rhs, (((0,), (0,)), ((), ())), preferred_element_typ...  89.9 us
    pallas_call x3, Pallas kernels, ffn_act(): pl.pallas_call(functools.partial(act_kernel, with_y, len(kept)), grid=(n_...  87.2 us
    pallas_call x1, Pallas kernels, ffn_pair(): pl.pallas_call(pair_kernel, grid=(n_tiles,), in_specs=[at(first), at(firs...  41.5 us
    pallas_call x2, Pallas kernels, pick_rows(): pl.pallas_call(functools.partial(pick_kernel, gates is not None, win), gr...  41.3 us
    dot_general x1, matrix products, layer(): lax.dot_general(route_w, h_all, (((0,), (2,)), ((), ())), preferred_eleme...  17.4 us
  transfers between devices with their start and end apart: 11, of which 4 were waited for; matrix products, arithmetic and copies ran while one was open for 18% of the time, Pallas kernels for 40%

profile of v2, /device:TPU:0, one launch (start us, length us, event | category | flops | bytes accessed | tf_op | source)
XLA Modules:
  0.0 790.3 jit_solution(12336013774515185924)
XLA Ops:
  10.7 148.7 %spread_all.1 = (bf16[32,520,1024]{2,1,0:T(8,128)(2,1)}, bf16[4,512,1024]{2,1,0:T(8,128)(2,1)S(1)}) custom-call(bf16[520,1024]{1,0:T(8,128)(2,1)S(1)} %maximum_maximum_fusion.h_ref, bf16[512,1024]{1,0:T(8,128)(2,1)S(1)} %copy-done.3), custom_call_target="tpu_custom_call" | custom-call | flops 99999997952 | bytes 34078720 | tf_op jit(solution)/shard_map/spread_all/pallas_call | solution.py:172
  170.6 17.4 %fusion.30 = f32[24,32,520]{2,0,1:T(8,128)S(1)} fusion(bf16[32,520,1024]{2,1,0:T(8,128)(2,1)} %get-tuple-element.152, bf16[1024,8]{0,1:T(8,128)(2,1)S(1)} %get-tuple-element.224, bf16[1024,8]{0,1:T(8,128)(2,1)S(1)} %get-tuple-element.225, bf16[1024,8]{0,1:T(8,128)(2,1)S(1)} %get-tuple-element.223), kind=kOutput, calls=%fused_computation.68 | convolution fusion | flops 818036736 | bytes 35725312 | tf_op jit(solution)/shard_map/dot_general | solution.py:579
  191.6 20.9 %pick_rows.6.x_ref = bf16[5888,1024]{1,0:T(8,128)(2,1)} custom-call(s32[4]{0:T(128)} %pad_add_fusion.planes_ref.slots_ref, s32[4]{0:T(128)} %pad_add_fusion.planes_ref.slots_ref, s32[4,8]{1,0:T(4,128)} %gather_fusion, bf16[8,4,520,1024]{3,2,1,0:T(8,128)(2,1)} %bitcast.129, s32[8,4,1,512]{3,2,1,0:T(1,128)} %reshape.391.pos_ref), custom_call_target="tpu_custom_call" | custom-call | flops 7784628224 | bytes 68157440 | tf_op jit(solution)/shard_map/pick_rows/pallas_call | solution.py:226
  213.6 39.7 %ffn_act.3 = (f32[5888,1792]{1,0:T(8,128)}, f32[5888,1792]{1,0:T(8,128)}, bf16[5888,1792]{1,0:T(8,128)(2,1)}, f32[2944,1024]{1,0:T(8,128)}) custom-call(bf16[5888,1024]{1,0:T(8,128)(2,1)} %pick_rows.6.x_ref, bf16[1024,1792]{1,0:T(8,128)(2,1)S(1)} %bitcast.138, bf16[1024,1792]{1,0:T(8,128)(2,1)} %bitcast.140, bf16[1792,1024]{1,0:T(8,128)(2,1)} %bitcast.146), custom_call_target="tpu_custom_call" | custom-call | flops 32413581312 | bytes 63766528 | tf_op jit(solution)/shard_map/ffn_act/pallas_call | solution.py:288
  262.4 29.7 %ffn_act.4 = (f32[5888,1792]{1,0:T(8,128)}, f32[5888,1792]{1,0:T(8,128)}, bf16[5888,1792]{1,0:T(8,128)(2,1)}) custom-call(bf16[5888,1024]{1,0:T(8,128)(2,1)} %pick_rows.6.x_ref, bf16[1024,1792]{1,0:T(8,128)(2,1)} %bitcast.134, bf16[1024,1792]{1,0:T(8,128)(2,1)} %bitcast.141, ...), custom_call_target="tpu_custom_call", output_to_operand_aliasing={{0}: (3, {}), {1}: (4, {}), {2}: (5, {})} | custom-call | flops 21609054208 | bytes 63766528 | tf_op jit(solution)/shard_map/ffn_act/pallas_call | solution.py:288
  292.1 30.1 %collective-permute-done.1.w3.refs_1_.refs_2_ = bf16[1024,1792]{1,0:T(8,128)(2,1)} collective-permute-done((bf16[1024,1792]{1,0:T(8,128)(2,1)}, bf16[1024,1792]{1,0:T(8,128)(2,1)}, u32[]{:S(2)}, u32[]{:S(2)}) %collective-permute-start.1) | collective-permute-done | bytes 3670048 | tf_op jit(solution)/shard_map/ppermute | solution.py:542
  322.2 17.9 %ffn_act.5 = (f32[1472,1792]{1,0:T(8,128)}, f32[1472,1792]{1,0:T(8,128)}, bf16[1472,1792]{1,0:T(8,128)(2,1)}) custom-call(bf16[5888,1024]{1,0:T(8,128)(2,1)} %pick_rows.6.x_ref, bf16[1024,1792]{1,0:T(8,128)(2,1)} %collective-permute-done.w1.refs_0_.refs_1_, bf16[1024,1792]{1,0:T(8,128)(2,1)} %collective-permute-done.1.w3.refs_1_.refs_2_), custom_call_target="tpu_custom_call" | custom-call | flops 10804527104 | bytes 37388288 | tf_op jit(solution)/shard_map/ffn_act/pallas_call | solution.py:288
  340.1 60.8 %collective-permute-done.2.w2.refs_0_ = bf16[1792,1024]{1,0:T(8,128)(2,1)} collective-permute-done((bf16[1792,1024]{1,0:T(8,128)(2,1)}, bf16[1792,1024]{1,0:T(8,128)(2,1)}, u32[]{:S(2)}, u32[]{:S(2)}) %collective-permute-start.2) | collective-permute-done | bytes 3670048 | tf_op jit(solution)/shard_map/ppermute | solution.py:542
  400.8 8.2 %ffn_down.2 = f32[736,1024]{1,0:T(8,128)} custom-call(bf16[1472,1792]{1,0:T(8,128)(2,1)} %get-tuple-element.171.u_ref, bf16[1792,1024]{1,0:T(8,128)(2,1)} %collective-permute-done.2.w2.refs_0_, f32[2944,1024]{1,0:T(8,128)} %get-tuple-element.154.y_in), custom_call_target="tpu_custom_call" | custom-call | flops 2701131776 | bytes 9699328 | tf_op jit(solution)/shard_map/ffn_down/pallas_call | solution.py:307
  410.8 8.3 %ffn_down.3 = f32[736,1024]{1,0:T(8,128)} custom-call(bf16[1472,1792]{1,0:T(8,128)(2,1)} %get-tuple-element.171.u_ref, bf16[1792,1024]{1,0:T(8,128)(2,1)} %collective-permute-done.2.w2.refs_0_, f32[2944,1024]{1,0:T(8,128)} %get-tuple-element.154.y_in), custom_call_target="tpu_custom_call" | custom-call | flops 2701131776 | bytes 9699328 | tf_op jit(solution)/shard_map/ffn_down/pallas_call | solution.py:307
  421.2 20.4 %pick_rows.7.c_ref = bf16[5888,1024]{1,0:T(8,128)(2,1)} custom-call(s32[4]{0:T(128)} %pad_add_fusion.planes_ref.slots_ref, s32[4]{0:T(128)} %pad_add_fusion.planes_ref.slots_ref, s32[4,8]{1,0:T(4,128)} %gather_fusion, bf16[8,4,512,1024]{3,2,1,0:T(8,128)(2,1)} %bitcast.131, s32[8,4,1,512]{3,2,1,0:T(1,128)} %reshape.391.pos_ref, ...), custom_call_target="tpu_custom_call" | custom-call | flops 7784628224 | bytes 67108864 | tf_op jit(solution)/shard_map/pick_rows/pallas_call | solution.py:226
  441.6 26.7 %ffn_grad.5 = (bf16[5888,1792]{1,0:T(8,128)(2,1)}, bf16[5888,1792]{1,0:T(8,128)(2,1)}, f32[1472,1024]{1,0:T(8,128)}) custom-call(bf16[5888,1024]{1,0:T(8,128)(2,1)} %pick_rows.7.c_ref, f32[5888,1792]{1,0:T(8,128)} %get-tuple-element.158.a_ref, f32[5888,1792]{1,0:T(8,128)} %get-tuple-element.159.b_ref, bf16[1792,1024]{1,0:T(8,128)(2,1)} %bitcast.147, ...), custom_call_target="tpu_custom_call" | custom-call | flops 16206790656 | bytes 42663936 | tf_op jit(solution)/shard_map/ffn_grad/pallas_call | solution.py:352
  468.3 17.4 %ffn_grad.8 = f32[736,1024]{1,0:T(8,128)} custom-call(bf16[5888,1024]{1,0:T(8,128)(2,1)} %pick_rows.7.c_ref, f32[1472,1792]{1,0:T(8,128)} %get-tuple-element.177.a_ref, f32[1472,1792]{1,0:T(8,128)} %get-tuple-element.178.b_ref, bf16[1792,1024]{1,0:T(8,128)(2,1)} %collective-permute-done.2.w2.refs_0_, ...), custom_call_target="tpu_custom_call" | custom-call | flops 8103395328 | bytes 26836992 | tf_op jit(solution)/shard_map/ffn_grad/pallas_call | solution.py:352
  487.4 26.3 %ffn_grad.6 = (bf16[5888,1792]{1,0:T(8,128)(2,1)}, bf16[5888,1792]{1,0:T(8,128)(2,1)}, f32[1472,1024]{1,0:T(8,128)}) custom-call(bf16[5888,1024]{1,0:T(8,128)(2,1)} %pick_rows.7.c_ref, f32[5888,1792]{1,0:T(8,128)} %get-tuple-element.158.a_ref, f32[5888,1792]{1,0:T(8,128)} %get-tuple-element.159.b_ref, ...), custom_call_target="tpu_custom_call", output_to_operand_aliasing={{0}: (6, {}), {1}: (7, {})} | custom-call | flops 16206790656 | bytes 42663936 | tf_op jit(solution)/shard_map/ffn_grad/pallas_call | solution.py:352
  513.7 30.8 %ffn_grad.7 = (bf16[5888,1792]{1,0:T(8,128)(2,1)}, bf16[5888,1792]{1,0:T(8,128)(2,1)}) custom-call(bf16[5888,1024]{1,0:T(8,128)(2,1)} %pick_rows.7.c_ref, f32[5888,1792]{1,0:T(8,128)} %get-tuple-element.158.a_ref, f32[5888,1792]{1,0:T(8,128)} %get-tuple-element.159.b_ref, ...), custom_call_target="tpu_custom_call", output_to_operand_aliasing={{0}: (4, {}), {1}: (5, {})} | custom-call | flops 10804527104 | bytes 74317824 | tf_op jit(solution)/shard_map/ffn_grad/pallas_call | solution.py:352
  544.5 29.7 %fusion.56 = f32[1024,1792]{1,0:T(8,128)} fusion(bf16[5888,1024]{1,0:T(8,128)(2,1)} %pick_rows.6.x_ref, bf16[5888,1792]{1,0:T(8,128)(2,1)} %get-tuple-element.169), kind=kOutput, calls=%fused_computation.132 | convolution fusion | flops 21609054208 | bytes 40501248 | tf_op jit(solution)/shard_map/dot_general | solution.py:31
  574.2 41.5 %ffn_pair.1 = (f32[1472,1024]{1,0:T(8,128)}, f32[1472,1024]{1,0:T(8,128)}) custom-call(bf16[5888,1024]{1,0:T(8,128)(2,1)} %pick_rows.6.x_ref, bf16[5888,1024]{1,0:T(8,128)(2,1)} %pick_rows.7.c_ref, f32[2944,1024]{1,0:T(8,128)} %get-tuple-element.154.y_in, f32[1472,1024]{1,0:T(8,128)} %get-tuple-element.162.dx_in, ...), custom_call_target="tpu_custom_call" | custom-call | flops 32413581312 | bytes 41156608 | tf_op jit(solution)/shard_map/ffn_pair/pallas_call | solution.py:445
  618.0 7.7 home_blocks.2
  632.0 17.5 %ffn_grad.9 = f32[736,1024]{1,0:T(8,128)} custom-call(bf16[5888,1024]{1,0:T(8,128)(2,1)} %pick_rows.7.c_ref, f32[1472,1792]{1,0:T(8,128)} %get-tuple-element.177.a_ref, f32[1472,1792]{1,0:T(8,128)} %get-tuple-element.178.b_ref, bf16[1792,1024]{1,0:T(8,128)(2,1)} %collective-permute-done.2.w2.refs_0_, ...), custom_call_target="tpu_custom_call" | custom-call | flops 8103395328 | bytes 26836992 | tf_op jit(solution)/shard_map/ffn_grad/pallas_call | solution.py:352
  651.5 29.6 %fusion.57 = f32[1024,1792]{1,0:T(8,128)} fusion(bf16[5888,1024]{1,0:T(8,128)(2,1)} %pick_rows.6.x_ref, bf16[5888,1792]{1,0:T(8,128)(2,1)} %get-tuple-element.175), kind=kOutput, calls=%fused_computation.133 | convolution fusion | flops 21609054208 | bytes 40501248 | tf_op jit(solution)/shard_map/dot_general | solution.py:31
  694.6 23.5 %collective-permute-done.6.refs_1_ = f32[736,1024]{1,0:T(8,128)S(1)} collective-permute-done((f32[736,1024]{1,0:T(8,128)}, f32[736,1024]{1,0:T(8,128)S(1)}, u32[]{:S(2)}, u32[]{:S(2)}) %collective-permute-start.6) | collective-permute-done | bytes 3014688 | tf_op jit(solution)/shard_map/ppermute | solution.py:542
  718.2 7.0 home_blocks.3
  731.5 29.1 %fusion.58 = f32[1792,1024]{1,0:T(8,128)S(1)} fusion(bf16[5888,1792]{1,0:T(8,128)(2,1)} %get-tuple-element.184, bf16[5888,1024]{1,0:T(8,128)(2,1)} %pick_rows.7.c_ref), kind=kOutput, calls=%fused_computation.134 | convolution fusion | flops 21609054208 | bytes 40501248 | tf_op jit(solution)/shard_map/dot_general | solution.py:31
  770.4 6.5 all-to-all-done.1
  (160 shorter events, 79.6 us)
Async XLA Ops:
  7.2 414.0 %all-gather.5.cloned.1.call-start = ((), (), s32[]{:S(2)}) async-start(), calls=%async_computation.6 | async-start | bytes 37748736 | tf_op jit(solution)/shard_map/all_gather | solution.py:551
  161.5 130.6 %collective-permute-start = (bf16[1024,1792]{1,0:T(8,128)(2,1)}, bf16[1024,1792]{1,0:T(8,128)(2,1)}, u32[]{:S(2)}, u32[]{:S(2)}) collective-permute-start(bf16[1024,1792]{1,0:T(8,128)(2,1)} %bitcast.133), channel_id=1, source_target_pairs={{0,8},{1,25},{2,10},{3,27},{4,12},{5,29},{6,14},{7,31},{8,0},{9,17... | collective-permute-start | bytes 11010056 | tf_op jit(solution)/shard_map/ppermute | solution.py:542
  163.1 159.0 %collective-permute-start.1 = (bf16[1024,1792]{1,0:T(8,128)(2,1)}, bf16[1024,1792]{1,0:T(8,128)(2,1)}, u32[]{:S(2)}, u32[]{:S(2)}) collective-permute-start(bf16[1024,1792]{1,0:T(8,128)(2,1)} %bitcast.139), channel_id=1, source_target_pairs={{0,8},{1,25},{2,10},{3,27},{4,12},{5,29},{6,14},{7,31},{8,0},{9,17... | collective-permute-start | bytes 11010056 | tf_op jit(solution)/shard_map/ppermute | solution.py:542
  163.6 237.3 %collective-permute-start.2 = (bf16[1792,1024]{1,0:T(8,128)(2,1)}, bf16[1792,1024]{1,0:T(8,128)(2,1)}, u32[]{:S(2)}, u32[]{:S(2)}) collective-permute-start(bf16[1792,1024]{1,0:T(8,128)(2,1)} %bitcast.145), channel_id=1, source_target_pairs={{0,8},{1,25},{2,10},{3,27},{4,12},{5,29},{6,14},{7,31},{8,0},{9,17... | collective-permute-start | bytes 11010056 | tf_op jit(solution)/shard_map/ppermute | solution.py:542
  213.6 48.1 %copy-start.19 = (f32[1,16384]{1,0:T(1,128)}, f32[1,16384]{1,0:T(1,128)S(1)}, u32[]{:S(2)}) copy-start(f32[1,16384]{1,0:T(1,128)S(1)} %or_select_fusion) | copy-start | bytes 196612
  213.6 39.7 %copy-start.34 = (s32[4,8]{0,1:T(8,128)S(1)}, s32[4,8]{0,1:T(8,128)}, u32[]{:S(2)}) copy-start(s32[4,8]{0,1:T(8,128)} %get-tuple-element.217) | copy-start | bytes 388
  213.6 43.2 %copy-start.27 = (s32[512,2]{0,1:T(2,128)S(1)}, s32[512,2]{0,1:T(2,128)}, u32[]{:S(2)}) copy-start(s32[512,2]{0,1:T(2,128)} %param.13) | copy-start | bytes 12292
  213.6 45.7 %copy-start.36 = (f32[8]{0:T(128)S(1)}, f32[8]{0:T(128)}, u32[]{:S(2)}) copy-start(f32[8]{0:T(128)} %get-tuple-element.205) | copy-start | bytes 100
  256.1 36.0 %copy-start.17 = (f32[32,512]{1,0:T(8,128)}, f32[32,512]{1,0:T(8,128)S(1)}, u32[]{:S(2)}) copy-start(f32[32,512]{1,0:T(8,128)S(1)} %get-tuple-element.202) | copy-start | bytes 196612
  256.9 35.2 %copy-start.28 = (s32[512,1]{0,1:T(1,128)}, s32[512,1]{0,1:T(1,128)S(1)}, u32[]{:S(2)}) copy-start(s32[512,1]{0,1:T(1,128)S(1)} %get-tuple-element.228) | copy-start | bytes 6148
  256.9 35.2 %copy-start.30 = (s32[512,1]{0,1:T(1,128)}, s32[512,1]{0,1:T(1,128)S(1)}, u32[]{:S(2)}) copy-start(s32[512,1]{0,1:T(1,128)S(1)} %get-tuple-element.229) | copy-start | bytes 6148
  409.0 209.0 %collective-permute-start.3 = (f32[736,1024]{1,0:T(8,128)}, f32[736,1024]{1,0:T(8,128)}, u32[]{:S(2)}, u32[]{:S(2)}) collective-permute-start(f32[736,1024]{1,0:T(8,128)} %ffn_down.2), channel_id=1, source_target_pairs={{0,24},{1,9},{2,26},{3,11},{4,28},{5,13},{6,30},{7,15},{8,16},{9,1... | collective-permute-start | bytes 9043976 | tf_op jit(solution)/shard_map/ppermute | solution.py:542
  419.1 198.9 %collective-permute-start.4 = (f32[736,1024]{1,0:T(8,128)}, f32[736,1024]{1,0:T(8,128)}, u32[]{:S(2)}, u32[]{:S(2)}) collective-permute-start(f32[736,1024]{1,0:T(8,128)} %ffn_down.3), channel_id=1, source_target_pairs={{0,24},{1,9},{2,26},{3,11},{4,28},{5,13},{6,30},{7,15},{8,16},{9,1... | collective-permute-start | bytes 9043976 | tf_op jit(solution)/shard_map/ppermute | solution.py:542
  485.6 209.0 %collective-permute-start.5 = (f32[736,1024]{1,0:T(8,128)}, f32[736,1024]{1,0:T(8,128)}, u32[]{:S(2)}, u32[]{:S(2)}) collective-permute-start(f32[736,1024]{1,0:T(8,128)} %ffn_grad.8), channel_id=1, source_target_pairs={{0,24},{1,9},{2,26},{3,11},{4,28},{5,13},{6,30},{7,15},{8,16},{9,1... | collective-permute-start | bytes 9043976 | tf_op jit(solution)/shard_map/ppermute | solution.py:542
  574.2 41.5 %copy-start.18 = (f32[32,512]{1,0:T(8,128)S(1)}, f32[32,512]{1,0:T(8,128)}, u32[]{:S(2)}) copy-start(f32[32,512]{1,0:T(8,128)} %copy-done.17) | copy-start | bytes 196612
  574.2 41.5 %copy-start.20 = (f32[1,16384]{1,0:T(1,128)S(1)}, f32[1,16384]{1,0:T(1,128)}, u32[]{:S(2)}) copy-start(f32[1,16384]{1,0:T(1,128)} %copy-done.19) | copy-start | bytes 196612
  574.2 41.5 %copy-start.25 = (s32[32,512]{1,0:T(8,128)S(1)}, s32[32,512]{1,0:T(8,128)}, u32[]{:S(2)}) copy-start(s32[32,512]{1,0:T(8,128)} %get-tuple-element.233) | copy-start | bytes 196612
  574.2 41.5 %copy-start.33 = (s32[8,4,1]{0,1,2:T(4,128)S(1)}, s32[8,4,1]{0,1,2:T(4,128)}, u32[]{:S(2)}) copy-start(s32[8,4,1]{0,1,2:T(4,128)} %copy-done.32) | copy-start | bytes 388
  627.4 53.6 %all-to-all-start = ((bf16[8,224,1024]{2,1,0:T(8,128)(2,1)}), bf16[8,224,1024]{2,1,0:T(8,128)(2,1)}, u32[]{:S(2)}, u32[]{:S(2)}) async-start(bf16[8,224,1024]{2,1,0:T(8,128)(2,1)} %copy-done.1), calls=%async_computation.2 | async-start | bytes 7340032 | tf_op jit(solution)/shard_map/all_to_all | solution.py:630
  632.0 136.5 %all-gather.7.cloned.1.call-start = ((), (), s32[]{:S(2)}) async-start(), calls=%async_computation.7 | async-start | bytes 1081344 | tf_op jit(solution)/shard_map/all_gather | solution.py:666
  649.5 68.7 %collective-permute-start.6 = (f32[736,1024]{1,0:T(8,128)}, f32[736,1024]{1,0:T(8,128)S(1)}, u32[]{:S(2)}, u32[]{:S(2)}) collective-permute-start(f32[736,1024]{1,0:T(8,128)} %ffn_grad.9), channel_id=1, source_target_pairs={{0,24},{1,9},{2,26},{3,11},{4,28},{5,13},{6,30},{7,15},{8,16},{9,1... | collective-permute-start | bytes 9043976 | tf_op jit(solution)/shard_map/ppermute | solution.py:542
  651.5 29.6 %copy-start.38 = (s32[512,1]{0,1:T(1,128)S(1)}, s32[512,1]{0,1:T(1,128)}, u32[]{:S(2)}) copy-start(s32[512,1]{0,1:T(1,128)} %get-tuple-element.227) | copy-start | bytes 6148
  727.0 49.9 %all-to-all-start.1 = ((bf16[8,224,1024]{2,1,0:T(8,128)(2,1)}), bf16[8,224,1024]{2,1,0:T(8,128)(2,1)}, u32[]{:S(2)}, u32[]{:S(2)}) async-start(bf16[8,224,1024]{2,1,0:T(8,128)(2,1)} %copy-done), calls=%async_computation.3 | async-start | bytes 7340032 | tf_op jit(solution)/shard_map/all_to_all | solution.py:630
  731.5 29.1 %copy-start.8 = (bf16[1280,1024]{1,0:T(8,128)(2,1)S(1)}, bf16[1280,1024]{1,0:T(8,128)(2,1)}, u32[]{:S(2)}) copy-start(bf16[1280,1024]{1,0:T(8,128)(2,1)} %get-tuple-element.260) | copy-start | bytes 7864324
  (25 other events, 211.7 us)
Sparse Core Ops, SparseCore 0:
  161.6 160.6 all-gather.4
  694.7 55.0 all-gather.6

commit v3 on v2

v3 whole, which is shorter than its diff:
```python
import functools
import jax
import jax.numpy as jnp
from jax import lax
from jax.experimental import pallas as pl
from jax.experimental.pallas import tpu as pltpu
from jax.sharding import PartitionSpec as P


AUX_COEF = 0.01
OUT_SCALE = 2.0
ALL_AXES = ("ep", "etp")
BF16 = jnp.bfloat16
F32 = jnp.float32
MIB = 1 << 20
FF_STEP = 256

NEXT_PAIRS = (1, 0, 3, 2)
ENDS_PAIRS = (3, 2, 1, 0)


def mm(lhs, rhs):
    return jnp.dot(lhs, rhs, preferred_element_type=F32)


def mm_nt(lhs, rhs, precision=None):
    return lax.dot_general(lhs, rhs, (((1,), (1,)), ((), ())), precision=precision, preferred_element_type=F32)


def mm_tn(lhs, rhs, precision=None):
    return lax.dot_general(lhs, rhs, (((0,), (0,)), ((), ())), precision=precision, preferred_element_type=F32)


def params(vmem_mib):
    return pltpu.CompilerParams(dimension_semantics=("arbitrary",), vmem_limit_bytes=vmem_mib * MIB)


def cost(flops, bytes_accessed, transcendentals=0):
    return pl.CostEstimate(flops=flops, bytes_accessed=bytes_accessed, transcendentals=transcendentals)


def rows_at(rows, width, start=0):
    return pl.BlockSpec((rows, width), lambda i: (i + start, 0))


def by_columns(width, step):
    def at(i, carry):
        step(pl.ds(pl.multiple_of(i * FF_STEP, FF_STEP), FF_STEP))
        return carry

    lax.fori_loop(0, width // FF_STEP, at, 0, unroll=True)


def flip_col(col, bit):
    return col + bit * (1 - 2 * ((col // bit) % 2))


def one_hot(hit):
    return hit.astype(F32).astype(BF16)


def spread_kernel(n_etp, h_ref, dy_ref, h_all, dy_col, h_recv, dy_recv, z_send, x_send, y_send, c_send, own_sem):
    t = lax.axis_index("etp")
    o = lax.axis_index("ep")
    col_c, col_x, col_y = [flip_col(o, bit) for bit in (1, 2, 4)]
    col_d = flip_col(col_x, 4)
    order = [t, flip_col(t, 1), flip_col(t, 2), n_etp - 1 - t]
    has_left, has_right = t > 0, t < n_etp - 1

    barrier = pltpu.get_barrier_semaphore()
    for col in (col_c, col_x, col_y):
        pl.semaphore_signal(barrier, device_id={"ep": col}, device_id_type=pl.DeviceIdType.MESH)

    @pl.when(has_left)
    def _():
        pl.semaphore_signal(barrier, device_id={"etp": t - 1}, device_id_type=pl.DeviceIdType.MESH)

    @pl.when(has_right)
    def _():
        pl.semaphore_signal(barrier, device_id={"etp": t + 1}, device_id_type=pl.DeviceIdType.MESH)

    pl.semaphore_wait(barrier, 3 + (t + n_etp - 1) // n_etp + (2 * n_etp - 2 - t) // n_etp)

    keep = [pltpu.make_async_copy(h_ref, h_all.at[o * n_etp + t], own_sem.at[0]), pltpu.make_async_copy(dy_ref, dy_col.at[t], own_sem.at[1])]
    for copy in keep:
        copy.start()

    def h_copy(col, s, send_sem, to):
        slot = col * n_etp + s
        return pltpu.make_async_remote_copy(src_ref=h_all.at[slot], dst_ref=h_all.at[slot], send_sem=send_sem, recv_sem=h_recv.at[slot], device_id=to, device_id_type=pl.DeviceIdType.MESH)

    def own_copy(send_sem, to):
        slot = o * n_etp + t
        return pltpu.make_async_remote_copy(src_ref=h_ref, dst_ref=h_all.at[slot], send_sem=send_sem, recv_sem=h_recv.at[slot], device_id=to, device_id_type=pl.DeviceIdType.MESH)

    def dy_copy(s, send_sem, to, own=False):
        return pltpu.make_async_remote_copy(src_ref=dy_ref if own else dy_col.at[s], dst_ref=dy_col.at[s], send_sem=send_sem, recv_sem=dy_recv.at[s], device_id=to, device_id_type=pl.DeviceIdType.MESH)

    def h_arrived(col, s):
        h_copy(col, s, own_sem.at[0], {"ep": col_c}).wait_recv()

    def dy_arrived(s):
        dy_copy(s, own_sem.at[0], {"ep": col_c}).wait_recv()

    right, left = {"etp": t + 1}, {"etp": t - 1}
    to_x, to_y, to_c = {"ep": col_x}, {"ep": col_y}, {"ep": col_c}

    def z_copy(k, data, go):
        s, to, sem = (t - k, right, z_send.at[data, 0, k]) if go == 0 else (t + k, left, z_send.at[data, 1, k])
        if data == 0:
            return own_copy(sem, to) if k == 0 else h_copy(o, s, sem, to)
        return dy_copy(s, sem, to, own=k == 0)

    def z_goes(k, go):
        return has_right & (t >= k) if go == 0 else has_left & (t <= n_etp - 1 - k)

    def z_send_step(k, data):
        for go in (0, 1):
            pl.when(z_goes(k, go))(lambda: z_copy(k, data, go).start())

    def z_arrive(k, data):
        arrived = (lambda s: h_arrived(o, s)) if data == 0 else dy_arrived
        pl.when(t >= k)(lambda: arrived(t - k))
        pl.when(t <= n_etp - 1 - k)(lambda: arrived(t + k))

    def a_step(k):
        s = order[k]
        for sem, to in ((x_send.at[k], to_x), (y_send.at[k], to_y), (c_send.at[0, k], to_c)):
            (own_copy(sem, to) if k == 0 else h_copy(o, s, sem, to)).start()

    def b_step(k):
        s = order[k]
        h_arrived(col_x, s)
        if k % 2 == 0:
            h_copy(col_x, s, y_send.at[4 + k // 2], to_y).start()
        h_copy(col_x, s, c_send.at[1, k], to_c).start()
        h_arrived(col_y, s)
        if k % 2 == 1:
            h_copy(col_y, s, x_send.at[4 + k // 2], to_x).start()
        h_copy(col_y, s, c_send.at[2, k], to_c).start()

    def c_step(k):
        s = order[k]
        h_arrived(col_d, s)
        h_copy(col_d, s, c_send.at[3, k], to_c).start()

    steps = {
        "s": functools.partial(z_send_step, data=0),
        "S": functools.partial(z_send_step, data=1),
        "r": functools.partial(z_arrive, data=0),
        "R": functools.partial(z_arrive, data=1),
        "a": a_step,
        "b": b_step,
        "c": c_step,
    }
    plan = "s0a0r1s1a1b0r2s2S0a2b1r3a3c0b2c1R1S1b3R2S2c2c3R3"
    for kind, k in zip(plan[::2], plan[1::2]):
        steps[kind](int(k))

    for k in range(n_etp):
        for col in (col_x, col_y, col_d):
            h_arrived(flip_col(col, 1), order[k])
        h_arrived(col_c, order[k])
    for copy in keep:
        copy.wait()
    for k in range(n_etp - 1):
        for data in (0, 1):
            for go in (0, 1):
                pl.when(z_goes(k, go))(lambda: z_copy(k, data, go).wait_send())
    for i in range(6):
        h_copy(o, t, x_send.at[i], to_x).wait_send()
        h_copy(o, t, y_send.at[i], to_y).wait_send()
    for j in range(4):
        for k in range(n_etp):
            h_copy(o, t, c_send.at[j, k], to_c).wait_send()


def spread_all(h, dy, n_etp, n_ep):
    hbm = pl.BlockSpec(memory_space=pl.ANY)
    vmem = pl.BlockSpec(memory_space=pltpu.VMEM)
    dma = pltpu.SemaphoreType.DMA
    return pl.pallas_call(
        functools.partial(spread_kernel, n_etp),
        in_specs=[vmem, vmem],
        out_specs=[hbm, hbm],
        out_shape=[jax.ShapeDtypeStruct((n_ep * n_etp, *h.shape), h.dtype), jax.ShapeDtypeStruct((n_etp, *dy.shape), dy.dtype)],
        scratch_shapes=[dma((n_ep * n_etp,)), dma((n_etp,)), dma((2, 2, n_etp - 1)), dma((6,)), dma((6,)), dma((4, n_etp)), dma((2,))],
        compiler_params=pltpu.CompilerParams(collective_id=0, has_side_effects=True, vmem_limit_bytes=16 * MIB),
        cost_estimate=cost(10**11, 2 * n_ep * n_etp * h.size),
        name="spread_all",
    )(h, dy)


def pick_kernel(n_arrays, scaled, win, planes_ref, cols_ref, base_ref, *refs):
    sources, (pos_ref, *gate_ref, out_ref, acc_ref) = refs[:n_arrays], refs[n_arrays:]
    grp = pl.program_id(0)
    acc_ref[...] = jnp.zeros_like(acc_ref)
    for i in range(pos_ref.shape[0]):
        col = cols_ref[i]
        base = pl.multiple_of(base_ref[grp, col], 8)
        pos_row = pos_ref[col, 0]
        want = base + lax.broadcasted_iota(jnp.int32, (win, pos_row.shape[1]), 0)
        hit = want == pos_row
        block = sources[i][0] if n_arrays > 1 else sources[0][i, 0]
        part = mm(one_hot(hit), block)
        if scaled:
            part = part * jnp.sum(jnp.where(hit, gate_ref[0][col, 0], 0.0), axis=1, keepdims=True)
        acc_ref[pl.ds(base, win), :] += part
    out_ref[...] = acc_ref[: out_ref.shape[0], :].astype(out_ref.dtype)


def pick_rows(sources, cols, pos, gates, planes, base, n_rows, win, n_src, n_etp):
    blk_rows = pos.shape[-1]
    d_model = sources[0].shape[-1]
    n_grp = planes.shape[0]
    plane_map = lambda g, planes, cols, base: (0, planes[g], 0, 0)
    table_spec = pl.BlockSpec((n_src, 1, 1, blk_rows), plane_map)
    if len(sources) == 1:
        sources = [sources[0].reshape(n_src, n_etp, *sources[0].shape[1:])]
        source_spec = pl.BlockSpec((n_src, 1, blk_rows, d_model), plane_map)
    else:
        source_spec = pl.BlockSpec((1, blk_rows, d_model), lambda g, planes, cols, base: (planes[g], 0, 0))
    tables = [table.reshape(n_src, n_etp, 1, blk_rows) for table in (pos, gates) if table is not None]
    work = n_grp * n_src * blk_rows * d_model
    return pl.pallas_call(
        functools.partial(pick_kernel, len(sources), gates is not None, win),
        grid_spec=pltpu.PrefetchScalarGridSpec(
            num_scalar_prefetch=3,
            grid=(n_grp,),
            in_specs=[source_spec] * len(sources) + [table_spec] * len(tables),
            out_specs=pl.BlockSpec((n_rows, d_model), lambda g, planes, cols, base: (g, 0)),
            scratch_shapes=[pltpu.VMEM((n_rows + win, d_model), F32)],
        ),
        out_shape=jax.ShapeDtypeStruct((n_grp * n_rows, d_model), BF16),
        compiler_params=params(58),
        cost_estimate=cost(2 * win * work, 4 * work),
        name="pick_rows",
    )(planes, cols, base, *sources, *tables)


def whole(array):
    return pl.BlockSpec(array.shape, lambda i: (0, 0), pipeline_mode=pl.Buffered(1))


def sum_into(out_ref, base_ref, product):
    def step(cols):
        part = product(cols)
        out_ref[:, cols] = part if base_ref is None else base_ref[:, cols] + part

    by_columns(out_ref.shape[1], step)


def act_kernel(with_y, n_alias, x_ref, *refs):
    (w1, w3, *w2), refs = refs[: 2 + with_y], refs[2 + with_y + n_alias :]
    a_ref, b_ref, u_ref = refs[:3]

    def step(cols):
        act_a = mm(x_ref[...], w1[:, cols])
        act_b = mm(x_ref[...], w3[:, cols])
        a_ref[:, cols] = act_a
        b_ref[:, cols] = act_b
        u_ref[:, cols] = (act_a * jax.nn.sigmoid(act_a) * act_b).astype(BF16)

    by_columns(w1.shape[1], step)
    if with_y:
        sum_into(refs[3], None, lambda cols: mm(u_ref[...], w2[0][:, cols]))


def ffn_act(x, weights, tile, first, n_tiles, kept, total):
    d_model, d_ff = weights[0].shape
    with_y = len(weights) == 3
    rows = n_tiles * tile
    out_specs = [rows_at(tile, d_ff, first)] * 3
    out_shape = [jax.ShapeDtypeStruct((total, d_ff), dtype) for dtype in (F32, F32, BF16)]
    if with_y:
        out_specs.append(rows_at(tile, d_model))
        out_shape.append(jax.ShapeDtypeStruct((rows, d_model), F32))
    n_in = 1 + len(weights)
    return pl.pallas_call(
        functools.partial(act_kernel, with_y, len(kept)),
        grid=(n_tiles,),
        in_specs=[rows_at(tile, d_model, first)] + [whole(w) for w in weights] + [pl.BlockSpec(memory_space=pl.ANY)] * len(kept),
        out_specs=out_specs,
        out_shape=out_shape,
        input_output_aliases={n_in + i: i for i in range(len(kept))},
        compiler_params=params(60),
        cost_estimate=cost(2 * len(weights) * rows * d_model * d_ff, 6 * d_model * d_ff + 10 * rows * d_ff, rows * d_ff),
        name="ffn_act",
    )(x, *weights, *kept)


def down_kernel(u_ref, w2, y_in, y_ref):
    sum_into(y_ref, y_in, lambda cols: mm(u_ref[...], w2[:, cols]))


def ffn_down(u, w2, y_in, tile, first, n_tiles):
    d_ff, d_model = w2.shape
    rows = n_tiles * tile
    return pl.pallas_call(
        down_kernel,
        grid=(n_tiles,),
        in_specs=[rows_at(tile, d_ff, first), whole(w2), rows_at(tile, d_model, first)],
        out_specs=rows_at(tile, d_model),
        out_shape=jax.ShapeDtypeStruct((rows, d_model), F32),
        compiler_params=params(48),
        cost_estimate=cost(2 * rows * d_model * d_ff, 2 * d_model * d_ff + 8 * rows * d_model),
        name="ffn_down",
    )(u, w2, y_in)


def grad_kernel(with_dx, keeps, n_base, n_alias, c_ref, a_ref, b_ref, *refs):
    n_w = 3 if with_dx else 1
    (w2, *w13), base, refs = refs[:n_w], refs[n_w : n_w + n_base], list(refs[n_w + n_base + n_alias :])
    dx_ref = refs.pop(2 if keeps else 0) if with_dx else None
    da_ref, db_ref = refs

    def step(cols):
        d_inner = mm_nt(c_ref[...], w2[cols, :])
        act_a = a_ref[:, cols]
        sig_a = jax.nn.sigmoid(act_a)
        da_ref[:, cols] = (d_inner * b_ref[:, cols] * sig_a * (1.0 + act_a * (1.0 - sig_a))).astype(BF16)
        db_ref[:, cols] = (d_inner * (act_a * sig_a)).astype(BF16)

    by_columns(w2.shape[0], step)
    if with_dx:
        w1, w3 = w13
        sum_into(dx_ref, base[0] if base else None, lambda cols: mm_nt(da_ref[...], w1[cols, :]) + mm_nt(db_ref[...], w3[cols, :]))


def ffn_grad(c, act_a, act_b, weights, tile, first, first_act, n_tiles, kept, total=0, base=()):
    w2, *w13 = weights
    d_ff, d_model = w2.shape
    with_dx = bool(w13)
    rows = n_tiles * tile
    at = functools.partial(rows_at, tile)
    out_specs = [at(d_ff, first)] * 2 if total else []
    out_shape = [jax.ShapeDtypeStruct((total, d_ff), BF16)] * 2 if total else []
    if with_dx:
        out_specs.append(at(d_model))
        out_shape.append(jax.ShapeDtypeStruct((rows, d_model), F32))
    n_in = 3 + len(weights) + len(base)
    return pl.pallas_call(
        functools.partial(grad_kernel, with_dx, bool(total), len(base), len(kept)),
        grid=(n_tiles,),
        in_specs=[at(d_model, first), at(d_ff, first_act), at(d_ff, first_act)] + [whole(w) for w in weights] + [at(d_model, first)] * len(base) + [pl.BlockSpec(memory_space=pl.ANY)] * len(kept),
        out_specs=out_specs,
        out_shape=out_shape,
        scratch_shapes=[] if total else [pltpu.VMEM((tile, d_ff), BF16)] * 2,
        input_output_aliases={n_in + i: i for i in range(len(kept))},
        compiler_params=params(62),
        cost_estimate=cost(2 * len(weights) * rows * d_model * d_ff, 6 * d_model * d_ff + 12 * rows * d_ff, rows * d_ff),
        name="ffn_grad",
    )(c, act_a, act_b, *weights, *base, *kept)


def pair_kernel(x_ref, c_ref, y_in, dx_in, w1, w3, w2, y_ref, dx_ref, u_ref, da_ref, db_ref):
    def step(cols):
        act_a = mm(x_ref[...], w1[:, cols])
        act_b = mm(x_ref[...], w3[:, cols])
        d_inner = mm_nt(c_ref[...], w2[cols, :])
        sig_a = jax.nn.sigmoid(act_a)
        silu_a = act_a * sig_a
        u_ref[:, cols] = (silu_a * act_b).astype(BF16)
        da_ref[:, cols] = (d_inner * act_b * sig_a * (1.0 + act_a * (1.0 - sig_a))).astype(BF16)
        db_ref[:, cols] = (d_inner * silu_a).astype(BF16)

    by_columns(w1.shape[1], step)
    sum_into(y_ref, y_in, lambda cols: mm(u_ref[...], w2[:, cols]))
    sum_into(dx_ref, dx_in, lambda cols: mm_nt(da_ref[...], w1[cols, :]) + mm_nt(db_ref[...], w3[cols, :]))


def ffn_pair(x, c, y_in, dx_in, weights, tile, first, n_tiles, first_dx):
    d_model, d_ff = weights[0].shape
    rows = n_tiles * tile
    at = functools.partial(rows_at, tile, d_model)
    return pl.pallas_call(
        pair_kernel,
        grid=(n_tiles,),
        in_specs=[at(first), at(first), at(first), at(first_dx)] + [whole(w) for w in weights],
        out_specs=[at()] * 2,
        out_shape=[jax.ShapeDtypeStruct((rows, d_model), F32)] * 2,
        scratch_shapes=[pltpu.VMEM((tile, d_ff), BF16)] * 3,
        compiler_params=params(60),
        cost_estimate=cost(12 * rows * d_model * d_ff, 6 * d_model * d_ff + 20 * rows * d_model, rows * d_ff),
        name="ffn_pair",
    )(x, c, y_in, dx_in, *weights)


def unset(*shapes):
    return pl.pallas_call(
        lambda *refs: None,
        out_specs=[pl.BlockSpec(memory_space=pl.ANY)] * len(shapes),
        out_shape=[jax.ShapeDtypeStruct(shape, BF16) for shape in shapes],
        name="unset",
    )()


def home_kernel(win, n_far, start_ref, near_ref, *refs):
    fars, (more_ref, out_ref, sum_ref) = refs[:n_far], refs[n_far:]
    row = 0
    for far in fars:
        rows = far.shape[0]
        sum_ref[row : row + rows, :] = (near_ref[row : row + rows, :] + far[...]).astype(BF16).astype(F32)
        row += rows
    sum_ref[row : row + more_ref.shape[0], :] = more_ref[...].astype(F32)
    row += more_ref.shape[0]
    sum_ref[row:, :] = jnp.zeros((sum_ref.shape[0] - row, sum_ref.shape[1]), F32)
    out_rows = out_ref.shape[1]
    to = lax.broadcasted_iota(jnp.int32, (out_rows, win), 0)
    frm = lax.broadcasted_iota(jnp.int32, (out_rows, win), 1)

    def block(o, _):
        start = start_ref[o]
        base = pl.multiple_of(start // 8 * 8, 8)
        rows = sum_ref[pl.ds(base, win), :].astype(BF16)
        move = one_hot(frm == to + (start - base))
        out_ref[o] = mm(move, rows).astype(BF16)
        return 0

    lax.fori_loop(0, out_ref.shape[0], block, 0)


def home_blocks(starts, near, fars, more, out_rows):
    n_out = starts.shape[0]
    d_model = near.shape[1]
    win = out_rows + 8
    vmem = pl.BlockSpec(memory_space=pltpu.VMEM)
    return pl.pallas_call(
        functools.partial(home_kernel, win, len(fars)),
        in_specs=[pl.BlockSpec(memory_space=pltpu.SMEM)] + [vmem] * (2 + len(fars)),
        out_specs=vmem,
        out_shape=jax.ShapeDtypeStruct((n_out, out_rows, d_model), BF16),
        scratch_shapes=[pltpu.VMEM((near.shape[0] + more.shape[0] + win, d_model), F32)],
        compiler_params=pltpu.CompilerParams(vmem_limit_bytes=40 * MIB),
        cost_estimate=cost(2 * n_out * out_rows * win * d_model, 12 * near.size),
        name="home_blocks",
    )(starts, near, *fars, more)


def return_kernel(n_etp, start_ref, first_ref, near_ref, far_ref, more_ref, part_ref, slot_ref, rest_ref, out_ref, total_ref, sum_ref, send_ref, back_ref, z_part, col_part, col_sum, send_sem, back_sem, z_sem, col_sem):
    t = lax.axis_index("etp")
    o = lax.axis_index("ep")
    n_ep = send_ref.shape[0]

    def col_at(i):
        col = o
        for bit in (1, 2, 4):
            if i & bit:
                col = flip_col(col, bit)
        return col

    barrier = pltpu.get_barrier_semaphore()
    planes = [(t + k) % n_etp for k in range(1, n_etp)]
    for i in range(1, n_ep):
        pl.semaphore_signal(barrier, device_id={"ep": col_at(i)}, device_id_type=pl.DeviceIdType.MESH)
    for plane in planes:
        pl.semaphore_signal(barrier, device_id={"etp": plane}, device_id_type=pl.DeviceIdType.MESH)
    pl.semaphore_wait(barrier, n_ep - 1 + n_etp - 1)

    def to(src, dst, sem, got, peer):
        return pltpu.make_async_remote_copy(src_ref=src, dst_ref=dst, send_sem=sem, recv_sem=got, device_id=peer, device_id_type=pl.DeviceIdType.MESH)

    z_copies = [to(part_ref, z_part.at[t], z_sem.at[0, k], z_sem.at[1, t], {"etp": plane}) for k, plane in enumerate(planes)]
    for copy in z_copies:
        copy.start()

    rows = first_ref.shape[0]
    sum_ref[:rows, :] = first_ref[...]
    end = rows + far_ref.shape[0]
    sum_ref[rows:end, :] = (near_ref[...] + far_ref[...]).astype(BF16)
    sum_ref[end:, :] = more_ref[...]

    blk_rows = send_ref.shape[1]
    put = lax.broadcasted_iota(jnp.int32, (blk_rows, sum_ref.shape[0]), 0)
    frm = lax.broadcasted_iota(jnp.int32, (blk_rows, sum_ref.shape[0]), 1)
    order = [6, 7, 2, 4, 3, 5, 1, 0]
    copies = {i: to(send_ref.at[i], back_ref.at[o], send_sem.at[i], back_sem.at[o], {"ep": col_at(i)}) for i in order if i}
    for k, i in enumerate(order):
        move = one_hot(frm == put + start_ref[col_at(i)])
        block = mm(move, sum_ref[...]).astype(BF16)
        if i:
            send_ref[i] = block
        else:
            back_ref[o] = block
        if k:
            copies[order[k - 1]].start()

    z_part[t] = part_ref[...]
    for plane in planes:
        to(part_ref, z_part.at[plane], z_sem.at[0, 0], z_sem.at[1, plane], {"etp": plane}).wait_recv()
    total = z_part[0]
    for k in range(1, n_etp):
        total += z_part[k]
    col_sum[...] = total

    cols = lax.broadcasted_iota(jnp.int32, (slot_ref.shape[0], blk_rows), 1)
    acc = rest_ref[...]
    col_copies = {i: to(col_sum, col_part.at[o], col_sem.at[0, i], col_sem.at[1, o], {"ep": col_at(i)}) for i in range(1, n_ep)}
    for k, i in enumerate((0, 1, 2, 4, 3, 5, 6, 7)):
        col = col_at(i)
        if i:
            to(send_ref.at[i], back_ref.at[col], send_sem.at[i], back_sem.at[col], {"ep": col}).wait_recv()
        local = cols + col * blk_rows
        hit = (slot_ref[:, 0:1] == local) | (slot_ref[:, 1:2] == local)
        acc += mm(one_hot(hit), back_ref[col])
        if k == 1:
            for copy in col_copies.values():
                copy.start()
    out_ref[...] = acc.astype(out_ref.dtype)

    col_part[o] = col_sum[...]
    for i in range(1, n_ep):
        col = col_at(i)
        to(col_sum, col_part.at[col], col_sem.at[0, i], col_sem.at[1, col], {"ep": col}).wait_recv()
    total = col_part[0]
    for k in range(1, n_ep):
        total += col_part[k]
    total_ref[...] = total
    for copy in [*z_copies, *copies.values(), *col_copies.values()]:
        copy.wait_send()


def return_rows(starts, first, near, far, more, part, slots, rest, n_etp, n_ep, blk_rows):
    d_model = near.shape[1]
    half = far.shape[0]
    dma = pltpu.SemaphoreType.DMA
    vmem = lambda array: rows_at(*array.shape)
    blocks = pltpu.VMEM((n_ep, blk_rows, d_model), BF16)
    return pl.pallas_call(
        functools.partial(return_kernel, n_etp),
        grid=(1,),
        in_specs=[pl.BlockSpec(memory_space=pltpu.SMEM), vmem(first), rows_at(half, d_model, 1), vmem(far), vmem(more), vmem(part), vmem(slots), vmem(rest)],
        out_specs=[vmem(rest), vmem(part)],
        out_shape=[jax.ShapeDtypeStruct(rest.shape, BF16), jax.ShapeDtypeStruct(part.shape, F32)],
        scratch_shapes=[
            pltpu.VMEM((2 * half + more.shape[0], d_model), BF16),
            blocks,
            blocks,
            pltpu.VMEM((n_etp, *part.shape), F32),
            pltpu.VMEM((n_ep, *part.shape), F32),
            pltpu.VMEM(part.shape, F32),
            dma((n_ep,)),
            dma((n_ep,)),
            dma((2, n_etp)),
            dma((2, n_ep)),
        ],
        compiler_params=pltpu.CompilerParams(collective_id=1, has_side_effects=True, vmem_limit_bytes=56 * MIB),
        cost_estimate=cost(10**10, 12 * near.size),
        name="return_rows",
    )(starts, first, near, far, more, part, slots, rest)


def split3(value):
    high = lax.reduce_precision(value, 8, 7)
    rest = value - high
    mid = lax.reduce_precision(rest, 8, 7)
    return high.astype(BF16), mid.astype(BF16), (rest - mid).astype(BF16)


def solution(mesh):
    ep_size = mesh.shape["ep"]
    etp_size = mesh.shape["etp"]
    n_dev = ep_size * etp_size
    tok_spec = P(ALL_AXES, None)
    gate_spec = P("ep", None, "etp")
    down_spec = P("ep", "etp", None)

    def layer(hidden, w_router, expert_ids, d_out, w_gate, w_up, w_down):
        tok_rows, d_model = hidden.shape
        n_experts = w_router.shape[1]
        n_tokens = tok_rows * n_dev
        capacity = (5 * n_tokens + 2 * n_experts - 1) // (2 * n_experts)
        per_expert = 7 * tok_rows // (2 * n_experts)
        list_max = ep_size * per_expert
        main_rows = 23 * tok_rows // 8
        more_rows = list_max - main_rows
        tile = main_rows // 4
        win = per_expert + 8
        ep_i = lax.axis_index("ep")
        etp_i = lax.axis_index("etp")
        block_idx = ep_i * etp_size + etp_i
        w1, w3, w2 = w_gate[0], w_up[0], w_down[0]

        def swap(array, even, odd):
            pairs = [(t * ep_size + o, (odd if o % 2 else even)[t] * ep_size + o) for t in range(etp_size) for o in range(ep_size)]
            return lax.ppermute(array, ("etp", "ep"), pairs)

        ids_row = expert_ids.T.astype(BF16).reshape(1, 2 * tok_rows)
        ids_row = jnp.concatenate([ids_row, jnp.zeros((7, 2 * tok_rows), BF16)])
        h_all, dy_col = spread_all(jnp.concatenate([hidden, ids_row]), d_out, etp_size, ep_size)
        w1_b, w3_b, w2_b, h_all, dy_b = lax.optimization_barrier((w1, w3, w2, h_all, dy_col))
        w1p = swap(w1_b, NEXT_PAIRS, ENDS_PAIRS)
        w3p = swap(w3_b, NEXT_PAIRS, ENDS_PAIRS)
        w2p = swap(w2_b, NEXT_PAIRS, ENDS_PAIRS)

        def flip(array, bit):
            return lax.ppermute(array, "ep", [(o, o ^ bit) for o in range(ep_size)])

        half_z = etp_size // 2
        dy_c, dy_x, dy_y = [flip(dy_b, bit) for bit in (1, 2, 4)]
        dy_d = flip(dy_y[:half_z], 2), flip(dy_x[half_z:], 4)
        dy_cx, dy_cy = flip(dy_x, 1), flip(dy_y, 1)
        dy_d = jnp.concatenate(dy_d)
        dy_cd = flip(dy_d, 1)
        dy_all = [dy_b, dy_c, dy_x, dy_cx, dy_y, dy_cy, dy_d, dy_cd]
        dy_cols = (ep_i ^ jnp.arange(ep_size)).astype(jnp.int32)
        all_cols = jnp.arange(ep_size, dtype=jnp.int32)

        ids_all = h_all[:, tok_rows, :].astype(jnp.int32).reshape(n_dev, 2, tok_rows)
        id0, id1 = ids_all[:, 0], ids_all[:, 1]
        experts = jnp.arange(n_experts, dtype=jnp.int32)[None, :, None]
        count = jnp.sum(((id0[:, None, :] == experts) | (id1[:, None, :] == experts)).astype(F32), axis=2)
        before = jnp.cumsum(count, axis=0) - count
        kept = jnp.clip(capacity - before, 0, count).astype(jnp.int32)
        kept_lists = kept.reshape(ep_size, etp_size, n_experts)
        list_start = jnp.cumsum(kept_lists, axis=0) - kept_lists
        list_len = jnp.sum(kept_lists, axis=0)
        earlier = (jnp.arange(tok_rows)[:, None] < jnp.arange(tok_rows)[None, :]).astype(BF16)

        my_member = (id0 == ep_i) | (id1 == ep_i)
        my_rank = mm(my_member.astype(BF16), earlier).astype(jnp.int32)
        my_start = lax.dynamic_index_in_dim(list_start, ep_i, 2, keepdims=False)
        my_kept = lax.dynamic_index_in_dim(kept, ep_i, 1, keepdims=True)
        my_pos = jnp.where(my_member & (my_rank < my_kept), my_start.reshape(n_dev, 1) + my_rank, -1)
        odd = ep_i % 2
        far = jnp.where(odd == 1, etp_i ^ 1, etp_size - 1 - etp_i)
        planes = jnp.stack([far, etp_i, far ^ 2, etp_i ^ 2]).astype(jnp.int32)
        my_base = jnp.minimum(my_start, main_rows) // 8 * 8
        pick = functools.partial(pick_rows, win=win, n_src=ep_size, n_etp=etp_size)
        main_pos = jnp.where(my_pos < main_rows, my_pos, -1)
        main_base = my_base.T[planes]
        x_main = pick([h_all], all_cols, main_pos, None, planes, main_base, main_rows)

        route_w = jnp.concatenate(split3(w_router), axis=1)
        logit_parts = lax.dot_general(route_w, h_all, (((0,), (2,)), ((), ())), preferred_element_type=F32)[:, :, :tok_rows].reshape(-1, n_tokens)
        logits = logit_parts[:n_experts] + logit_parts[n_experts : 2 * n_experts] + logit_parts[2 * n_experts :]
        probs_all = jax.nn.softmax(logits, axis=0)
        expert_col = jnp.arange(n_experts, dtype=jnp.int32)[:, None]
        picked_all = jnp.where((id0.reshape(1, -1) == expert_col) | (id1.reshape(1, -1) == expert_col), probs_all, 0.0)
        my_gate = lax.dynamic_index_in_dim(picked_all, ep_i, 0, keepdims=False) / jnp.sum(picked_all, axis=0)
        mean_prob = jnp.sum(probs_all, axis=1) / n_tokens
        my_scale = OUT_SCALE * my_gate.reshape(n_dev, tok_rows)
        c_main = pick(dy_all, dy_cols, main_pos, my_scale, planes, main_base, main_rows)

        n_rows = x_main.shape[0]
        *acts, y_base = ffn_act(x_main, (w1, w3, w2), tile, 0, 8, (), n_rows)
        act_a, act_b, inner = ffn_act(x_main, (w1, w3), tile, 8, 8, acts, n_rows)
        far_a, far_b, far_u = ffn_act(x_main, (w1p, w3p), tile, 0, 4, (), main_rows)
        *grads, dx_base = ffn_grad(c_main, act_a, act_b, (w2, w1, w3), tile, 0, 0, 4, (), n_rows)
        y_far, dx_far = [], []
        for i, n_tiles in enumerate((1, 3)):
            y_part = ffn_down(far_u, w2p, y_base, tile, i, n_tiles)
            y_far.append(swap(y_part, ENDS_PAIRS, NEXT_PAIRS))
        for i in range(2):
            (dx_part,) = ffn_grad(c_main, far_a, far_b, (w2p, w1p, w3p), tile, 2 * i, 2 * i, 2, (), base=(dx_base,))
            dx_far.append(swap(dx_part, ENDS_PAIRS, NEXT_PAIRS))
        *grads, dx_base = ffn_grad(c_main, act_a, act_b, (w2, w1, w3), tile, 4, 4, 4, grads, n_rows)
        y_near, dx_near = ffn_pair(x_main, c_main, y_base, dx_base, (w1p, w3p, w2p), tile, 4, 4, 0)
        d_a, d_b = ffn_grad(c_main, act_a, act_b, (w2,), tile, 8, 8, 8, grads, n_rows)

        def add_planes(parts):
            total = parts[etp_i]
            for k in range(1, etp_size):
                shift = [(t, (t + k) % etp_size) for t in range(etp_size)]
                total += lax.ppermute(parts[(etp_i + k) % etp_size], "etp", shift)
            return total

        def more_work(*_):
            more_pos = jnp.where(my_pos >= main_rows, my_pos - main_rows, -1)
            more_base = jnp.clip(my_start.T - main_rows, 0, more_rows) // 8 * 8
            order = jnp.arange(etp_size, dtype=jnp.int32)
            x_more = pick([h_all], all_cols, more_pos, None, order, more_base, more_rows)
            c_more = pick(dy_all, dy_cols, more_pos, my_scale, order, more_base, more_rows)
            act_a, act_b, inner, y_part = ffn_act(x_more, (w1, w3, w2), more_rows, 0, etp_size, (), n_more)
            d_a, d_b, dx_part = ffn_grad(c_more, act_a, act_b, (w2, w1, w3), more_rows, 0, 0, etp_size, (), n_more)
            sums = [add_planes(part.reshape(etp_size, more_rows, d_model)).astype(BF16) for part in (y_part, dx_part)]
            return *sums, x_more, c_more, inner, d_a, d_b

        n_more = etp_size * more_rows
        none = jnp.zeros((more_rows, d_model), BF16)
        spare = none, none, *unset(*[(n_more, d_model)] * 2, *[(n_more, w1.shape[1])] * 3)
        any_more = jnp.max(list_len) > main_rows
        y_more, dx_more, x_more, c_more, *more_acts = lax.cond(any_more, more_work, lambda *spare: spare, *spare)

        def more_grads(*grads):
            inner_more, d_a_more, d_b_more = more_acts
            return grads[0] + mm_tn(x_more, d_a_more), grads[1] + mm_tn(x_more, d_b_more), grads[2] + mm_tn(inner_more, c_more)

        home_start = lax.dynamic_index_in_dim(my_start, etp_i, 1, keepdims=False)

        hot = [(expert_ids[:, k : k + 1] == experts[0].T).astype(F32) for k in range(2)]
        probs = lax.dynamic_slice_in_dim(probs_all, block_idx * tok_rows, tok_rows, 1).T
        picked = [jnp.sum(probs * hot[k], axis=1, keepdims=True) for k in range(2)]
        pick_sum = picked[0] + picked[1]
        gates = [picked[k] / pick_sum for k in range(2)]
        my_kept_row = lax.dynamic_index_in_dim(kept, block_idx, 0, keepdims=True).astype(F32)
        rank = mm_tn(earlier, (hot[0] + hot[1]).astype(BF16))
        slot_row = jnp.arange(n_experts * per_expert, dtype=jnp.int32)[None, :]
        slots, chosen = [], []
        for k in range(2):
            rank_k = jnp.sum(rank * hot[k], axis=1, keepdims=True)
            kept_k = jnp.sum(my_kept_row * hot[k], axis=1, keepdims=True)
            slot_k = jnp.where(rank_k < kept_k, expert_ids[:, k : k + 1] * per_expert + rank_k.astype(jnp.int32), -1)
            slots.append(slot_k)
            chosen.append(slot_k == slot_row)

        dw1 = mm_tn(x_main, d_a)
        y_near, dw1, x_main = lax.optimization_barrier((y_near, dw1, x_main))
        y_back = home_blocks(home_start, y_near, y_far, y_more, per_expert)
        y_back = lax.all_to_all(y_back, "ep", 0, 0, tiled=True).reshape(n_experts * per_expert, d_model)
        dw3 = mm_tn(x_main, d_b)
        dw2 = mm_tn(inner, c_main)
        dw1, dw3, dw2 = lax.cond(any_more, more_grads, lambda *grads: grads, dw1, dw3, dw2)
        y_pair = [mm(chosen[k].astype(BF16), y_back) for k in range(2)]
        hidden_f = hidden.astype(F32)
        output = (hidden_f + OUT_SCALE * (gates[0] * y_pair[0] + gates[1] * y_pair[1])).astype(BF16)
        d_out_f = d_out.astype(F32)
        d_gates = [jnp.sum(OUT_SCALE * d_out_f * y_pair[k], axis=1, keepdims=True) for k in range(2)]

        route_frac = jnp.sum(count, axis=0) / (2 * n_tokens)
        aux_loss = AUX_COEF * n_experts * jnp.sum(route_frac * mean_prob)
        mix = gates[0] * d_gates[0] + gates[1] * d_gates[1]
        d_probs = (AUX_COEF * n_experts / n_tokens) * route_frac[None, :]
        for k in range(2):
            d_probs = d_probs + hot[k] * ((d_gates[k] - mix) / pick_sum)
        d_logits = probs * (d_probs - jnp.sum(probs * d_probs, axis=1, keepdims=True))
        d_router_part = mm_tn(d_logits, hidden_f, lax.Precision.HIGHEST)
        d_route = mm_nt(d_logits, w_router, lax.Precision.HIGHEST)
        rest = d_out_f + d_route
        rest, first_far = lax.optimization_barrier((rest, dx_far[0]))
        first_dx = (dx_near[: main_rows // 2] + first_far).astype(BF16)
        dx_near, dw1, dw3, dw2, rest, first_dx, output = lax.optimization_barrier((dx_near, dw1, dw3, dw2, rest, first_dx, output))
        d_hidden, d_router = return_rows(home_start, first_dx, dx_near, dx_far[1], dx_more, d_router_part, jnp.concatenate(slots, axis=1), rest, etp_size, ep_size, per_expert)
        d_router = d_router.T
        return output, d_hidden, d_router, aux_loss, dw1[None], dw3[None], dw2[None]

    return jax.shard_map(layer, mesh=mesh, in_specs=(tok_spec, P(), tok_spec, tok_spec, gate_spec, gate_spec, down_spec), out_specs=(tok_spec, tok_spec, P(), P(), gate_spec, gate_spec, down_spec), check_vma=False)
```

time: 800 us -> 831 us (1.039)
  Pallas kernels: 468 us -> 512 us
  between operations: 17.3 us -> 4.13 us
    pallas_call x4 -> x5, Pallas kernels: 57.8 us -> 109 us  [the longest x1 53.2 us: return_rows(): pl.pallas_call(functools.partial(return_kernel, n_etp), grid=(1,), in_spe...]
    ppermute x0 -> x8, waiting for transfers between devices: none -> 47.7 us  [flip(): return lax.ppermute(array, 'ep', [(o, o ^ bit) for o in range(ep_size)])]
    ppermute x7, waiting for transfers between devices: 114 us -> 76.2 us  [swap(): return lax.ppermute(array, ('etp', 'ep'), pairs)]
  transfers between devices with their start and end apart: 11 -> 16, of which waited for: 4 -> 6; matrix products, arithmetic and copies ran while one was open for 18% -> 18% of each run, Pallas kernels for 40% -> 37%
where the time goes in v3:
time: 831 us; the launch traced here: 820 us
  Pallas kernels  512 us (62%)
  waiting for transfers between devices  124 us (15%)
  matrix products  121 us (15%)
  local copies, waits for them, and re-layouts  23.8 us (3%)
  starting transfers between devices  21.5 us (3%)
  other arithmetic  13.2 us (2%)
    pallas_call x1, Pallas kernels, spread_all(): pl.pallas_call(functools.partial(spread_kernel, n_etp), in_specs=[vmem, v...  149 us
    pallas_call x5, Pallas kernels, ffn_grad(): pl.pallas_call(functools.partial(grad_kernel, with_dx, bool(total), len(b...  118 us
    dot_general x5, matrix products, mm_tn(): lax.dot_general(lhs, rhs, (((0,), (0,)), ((), ())), precision=precision,...  91.8 us
    pallas_call x3, Pallas kernels, ffn_act(): pl.pallas_call(functools.partial(act_kernel, with_y, len(kept)), grid=(n_...  87.4 us
    ppermute x7, waiting for transfers between devices, swap(): return lax.ppermute(array, ('etp', 'ep'), pairs)  76.2 us
    pallas_call x1, Pallas kernels, return_rows(): pl.pallas_call(functools.partial(return_kernel, n_etp), grid=(1,), in_spe...  53.2 us
    ppermute x8, waiting for transfers between devices, flip(): return lax.ppermute(array, 'ep', [(o, o ^ bit) for o in range(ep_size)])  47.7 us
    pallas_call x1, Pallas kernels, ffn_pair(): pl.pallas_call(pair_kernel, grid=(n_tiles,), in_specs=[at(first), at(firs...  41.6 us
  transfers between devices with their start and end apart: 16, of which 6 were waited for; matrix products, arithmetic and copies ran while one was open for 18% of the time, Pallas kernels for 37%

profile of v3, /device:TPU:0, one launch (start us, length us, event | category | flops | bytes accessed | tf_op | source)
XLA Modules:
  0.0 820.1 jit_solution(5674531662106032632)
XLA Ops:
  4.1 148.6 %spread_all.1 = (bf16[32,520,1024]{2,1,0:T(8,128)(2,1)}, bf16[4,512,1024]{2,1,0:T(8,128)(2,1)}) custom-call(bf16[520,1024]{1,0:T(8,128)(2,1)S(1)} %maximum_maximum_fusion.h_ref, bf16[512,1024]{1,0:T(8,128)(2,1)S(1)} %copy-done.1), custom_call_target="tpu_custom_call" | custom-call | flops 99999997952 | bytes 34078720 | tf_op jit(solution)/shard_map/spread_all/pallas_call | solution.py:182
  159.3 15.4 %fusion.27 = f32[24,32,520]{2,0,1:T(8,128)S(1)} fusion(bf16[32,520,1024]{2,1,0:T(8,128)(2,1)} %get-tuple-element.174, bf16[1024,8]{0,1:T(8,128)(2,1)S(1)} %get-tuple-element.254, bf16[1024,8]{0,1:T(8,128)(2,1)S(1)} %get-tuple-element.255, bf16[1024,8]{0,1:T(8,128)(2,1)S(1)} %get-tuple-element.253), kind=kOutput, calls=%fused_computation.76 | convolution fusion | flops 818036736 | bytes 35725312 | tf_op jit(solution)/shard_map/dot_general | solution.py:635
  180.7 20.4 %pick_rows.6.x_ref = bf16[5888,1024]{1,0:T(8,128)(2,1)} custom-call(s32[4]{0:T(128)} %pad_add_fusion.1.planes_ref, s32[8]{0:T(128)} %iota.44.cols_ref, s32[4,8]{1,0:T(4,128)} %gather_fusion, bf16[8,4,520,1024]{3,2,1,0:T(8,128)(2,1)} %bitcast.149, s32[8,4,1,512]{3,2,1,0:T(1,128)} %reshape.394.refs_1_.refs_8_), custom_call_target="tpu_custom_call" | custom-call | flops 7784628224 | bytes 67108864 | tf_op jit(solution)/shard_map/pick_rows/pallas_call | solution.py:225
  202.4 43.7 %collective-permute-done.9.refs_4_ = bf16[4,512,1024]{2,1,0:T(8,128)(2,1)} collective-permute-done((bf16[4,512,1024]{2,1,0:T(8,128)(2,1)}, bf16[4,512,1024]{2,1,0:T(8,128)(2,1)}, u32[]{:S(2)}, u32[]{:S(2)}) %collective-permute-start.9) | collective-permute-done | bytes 4194336 | tf_op jit(solution)/shard_map/ppermute | solution.py:597
  254.3 39.5 %ffn_act.5 = (f32[5888,1792]{1,0:T(8,128)}, f32[5888,1792]{1,0:T(8,128)}, bf16[5888,1792]{1,0:T(8,128)(2,1)}, f32[2944,1024]{1,0:T(8,128)}) custom-call(bf16[5888,1024]{1,0:T(8,128)(2,1)} %pick_rows.6.x_ref, bf16[1024,1792]{1,0:T(8,128)(2,1)} %bitcast.16.refs_0_.refs_1_, bf16[1024,1792]{1,0:T(8,128)(2,1)} %bitcast.17.refs_1_.refs_2_, ...), custom_call_target="tpu_custom_call" | custom-call | flops 32413581312 | bytes 63766528 | tf_op jit(solution)/shard_map/ffn_act/pallas_call | solution.py:279
  306.7 9.1 %collective-permute-done.15.w3.refs_1_.refs_2_ = bf16[1024,1792]{1,0:T(8,128)(2,1)} collective-permute-done((bf16[1024,1792]{1,0:T(8,128)(2,1)}, bf16[1024,1792]{1,0:T(8,128)(2,1)}, u32[]{:S(2)}, u32[]{:S(2)}) %collective-permute-start.15) | collective-permute-done | bytes 3670048 | tf_op jit(solution)/shard_map/ppermute | solution.py:586
  320.5 30.0 %ffn_act.6 = (f32[5888,1792]{1,0:T(8,128)}, f32[5888,1792]{1,0:T(8,128)}, bf16[5888,1792]{1,0:T(8,128)(2,1)}) custom-call(bf16[5888,1024]{1,0:T(8,128)(2,1)} %pick_rows.6.x_ref, bf16[1024,1792]{1,0:T(8,128)(2,1)} %bitcast.16.refs_0_.refs_1_, bf16[1024,1792]{1,0:T(8,128)(2,1)} %bitcast.17.refs_1_.refs_2_, ...), custom_call_target="tpu_custom_call", output_to_operand_aliasing={{0}: (3, {}), {1}: (4, {}), {2}: (5, {})} | custom-call | flops 21609054208 | bytes 63766528 | tf_op jit(solution)/shard_map/ffn_act/pallas_call | solution.py:279
  350.4 17.9 %ffn_act.7 = (f32[1472,1792]{1,0:T(8,128)}, f32[1472,1792]{1,0:T(8,128)}, bf16[1472,1792]{1,0:T(8,128)(2,1)}) custom-call(bf16[5888,1024]{1,0:T(8,128)(2,1)} %pick_rows.6.x_ref, bf16[1024,1792]{1,0:T(8,128)(2,1)} %collective-permute-done.14.w1.refs_0_.refs_1_, bf16[1024,1792]{1,0:T(8,128)(2,1)} %collective-permute-done.15.w3.refs_1_.refs_2_), custom_call_target="tpu_custom_call" | custom-call | flops 10804527104 | bytes 37388288 | tf_op jit(solution)/shard_map/ffn_act/pallas_call | solution.py:279
  368.3 28.6 %collective-permute-done.16.w2.refs_0_ = bf16[1792,1024]{1,0:T(8,128)(2,1)} collective-permute-done((bf16[1792,1024]{1,0:T(8,128)(2,1)}, bf16[1792,1024]{1,0:T(8,128)(2,1)}, u32[]{:S(2)}, u32[]{:S(2)}) %collective-permute-start.16) | collective-permute-done | bytes 3670048 | tf_op jit(solution)/shard_map/ppermute | solution.py:586
  396.9 9.5 %ffn_down.3 = f32[1104,1024]{1,0:T(8,128)} custom-call(bf16[1472,1792]{1,0:T(8,128)(2,1)} %get-tuple-element.206.u_ref, bf16[1792,1024]{1,0:T(8,128)(2,1)} %collective-permute-done.16.w2.refs_0_, f32[2944,1024]{1,0:T(8,128)} %get-tuple-element.176.y_in), custom_call_target="tpu_custom_call" | custom-call | flops 4051697664 | bytes 12713984 | tf_op jit(solution)/shard_map/ffn_down/pallas_call | solution.py:299
  409.4 5.6 ffn_down.2
  416.3 20.5 %pick_rows.7.c_ref = bf16[5888,1024]{1,0:T(8,128)(2,1)} custom-call(s32[4]{0:T(128)} %pad_add_fusion.1.planes_ref, s32[8]{0:T(128)S(1)} %iota_xor_fusion.cols_ref, s32[4,8]{1,0:T(4,128)} %gather_fusion, bf16[4,512,1024]{2,1,0:T(8,128)(2,1)} %get-tuple-element.175.refs_0_, bf16[4,512,1024]{2,1,0:T(8,128)(2,1)} %collective-permute-done.6.refs_1_, ...), custom_call_target="tpu_custom_call" | custom-call | flops 7784628224 | bytes 67108864 | tf_op jit(solution)/shard_map/pick_rows/pallas_call | solution.py:225
  436.8 26.3 %ffn_grad.7 = (bf16[5888,1792]{1,0:T(8,128)(2,1)}, bf16[5888,1792]{1,0:T(8,128)(2,1)}, f32[1472,1024]{1,0:T(8,128)}) custom-call(bf16[5888,1024]{1,0:T(8,128)(2,1)} %pick_rows.7.c_ref, f32[5888,1792]{1,0:T(8,128)} %get-tuple-element.180.a_ref, f32[5888,1792]{1,0:T(8,128)} %get-tuple-element.181.b_ref, bf16[1792,1024]{1,0:T(8,128)(2,1)} %bitcast.153, ...), custom_call_target="tpu_custom_call" | custom-call | flops 16206790656 | bytes 42663936 | tf_op jit(solution)/shard_map/ffn_grad/pallas_call | solution.py:342
  463.1 26.3 %ffn_grad.8 = (bf16[5888,1792]{1,0:T(8,128)(2,1)}, bf16[5888,1792]{1,0:T(8,128)(2,1)}, f32[1472,1024]{1,0:T(8,128)}) custom-call(bf16[5888,1024]{1,0:T(8,128)(2,1)} %pick_rows.7.c_ref, f32[5888,1792]{1,0:T(8,128)} %get-tuple-element.180.a_ref, f32[5888,1792]{1,0:T(8,128)} %get-tuple-element.181.b_ref, ...), custom_call_target="tpu_custom_call", output_to_operand_aliasing={{0}: (6, {}), {1}: (7, {})} | custom-call | flops 16206790656 | bytes 42663936 | tf_op jit(solution)/shard_map/ffn_grad/pallas_call | solution.py:342
  489.4 41.6 %ffn_pair.1 = (f32[1472,1024]{1,0:T(8,128)}, f32[1472,1024]{1,0:T(8,128)}) custom-call(bf16[5888,1024]{1,0:T(8,128)(2,1)} %pick_rows.6.x_ref, bf16[5888,1024]{1,0:T(8,128)(2,1)} %pick_rows.7.c_ref, f32[2944,1024]{1,0:T(8,128)} %get-tuple-element.176.y_in, f32[1472,1024]{1,0:T(8,128)} %get-tuple-element.184.dx_in, ...), custom_call_target="tpu_custom_call" | custom-call | flops 32413581312 | bytes 41156608 | tf_op jit(solution)/shard_map/ffn_pair/pallas_call | solution.py:376
  530.9 30.8 %ffn_grad.9 = (bf16[5888,1792]{1,0:T(8,128)(2,1)}, bf16[5888,1792]{1,0:T(8,128)(2,1)}) custom-call(bf16[5888,1024]{1,0:T(8,128)(2,1)} %pick_rows.7.c_ref, f32[5888,1792]{1,0:T(8,128)} %get-tuple-element.180.a_ref, f32[5888,1792]{1,0:T(8,128)} %get-tuple-element.181.b_ref, ...), custom_call_target="tpu_custom_call", output_to_operand_aliasing={{0}: (4, {}), {1}: (5, {})} | custom-call | flops 10804527104 | bytes 74317824 | tf_op jit(solution)/shard_map/ffn_grad/pallas_call | solution.py:342
  561.7 30.1 %fusion.53 = f32[1024,1792]{1,0:T(8,128)} fusion(bf16[5888,1024]{1,0:T(8,128)(2,1)} %pick_rows.6.x_ref, bf16[5888,1792]{1,0:T(8,128)(2,1)} %get-tuple-element.192), kind=kOutput, calls=%fused_computation.144 | convolution fusion | flops 21609054208 | bytes 40501248 | tf_op jit(solution)/shard_map/dot_general | solution.py:31
  591.8 7.6 home_blocks.1
  605.8 17.5 %ffn_grad.11 = f32[736,1024]{1,0:T(8,128)} custom-call(bf16[5888,1024]{1,0:T(8,128)(2,1)} %pick_rows.7.c_ref, f32[1472,1792]{1,0:T(8,128)} %get-tuple-element.208.a_ref, f32[1472,1792]{1,0:T(8,128)} %get-tuple-element.209.b_ref, bf16[1792,1024]{1,0:T(8,128)(2,1)} %collective-permute-done.16.w2.refs_0_, ...), custom_call_target="tpu_custom_call" | custom-call | flops 8103395328 | bytes 26836992 | tf_op jit(solution)/shard_map/ffn_grad/pallas_call | solution.py:342
  625.7 17.4 %ffn_grad.10 = f32[736,1024]{1,0:T(8,128)} custom-call(bf16[5888,1024]{1,0:T(8,128)(2,1)} %pick_rows.7.c_ref, f32[1472,1792]{1,0:T(8,128)} %get-tuple-element.208.a_ref, f32[1472,1792]{1,0:T(8,128)} %get-tuple-element.209.b_ref, bf16[1792,1024]{1,0:T(8,128)(2,1)} %collective-permute-done.16.w2.refs_0_, ...), custom_call_target="tpu_custom_call" | custom-call | flops 8103395328 | bytes 26836992 | tf_op jit(solution)/shard_map/ffn_grad/pallas_call | solution.py:342
  644.5 29.5 %fusion.55 = f32[1792,1024]{1,0:T(8,128)} fusion(bf16[5888,1792]{1,0:T(8,128)(2,1)} %get-tuple-element.196, bf16[5888,1024]{1,0:T(8,128)(2,1)} %pick_rows.7.c_ref), kind=kOutput, calls=%fused_computation.146 | convolution fusion | flops 21609054208 | bytes 40501248 | tf_op jit(solution)/shard_map/dot_general | solution.py:31
  674.0 29.7 %fusion.54 = f32[1024,1792]{1,0:T(8,128)} fusion(bf16[5888,1024]{1,0:T(8,128)(2,1)} %pick_rows.6.x_ref, bf16[5888,1792]{1,0:T(8,128)(2,1)} %get-tuple-element.195), kind=kOutput, calls=%fused_computation.145 | convolution fusion | flops 21609054208 | bytes 40501248 | tf_op jit(solution)/shard_map/dot_general | solution.py:31
  718.2 38.5 %collective-permute-done.19 = f32[736,1024]{1,0:T(8,128)S(1)} collective-permute-done((f32[736,1024]{1,0:T(8,128)}, f32[736,1024]{1,0:T(8,128)S(1)}, u32[]{:S(2)}, u32[]{:S(2)}) %collective-permute-start.19) | collective-permute-done | bytes 3014688 | tf_op jit(solution)/shard_map/ppermute | solution.py:586
  761.8 53.2 %return_rows.1 = (bf16[512,1024]{1,0:T(8,128)(2,1)}, f32[8,1024]{1,0:T(8,128)}) custom-call(s32[8]{0:T(128)} %copy-done.3, bf16[736,1024]{1,0:T(8,128)(2,1)} %add_convert_fusion.first_ref, f32[1472,1024]{1,0:T(8,128)} %get-tuple-element.215.near_ref, f32[736,1024]{1,0:T(8,128)} %collective-permute-done.20.far_ref, bf16[320,1024]{1,0:T(8,128)(2,1)S(1)} %copy-done.13, ...), custom_call_target="tpu_custom_call" | custom-call | flops 10000000000 | bytes 18087936 | tf_op jit(solution)/shard_map/return_rows/pallas_call | solution.py:529
  (159 shorter events, 79.2 us)
Async XLA Ops:
  4.1 153.1 %copy-start.17 = (s32[512,2]{0,1:T(2,128)S(1)}, s32[512,2]{0,1:T(2,128)}, u32[]{:S(2)}) copy-start(s32[512,2]{0,1:T(2,128)} %param.13) | copy-start | bytes 12292
  4.1 155.2 %copy-start.14 = (f32[1024,8]{0,1:T(8,128)S(1)}, f32[1024,8]{0,1:T(8,128)}, u32[]{:S(2)}) copy-start(f32[1024,8]{0,1:T(8,128)} %param.12) | copy-start | bytes 98308
  152.8 93.3 %collective-permute-start.9 = (bf16[4,512,1024]{2,1,0:T(8,128)(2,1)}, bf16[4,512,1024]{2,1,0:T(8,128)(2,1)}, u32[]{:S(2)}, u32[]{:S(2)}) collective-permute-start(bf16[4,512,1024]{2,1,0:T(8,128)(2,1)} %get-tuple-element.175.refs_0_), channel_id=1, source_target_pairs={{0,4},{1,5},{2,6},{3,7},{4,0},{5,1},{6,2},{7,3},{8,12},{9,13},{10,... | collective-permute-start | bytes 12582920 | tf_op jit(solution)/shard_map/ppermute | solution.py:597
  153.9 96.7 %collective-permute-start.7 = (bf16[4,512,1024]{2,1,0:T(8,128)(2,1)}, bf16[4,512,1024]{2,1,0:T(8,128)(2,1)}, u32[]{:S(2)}, u32[]{:S(2)}) collective-permute-start(bf16[4,512,1024]{2,1,0:T(8,128)(2,1)} %get-tuple-element.175.refs_0_), channel_id=1, source_target_pairs={{0,2},{1,3},{2,0},{3,1},{4,6},{5,7},{6,4},{7,5},{8,10},{9,11},{10,... | collective-permute-start | bytes 12582920 | tf_op jit(solution)/shard_map/ppermute | solution.py:597
  154.9 251.5 %collective-permute-start.6 = (bf16[4,512,1024]{2,1,0:T(8,128)(2,1)}, bf16[4,512,1024]{2,1,0:T(8,128)(2,1)}, u32[]{:S(2)}, u32[]{:S(2)}) collective-permute-start(bf16[4,512,1024]{2,1,0:T(8,128)(2,1)} %get-tuple-element.175.refs_0_), channel_id=1, source_target_pairs={{0,1},{1,0},{2,3},{3,2},{4,5},{5,4},{6,7},{7,6},{8,9},{9,8},{10,11... | collective-permute-start | bytes 12582920 | tf_op jit(solution)/shard_map/ppermute | solution.py:597
  154.9 149.0 %collective-permute-start.14 = (bf16[1024,1792]{1,0:T(8,128)(2,1)}, bf16[1024,1792]{1,0:T(8,128)(2,1)}, u32[]{:S(2)}, u32[]{:S(2)}) collective-permute-start(bf16[1024,1792]{1,0:T(8,128)(2,1)} %bitcast.16.refs_0_.refs_1_), channel_id=1, source_target_pairs={{0,8},{1,25},{2,10},{3,27},{4,12},{5,29},{6,14},{7,31},{8,0},{9,17... | collective-permute-start | bytes 11010056 | tf_op jit(solution)/shard_map/ppermute | solution.py:586
  157.2 158.6 %collective-permute-start.15 = (bf16[1024,1792]{1,0:T(8,128)(2,1)}, bf16[1024,1792]{1,0:T(8,128)(2,1)}, u32[]{:S(2)}, u32[]{:S(2)}) collective-permute-start(bf16[1024,1792]{1,0:T(8,128)(2,1)} %bitcast.17.refs_1_.refs_2_), channel_id=1, source_target_pairs={{0,8},{1,25},{2,10},{3,27},{4,12},{5,29},{6,14},{7,31},{8,0},{9,17... | collective-permute-start | bytes 11010056 | tf_op jit(solution)/shard_map/ppermute | solution.py:586
  202.0 102.5 %copy-start.23 = (s32[512,1]{0,1:T(1,128)}, s32[512,1]{0,1:T(1,128)S(1)}, u32[]{:S(2)}) copy-start(s32[512,1]{0,1:T(1,128)S(1)} %get-tuple-element.257) | copy-start | bytes 6148
  202.0 102.5 %copy-start.25 = (s32[512,1]{0,1:T(1,128)}, s32[512,1]{0,1:T(1,128)S(1)}, u32[]{:S(2)}) copy-start(s32[512,1]{0,1:T(1,128)S(1)} %get-tuple-element.256) | copy-start | bytes 6148
  202.4 52.0 %copy-start.4 = (bf16[1,1792,1024]{2,1,0:T(8,128)(2,1)S(1)}, bf16[1,1792,1024]{2,1,0:T(8,128)(2,1)}, u32[]{:S(2)}) copy-start(bf16[1,1792,1024]{2,1,0:T(8,128)(2,1)} %param.17) | copy-start | bytes 11010052
  249.1 47.4 %collective-permute-start.11 = (bf16[2,512,1024]{2,1,0:T(8,128)(2,1)}, bf16[2,512,1024]{2,1,0:T(8,128)(2,1)}, u32[]{:S(2)}, u32[]{:S(2)}) collective-permute-start(bf16[2,512,1024]{2,1,0:T(8,128)(2,1)} %slice.57), channel_id=1, source_target_pairs={{0,2},{1,3},{2,0},{3,1},{4,6},{5,7},{6,4},{7,5},{8,10},{9,11},{10,... | collective-permute-start | bytes 6291464 | tf_op jit(solution)/shard_map/ppermute | solution.py:597
  253.7 47.1 %collective-permute-start.12 = (bf16[2,512,1024]{2,1,0:T(8,128)(2,1)}, bf16[2,512,1024]{2,1,0:T(8,128)(2,1)}, u32[]{:S(2)}, u32[]{:S(2)}) collective-permute-start(bf16[2,512,1024]{2,1,0:T(8,128)(2,1)} %slice.58), channel_id=1, source_target_pairs={{0,4},{1,5},{2,6},{3,7},{4,0},{5,1},{6,2},{7,3},{8,12},{9,13},{10,... | collective-permute-start | bytes 6291464 | tf_op jit(solution)/shard_map/ppermute | solution.py:597
  296.6 109.9 %collective-permute-start.10 = (bf16[4,512,1024]{2,1,0:T(8,128)(2,1)}, bf16[4,512,1024]{2,1,0:T(8,128)(2,1)}, u32[]{:S(2)}, u32[]{:S(2)}) collective-permute-start(bf16[4,512,1024]{2,1,0:T(8,128)(2,1)} %collective-permute-done.9.refs_4_), channel_id=1, source_target_pairs={{0,1},{1,0},{2,3},{3,2},{4,5},{5,4},{6,7},{7,6},{8,9},{9,8},{10,11... | collective-permute-start | bytes 12582920 | tf_op jit(solution)/shard_map/ppermute | solution.py:597
  300.8 105.6 %collective-permute-start.8 = (bf16[4,512,1024]{2,1,0:T(8,128)(2,1)}, bf16[4,512,1024]{2,1,0:T(8,128)(2,1)}, u32[]{:S(2)}, u32[]{:S(2)}) collective-permute-start(bf16[4,512,1024]{2,1,0:T(8,128)(2,1)} %collective-permute-done.7.refs_2_), channel_id=1, source_target_pairs={{0,1},{1,0},{2,3},{3,2},{4,5},{5,4},{6,7},{7,6},{8,9},{9,8},{10,11... | collective-permute-start | bytes 12582920 | tf_op jit(solution)/shard_map/ppermute | solution.py:597
  303.9 102.5 %collective-permute-start.13 = (bf16[4,512,1024]{2,1,0:T(8,128)(2,1)}, bf16[4,512,1024]{2,1,0:T(8,128)(2,1)}, u32[]{:S(2)}, u32[]{:S(2)}) collective-permute-start(bf16[4,512,1024]{2,1,0:T(8,128)(2,1)} %constant_dynamic-update-slice_fusion.refs_6_), channel_id=1, source_target_pairs={{0,1},{1,0},{2,3},{3,2},{4,5},{5,4},{6,7},{7,6},{8,9},{9,8},{10,11... | collective-permute-start | bytes 12582920 | tf_op jit(solution)/shard_map/ppermute | solution.py:597
  315.8 81.2 %collective-permute-start.16 = (bf16[1792,1024]{1,0:T(8,128)(2,1)}, bf16[1792,1024]{1,0:T(8,128)(2,1)}, u32[]{:S(2)}, u32[]{:S(2)}) collective-permute-start(bf16[1792,1024]{1,0:T(8,128)(2,1)} %bitcast.151), channel_id=1, source_target_pairs={{0,8},{1,25},{2,10},{3,27},{4,12},{5,29},{6,14},{7,31},{8,0},{9,17... | collective-permute-start | bytes 11010056 | tf_op jit(solution)/shard_map/ppermute | solution.py:586
  319.8 272.0 %copy-start.3 = (s32[8]{0:T(128)}, s32[8]{0:T(128)S(1)}, u32[]{:S(2)}) copy-start(s32[8]{0:T(128)S(1)} %fusion.45.start_ref) | copy-start | bytes 100
  406.8 185.0 %collective-permute-start.18 = (f32[1104,1024]{1,0:T(8,128)}, f32[1104,1024]{1,0:T(8,128)}, u32[]{:S(2)}, u32[]{:S(2)}) collective-permute-start(f32[1104,1024]{1,0:T(8,128)} %ffn_down.3), channel_id=1, source_target_pairs={{0,24},{1,9},{2,26},{3,11},{4,28},{5,13},{6,30},{7,15},{8,16},{9,1... | collective-permute-start | bytes 13565960 | tf_op jit(solution)/shard_map/ppermute | solution.py:586
  415.0 176.8 %collective-permute-start.17 = (f32[368,1024]{1,0:T(8,128)}, f32[368,1024]{1,0:T(8,128)}, u32[]{:S(2)}, u32[]{:S(2)}) collective-permute-start(f32[368,1024]{1,0:T(8,128)} %ffn_down.2), channel_id=1, source_target_pairs={{0,24},{1,9},{2,26},{3,11},{4,28},{5,13},{6,30},{7,15},{8,16},{9,1... | collective-permute-start | bytes 4521992 | tf_op jit(solution)/shard_map/ppermute | solution.py:586
  601.2 102.7 %all-to-all-start = ((bf16[8,224,1024]{2,1,0:T(8,128)(2,1)}), bf16[8,224,1024]{2,1,0:T(8,128)(2,1)}, u32[]{:S(2)}, u32[]{:S(2)}) async-start(bf16[8,224,1024]{2,1,0:T(8,128)(2,1)} %copy-done), calls=%async_computation | async-start | bytes 7340032 | tf_op jit(solution)/shard_map/all_to_all | solution.py:710
  623.2 138.5 %collective-permute-start.20 = (f32[736,1024]{1,0:T(8,128)}, f32[736,1024]{1,0:T(8,128)}, u32[]{:S(2)}, u32[]{:S(2)}) collective-permute-start(f32[736,1024]{1,0:T(8,128)} %ffn_grad.11), channel_id=1, source_target_pairs={{0,24},{1,9},{2,26},{3,11},{4,28},{5,13},{6,30},{7,15},{8,16},{9,1... | collective-permute-start | bytes 9043976 | tf_op jit(solution)/shard_map/ppermute | solution.py:586
  643.1 113.6 %collective-permute-start.19 = (f32[736,1024]{1,0:T(8,128)}, f32[736,1024]{1,0:T(8,128)S(1)}, u32[]{:S(2)}, u32[]{:S(2)}) collective-permute-start(f32[736,1024]{1,0:T(8,128)} %ffn_grad.10), channel_id=1, source_target_pairs={{0,24},{1,9},{2,26},{3,11},{4,28},{5,13},{6,30},{7,15},{8,16},{9,1... | collective-permute-start | bytes 9043976 | tf_op jit(solution)/shard_map/ppermute | solution.py:586
  704.4 53.9 %slice-start.2 = ((s8[6029312]{0:T(1024)(128)(4,1)}), s8[4194304]{0:T(1024)(128)(4,1)S(1)}, s32[]{:S(2)}) async-start(s8[6029312]{0:T(1024)(128)(4,1)} %bitcast.166), calls=%async_computation.3 | async-start | bytes 8388608
  708.7 49.5 %slice-start.3 = ((s8[6029312]{0:T(1024)(128)(4,1)}), s8[1835008]{0:T(1024)(128)(4,1)S(1)}, s32[]{:S(2)}) async-start(s8[6029312]{0:T(1024)(128)(4,1)} %bitcast.166), calls=%async_computation.4 | async-start | bytes 3670016
  (20 other events, 254.0 us)

commit v4 on v3

--- a/solution.py
+++ b/solution.py
@@ -327,7 +327,7 @@
         sum_into(dx_ref, base[0] if base else None, lambda cols: mm_nt(da_ref[...], w1[cols, :]) + mm_nt(db_ref[...], w3[cols, :]))
 
 
-def ffn_grad(c, act_a, act_b, weights, tile, first, first_act, n_tiles, kept, total=0, base=()):
+def ffn_grad(c, act_a, act_b, weights, tile, first, first_act, n_tiles, kept, total=0, base=(), dx_rows=0, first_dx=0):
     w2, *w13 = weights
     d_ff, d_model = w2.shape
     with_dx = bool(w13)
@@ -336,8 +336,8 @@
     out_specs = [at(d_ff, first)] * 2 if total else []
     out_shape = [jax.ShapeDtypeStruct((total, d_ff), BF16)] * 2 if total else []
     if with_dx:
-        out_specs.append(at(d_model))
-        out_shape.append(jax.ShapeDtypeStruct((rows, d_model), F32))
+        out_specs.append(at(d_model, first_dx))
+        out_shape.append(jax.ShapeDtypeStruct((dx_rows or rows, d_model), F32))
     n_in = 3 + len(weights) + len(base)
     return pl.pallas_call(
         functools.partial(grad_kernel, with_dx, bool(total), len(base), len(kept)),
@@ -431,13 +431,13 @@
         out_specs=vmem,
         out_shape=jax.ShapeDtypeStruct((n_out, out_rows, d_model), BF16),
         scratch_shapes=[pltpu.VMEM((near.shape[0] + more.shape[0] + win, d_model), F32)],
-        compiler_params=pltpu.CompilerParams(vmem_limit_bytes=40 * MIB),
+        compiler_params=pltpu.CompilerParams(vmem_limit_bytes=58 * MIB),
         cost_estimate=cost(2 * n_out * out_rows * win * d_model, 12 * near.size),
         name="home_blocks",
     )(starts, near, *fars, more)
 
 
-def return_kernel(n_etp, start_ref, first_ref, near_ref, far_ref, more_ref, part_ref, slot_ref, rest_ref, out_ref, total_ref, sum_ref, send_ref, back_ref, z_part, col_part, col_sum, send_sem, back_sem, z_sem, col_sem):
+def return_kernel(n_etp, start_ref, first_ref, near_ref, far_ref, more_ref, part_ref, slot_ref, out_ref, total_ref, sum_ref, send_ref, back_ref, z_part, col_part, col_sum, send_sem, back_sem, z_sem, col_sem):
     t = lax.axis_index("etp")
     o = lax.axis_index("ep")
     n_ep = send_ref.shape[0]
@@ -494,7 +494,7 @@
     col_sum[...] = total
 
     cols = lax.broadcasted_iota(jnp.int32, (slot_ref.shape[0], blk_rows), 1)
-    acc = rest_ref[...]
+    acc = jnp.zeros(out_ref.shape, F32)
     col_copies = {i: to(col_sum, col_part.at[o], col_sem.at[0, i], col_sem.at[1, o], {"ep": col_at(i)}) for i in range(1, n_ep)}
     for k, i in enumerate((0, 1, 2, 4, 3, 5, 6, 7)):
         col = col_at(i)
@@ -506,7 +506,7 @@
         if k == 1:
             for copy in col_copies.values():
                 copy.start()
-    out_ref[...] = acc.astype(out_ref.dtype)
+    out_ref[...] = acc
 
     col_part[o] = col_sum[...]
     for i in range(1, n_ep):
@@ -520,8 +520,9 @@
         copy.wait_send()
 
 
-def return_rows(starts, first, near, far, more, part, slots, rest, n_etp, n_ep, blk_rows):
+def return_rows(starts, first, near, far, more, part, slots, n_etp, n_ep, blk_rows):
     d_model = near.shape[1]
+    out = jax.ShapeDtypeStruct((slots.shape[0], d_model), F32)
     half = far.shape[0]
     dma = pltpu.SemaphoreType.DMA
     vmem = lambda array: rows_at(*array.shape)
@@ -529,9 +530,9 @@
     return pl.pallas_call(
         functools.partial(return_kernel, n_etp),
         grid=(1,),
-        in_specs=[pl.BlockSpec(memory_space=pltpu.SMEM), vmem(first), rows_at(half, d_model, 1), vmem(far), vmem(more), vmem(part), vmem(slots), vmem(rest)],
-        out_specs=[vmem(rest), vmem(part)],
-        out_shape=[jax.ShapeDtypeStruct(rest.shape, BF16), jax.ShapeDtypeStruct(part.shape, F32)],
+        in_specs=[pl.BlockSpec(memory_space=pltpu.SMEM), vmem(first), rows_at(half, d_model, 1), vmem(far), vmem(more), vmem(part), vmem(slots)],
+        out_specs=[vmem(out), vmem(part)],
+        out_shape=[out, jax.ShapeDtypeStruct(part.shape, F32)],
         scratch_shapes=[
             pltpu.VMEM((2 * half + more.shape[0], d_model), BF16),
             blocks,
@@ -547,7 +548,7 @@
         compiler_params=pltpu.CompilerParams(collective_id=1, has_side_effects=True, vmem_limit_bytes=56 * MIB),
         cost_estimate=cost(10**10, 12 * near.size),
         name="return_rows",
-    )(starts, first, near, far, more, part, slots, rest)
+    )(starts, first, near, far, more, part, slots)
 
 
 def split3(value):
@@ -654,7 +655,8 @@
         for i in range(2):
             (dx_part,) = ffn_grad(c_main, far_a, far_b, (w2p, w1p, w3p), tile, 2 * i, 2 * i, 2, (), base=(dx_base,))
             dx_far.append(swap(dx_part, ENDS_PAIRS, NEXT_PAIRS))
-        *grads, dx_base = ffn_grad(c_main, act_a, act_b, (w2, w1, w3), tile, 4, 4, 4, grads, n_rows)
+        grads = ffn_grad(c_main, act_a, act_b, (w2, w1, w3), tile, 4, 4, 2, grads, n_rows, dx_rows=main_rows)
+        *grads, dx_base = ffn_grad(c_main, act_a, act_b, (w2, w1, w3), tile, 6, 6, 2, grads, n_rows, dx_rows=main_rows, first_dx=2)
         y_near, dx_near = ffn_pair(x_main, c_main, y_base, dx_base, (w1p, w3p, w2p), tile, 4, 4, 0)
         d_a, d_b = ffn_grad(c_main, act_a, act_b, (w2,), tile, 8, 8, 8, grads, n_rows)
 
@@ -730,7 +732,8 @@
         rest, first_far = lax.optimization_barrier((rest, dx_far[0]))
         first_dx = (dx_near[: main_rows // 2] + first_far).astype(BF16)
         dx_near, dw1, dw3, dw2, rest, first_dx, output = lax.optimization_barrier((dx_near, dw1, dw3, dw2, rest, first_dx, output))
-        d_hidden, d_router = return_rows(home_start, first_dx, dx_near, dx_far[1], dx_more, d_router_part, jnp.concatenate(slots, axis=1), rest, etp_size, ep_size, per_expert)
+        dx_sum, d_router = return_rows(home_start, first_dx, dx_near, dx_far[1], dx_more, d_router_part, jnp.concatenate(slots, axis=1), etp_size, ep_size, per_expert)
+        d_hidden = (rest + dx_sum).astype(BF16)
         d_router = d_router.T
         return output, d_hidden, d_router, aux_loss, dw1[None], dw3[None], dw2[None]
 

time: 831 us -> 840 us (1.011)
  Pallas kernels: 512 us -> 522 us
    pallas_call x5 -> x6, Pallas kernels: 118 us -> 126 us  [ffn_grad(): pl.pallas_call(functools.partial(grad_kernel, with_dx, bool(total), len(b...]
where the time goes in v4:
time: 840 us; the launch traced here: 829 us
  Pallas kernels  522 us (62%)
  waiting for transfers between devices  125 us (15%)
  matrix products  119 us (14%)
  starting transfers between devices  21.4 us (3%)
  local copies, waits for them, and re-layouts  21.2 us (3%)
  other arithmetic  16.1 us (2%)
    pallas_call x1, Pallas kernels, spread_all(): pl.pallas_call(functools.partial(spread_kernel, n_etp), in_specs=[vmem, v...  149 us
    pallas_call x6, Pallas kernels, ffn_grad(): pl.pallas_call(functools.partial(grad_kernel, with_dx, bool(total), len(b...  126 us
    dot_general x5, matrix products, mm_tn(): lax.dot_general(lhs, rhs, (((0,), (0,)), ((), ())), precision=precision,...  91.8 us
    pallas_call x3, Pallas kernels, ffn_act(): pl.pallas_call(functools.partial(act_kernel, with_y, len(kept)), grid=(n_...  87.4 us
    ppermute x7, waiting for transfers between devices, swap(): return lax.ppermute(array, ('etp', 'ep'), pairs)  77 us
    pallas_call x1, Pallas kernels, return_rows(): pl.pallas_call(functools.partial(return_kernel, n_etp), grid=(1,), in_spe...  53.1 us
    ppermute x8, waiting for transfers between devices, flip(): return lax.ppermute(array, 'ep', [(o, o ^ bit) for o in range(ep_size)])  48.4 us
    pallas_call x1, Pallas kernels, ffn_pair(): pl.pallas_call(pair_kernel, grid=(n_tiles,), in_specs=[at(first), at(firs...  41.3 us
  transfers between devices with their start and end apart: 16, of which 6 were waited for; matrix products, arithmetic and copies ran while one was open for 18% of the time, Pallas kernels for 37%

profile of v4, /device:TPU:0, one launch (start us, length us, event | category | flops | bytes accessed | tf_op | source)
XLA Modules:
  0.0 829.4 jit_solution(16868423663202172636)
XLA Ops:
  4.1 148.6 %spread_all.1 = (bf16[32,520,1024]{2,1,0:T(8,128)(2,1)}, bf16[4,512,1024]{2,1,0:T(8,128)(2,1)}) custom-call(bf16[520,1024]{1,0:T(8,128)(2,1)S(1)} %maximum_maximum_fusion.h_ref, bf16[512,1024]{1,0:T(8,128)(2,1)S(1)} %copy-done), custom_call_target="tpu_custom_call" | custom-call | flops 99999997952 | bytes 34078720 | tf_op jit(solution)/shard_map/spread_all/pallas_call | solution.py:182
  159.3 15.4 %fusion.27 = f32[24,32,520]{2,0,1:T(8,128)S(1)} fusion(bf16[32,520,1024]{2,1,0:T(8,128)(2,1)} %get-tuple-element.177, bf16[1024,8]{0,1:T(8,128)(2,1)S(1)} %get-tuple-element.260, bf16[1024,8]{0,1:T(8,128)(2,1)S(1)} %get-tuple-element.261, bf16[1024,8]{0,1:T(8,128)(2,1)S(1)} %get-tuple-element.259), kind=kOutput, calls=%fused_computation.77 | convolution fusion | flops 818036736 | bytes 35725312 | tf_op jit(solution)/shard_map/dot_general | solution.py:636
  180.0 20.3 %pick_rows.6.x_ref = bf16[5888,1024]{1,0:T(8,128)(2,1)} custom-call(s32[4]{0:T(128)} %pad_add_fusion.1.planes_ref, s32[8]{0:T(128)} %iota.44.cols_ref, s32[4,8]{1,0:T(4,128)} %gather_fusion, bf16[8,4,520,1024]{3,2,1,0:T(8,128)(2,1)} %bitcast.149, s32[8,4,1,512]{3,2,1,0:T(1,128)} %reshape.394.refs_1_.refs_8_), custom_call_target="tpu_custom_call" | custom-call | flops 7784628224 | bytes 67108864 | tf_op jit(solution)/shard_map/pick_rows/pallas_call | solution.py:225
  201.6 44.5 %collective-permute-done.9.refs_4_ = bf16[4,512,1024]{2,1,0:T(8,128)(2,1)} collective-permute-done((bf16[4,512,1024]{2,1,0:T(8,128)(2,1)}, bf16[4,512,1024]{2,1,0:T(8,128)(2,1)}, u32[]{:S(2)}, u32[]{:S(2)}) %collective-permute-start.9) | collective-permute-done | bytes 4194336 | tf_op jit(solution)/shard_map/ppermute | solution.py:598
  254.3 39.6 %ffn_act.5 = (f32[5888,1792]{1,0:T(8,128)}, f32[5888,1792]{1,0:T(8,128)}, bf16[5888,1792]{1,0:T(8,128)(2,1)}, f32[2944,1024]{1,0:T(8,128)}) custom-call(bf16[5888,1024]{1,0:T(8,128)(2,1)} %pick_rows.6.x_ref, bf16[1024,1792]{1,0:T(8,128)(2,1)} %bitcast.16.refs_0_.refs_1_, bf16[1024,1792]{1,0:T(8,128)(2,1)} %bitcast.17.refs_1_.refs_2_, ...), custom_call_target="tpu_custom_call" | custom-call | flops 32413581312 | bytes 63766528 | tf_op jit(solution)/shard_map/ffn_act/pallas_call | solution.py:279
  306.7 9.0 %collective-permute-done.15.w3.refs_1_.refs_2_ = bf16[1024,1792]{1,0:T(8,128)(2,1)} collective-permute-done((bf16[1024,1792]{1,0:T(8,128)(2,1)}, bf16[1024,1792]{1,0:T(8,128)(2,1)}, u32[]{:S(2)}, u32[]{:S(2)}) %collective-permute-start.15) | collective-permute-done | bytes 3670048 | tf_op jit(solution)/shard_map/ppermute | solution.py:587
  320.9 29.9 %ffn_act.6 = (f32[5888,1792]{1,0:T(8,128)}, f32[5888,1792]{1,0:T(8,128)}, bf16[5888,1792]{1,0:T(8,128)(2,1)}) custom-call(bf16[5888,1024]{1,0:T(8,128)(2,1)} %pick_rows.6.x_ref, bf16[1024,1792]{1,0:T(8,128)(2,1)} %bitcast.16.refs_0_.refs_1_, bf16[1024,1792]{1,0:T(8,128)(2,1)} %bitcast.17.refs_1_.refs_2_, ...), custom_call_target="tpu_custom_call", output_to_operand_aliasing={{0}: (3, {}), {1}: (4, {}), {2}: (5, {})} | custom-call | flops 21609054208 | bytes 63766528 | tf_op jit(solution)/shard_map/ffn_act/pallas_call | solution.py:279
  350.8 17.9 %ffn_act.7 = (f32[1472,1792]{1,0:T(8,128)}, f32[1472,1792]{1,0:T(8,128)}, bf16[1472,1792]{1,0:T(8,128)(2,1)}) custom-call(bf16[5888,1024]{1,0:T(8,128)(2,1)} %pick_rows.6.x_ref, bf16[1024,1792]{1,0:T(8,128)(2,1)} %collective-permute-done.14.w1.refs_0_.refs_1_, bf16[1024,1792]{1,0:T(8,128)(2,1)} %collective-permute-done.15.w3.refs_1_.refs_2_), custom_call_target="tpu_custom_call" | custom-call | flops 10804527104 | bytes 37388288 | tf_op jit(solution)/shard_map/ffn_act/pallas_call | solution.py:279
  368.7 28.2 %collective-permute-done.16.w2.refs_0_ = bf16[1792,1024]{1,0:T(8,128)(2,1)} collective-permute-done((bf16[1792,1024]{1,0:T(8,128)(2,1)}, bf16[1792,1024]{1,0:T(8,128)(2,1)}, u32[]{:S(2)}, u32[]{:S(2)}) %collective-permute-start.16) | collective-permute-done | bytes 3670048 | tf_op jit(solution)/shard_map/ppermute | solution.py:587
  396.9 9.4 %ffn_down.3 = f32[1104,1024]{1,0:T(8,128)} custom-call(bf16[1472,1792]{1,0:T(8,128)(2,1)} %get-tuple-element.212.u_ref, bf16[1792,1024]{1,0:T(8,128)(2,1)} %collective-permute-done.16.w2.refs_0_, f32[2944,1024]{1,0:T(8,128)} %get-tuple-element.179.y_in), custom_call_target="tpu_custom_call" | custom-call | flops 4051697664 | bytes 12713984 | tf_op jit(solution)/shard_map/ffn_down/pallas_call | solution.py:299
  417.9 20.5 %pick_rows.7.c_ref = bf16[5888,1024]{1,0:T(8,128)(2,1)} custom-call(s32[4]{0:T(128)} %pad_add_fusion.1.planes_ref, s32[8]{0:T(128)S(1)} %iota_xor_fusion.cols_ref, s32[4,8]{1,0:T(4,128)} %gather_fusion, bf16[4,512,1024]{2,1,0:T(8,128)(2,1)} %get-tuple-element.178.refs_0_, bf16[4,512,1024]{2,1,0:T(8,128)(2,1)} %collective-permute-done.6.refs_1_, ...), custom_call_target="tpu_custom_call" | custom-call | flops 7784628224 | bytes 67108864 | tf_op jit(solution)/shard_map/pick_rows/pallas_call | solution.py:225
  438.3 26.3 %ffn_grad.8 = (bf16[5888,1792]{1,0:T(8,128)(2,1)}, bf16[5888,1792]{1,0:T(8,128)(2,1)}, f32[1472,1024]{1,0:T(8,128)}) custom-call(bf16[5888,1024]{1,0:T(8,128)(2,1)} %pick_rows.7.c_ref, f32[5888,1792]{1,0:T(8,128)} %get-tuple-element.183.a_ref, f32[5888,1792]{1,0:T(8,128)} %get-tuple-element.184.b_ref, bf16[1792,1024]{1,0:T(8,128)(2,1)} %bitcast.153, ...), custom_call_target="tpu_custom_call" | custom-call | flops 16206790656 | bytes 42663936 | tf_op jit(solution)/shard_map/ffn_grad/pallas_call | solution.py:342
  464.6 17.0 %ffn_grad.9 = (bf16[5888,1792]{1,0:T(8,128)(2,1)}, bf16[5888,1792]{1,0:T(8,128)(2,1)}, f32[1472,1024]{1,0:T(8,128)}) custom-call(bf16[5888,1024]{1,0:T(8,128)(2,1)} %pick_rows.7.c_ref, f32[5888,1792]{1,0:T(8,128)} %get-tuple-element.183.a_ref, f32[5888,1792]{1,0:T(8,128)} %get-tuple-element.184.b_ref, ...), custom_call_target="tpu_custom_call", output_to_operand_aliasing={{0}: (6, {}), {1}: (7, {})} | custom-call | flops 8103395328 | bytes 26836992 | tf_op jit(solution)/shard_map/ffn_grad/pallas_call | solution.py:342
  481.6 17.2 %ffn_grad.10 = (bf16[5888,1792]{1,0:T(8,128)(2,1)}, bf16[5888,1792]{1,0:T(8,128)(2,1)}, f32[1472,1024]{1,0:T(8,128)}) custom-call(bf16[5888,1024]{1,0:T(8,128)(2,1)} %pick_rows.7.c_ref, f32[5888,1792]{1,0:T(8,128)} %get-tuple-element.183.a_ref, f32[5888,1792]{1,0:T(8,128)} %get-tuple-element.184.b_ref, ...), custom_call_target="tpu_custom_call", output_to_operand_aliasing={{0}: (6, {}), {1}: (7, {}), {2}: (8, {})} | custom-call | flops 8103395328 | bytes 26836992 | tf_op jit(solution)/shard_map/ffn_grad/pallas_call | solution.py:342
  498.9 41.3 %ffn_pair.1 = (f32[1472,1024]{1,0:T(8,128)}, f32[1472,1024]{1,0:T(8,128)}) custom-call(bf16[5888,1024]{1,0:T(8,128)(2,1)} %pick_rows.6.x_ref, bf16[5888,1024]{1,0:T(8,128)(2,1)} %pick_rows.7.c_ref, f32[2944,1024]{1,0:T(8,128)} %get-tuple-element.179.y_in, f32[1472,1024]{1,0:T(8,128)} %get-tuple-element.190.dx_in, ...), custom_call_target="tpu_custom_call" | custom-call | flops 32413581312 | bytes 41156608 | tf_op jit(solution)/shard_map/ffn_pair/pallas_call | solution.py:376
  540.2 30.8 %ffn_grad.11 = (bf16[5888,1792]{1,0:T(8,128)(2,1)}, bf16[5888,1792]{1,0:T(8,128)(2,1)}) custom-call(bf16[5888,1024]{1,0:T(8,128)(2,1)} %pick_rows.7.c_ref, f32[5888,1792]{1,0:T(8,128)} %get-tuple-element.183.a_ref, f32[5888,1792]{1,0:T(8,128)} %get-tuple-element.184.b_ref, ...), custom_call_target="tpu_custom_call", output_to_operand_aliasing={{0}: (4, {}), {1}: (5, {})} | custom-call | flops 10804527104 | bytes 74317824 | tf_op jit(solution)/shard_map/ffn_grad/pallas_call | solution.py:342
  571.0 30.0 %fusion.53 = f32[1024,1792]{1,0:T(8,128)} fusion(bf16[5888,1024]{1,0:T(8,128)(2,1)} %pick_rows.6.x_ref, bf16[5888,1792]{1,0:T(8,128)(2,1)} %get-tuple-element.198), kind=kOutput, calls=%fused_computation.145 | convolution fusion | flops 21609054208 | bytes 40501248 | tf_op jit(solution)/shard_map/dot_general | solution.py:31
  601.1 9.4 %home_blocks.1 = bf16[8,224,1024]{2,1,0:T(8,128)(2,1)} custom-call(s32[8]{0:T(128)} %fusion.45.start_ref, f32[1472,1024]{1,0:T(8,128)} %get-tuple-element.211.near_ref, f32[368,1024]{1,0:T(8,128)} %collective-permute-done.17.refs_0_, f32[1104,1024]{1,0:T(8,128)} %collective-permute-done.18.refs_1_, bf16[320,1024]{1,0:T(8,128)(2,1)} %get-tuple-element.213.refs_2_), custom_call_target="tpu_custom_call" | custom-call | flops 851443712 | bytes 18087936 | tf_op jit(solution)/shard_map/home_blocks/pallas_call | solution.py:428
  615.0 17.5 %ffn_grad.13 = f32[736,1024]{1,0:T(8,128)} custom-call(bf16[5888,1024]{1,0:T(8,128)(2,1)} %pick_rows.7.c_ref, f32[1472,1792]{1,0:T(8,128)} %get-tuple-element.214.a_ref, f32[1472,1792]{1,0:T(8,128)} %get-tuple-element.215.b_ref, bf16[1792,1024]{1,0:T(8,128)(2,1)} %collective-permute-done.16.w2.refs_0_, ...), custom_call_target="tpu_custom_call" | custom-call | flops 8103395328 | bytes 26836992 | tf_op jit(solution)/shard_map/ffn_grad/pallas_call | solution.py:342
  635.1 17.6 %ffn_grad.12 = f32[736,1024]{1,0:T(8,128)} custom-call(bf16[5888,1024]{1,0:T(8,128)(2,1)} %pick_rows.7.c_ref, f32[1472,1792]{1,0:T(8,128)} %get-tuple-element.214.a_ref, f32[1472,1792]{1,0:T(8,128)} %get-tuple-element.215.b_ref, bf16[1792,1024]{1,0:T(8,128)(2,1)} %collective-permute-done.16.w2.refs_0_, ...), custom_call_target="tpu_custom_call" | custom-call | flops 8103395328 | bytes 26836992 | tf_op jit(solution)/shard_map/ffn_grad/pallas_call | solution.py:342
  654.0 29.5 %fusion.55 = f32[1792,1024]{1,0:T(8,128)} fusion(bf16[5888,1792]{1,0:T(8,128)(2,1)} %get-tuple-element.202, bf16[5888,1024]{1,0:T(8,128)(2,1)} %pick_rows.7.c_ref), kind=kOutput, calls=%fused_computation.147 | convolution fusion | flops 21609054208 | bytes 40501248 | tf_op jit(solution)/shard_map/dot_general | solution.py:31
  683.5 29.7 %fusion.54 = f32[1024,1792]{1,0:T(8,128)} fusion(bf16[5888,1024]{1,0:T(8,128)(2,1)} %pick_rows.6.x_ref, bf16[5888,1792]{1,0:T(8,128)(2,1)} %get-tuple-element.201), kind=kOutput, calls=%fused_computation.146 | convolution fusion | flops 21609054208 | bytes 40501248 | tf_op jit(solution)/shard_map/dot_general | solution.py:31
  726.4 39.7 %collective-permute-done.19 = f32[736,1024]{1,0:T(8,128)S(1)} collective-permute-done((f32[736,1024]{1,0:T(8,128)}, f32[736,1024]{1,0:T(8,128)S(1)}, u32[]{:S(2)}, u32[]{:S(2)}) %collective-permute-start.19) | collective-permute-done | bytes 3014688 | tf_op jit(solution)/shard_map/ppermute | solution.py:587
  771.2 53.1 %return_rows.1 = (f32[512,1024]{1,0:T(8,128)}, f32[8,1024]{1,0:T(8,128)}) custom-call(s32[8]{0:T(128)} %fusion.45.start_ref, bf16[736,1024]{1,0:T(8,128)(2,1)} %add_convert_fusion.first_ref, f32[1472,1024]{1,0:T(8,128)} %get-tuple-element.222.near_ref, f32[736,1024]{1,0:T(8,128)} %collective-permute-done.20.far_ref, ...), custom_call_target="tpu_custom_call" | custom-call | flops 10000000000 | bytes 18087936 | tf_op jit(solution)/shard_map/return_rows/pallas_call | solution.py:530
  (148 shorter events, 84.6 us)
Async XLA Ops:
  4.1 153.1 %copy-start.11 = (s32[512,2]{0,1:T(2,128)S(1)}, s32[512,2]{0,1:T(2,128)}, u32[]{:S(2)}) copy-start(s32[512,2]{0,1:T(2,128)} %param.13) | copy-start | bytes 12292
  4.1 155.2 %copy-start.9 = (f32[1024,8]{0,1:T(8,128)S(1)}, f32[1024,8]{0,1:T(8,128)}, u32[]{:S(2)}) copy-start(f32[1024,8]{0,1:T(8,128)} %param.12) | copy-start | bytes 98308
  152.8 93.3 %collective-permute-start.9 = (bf16[4,512,1024]{2,1,0:T(8,128)(2,1)}, bf16[4,512,1024]{2,1,0:T(8,128)(2,1)}, u32[]{:S(2)}, u32[]{:S(2)}) collective-permute-start(bf16[4,512,1024]{2,1,0:T(8,128)(2,1)} %get-tuple-element.178.refs_0_), channel_id=1, source_target_pairs={{0,4},{1,5},{2,6},{3,7},{4,0},{5,1},{6,2},{7,3},{8,12},{9,13},{10,... | collective-permute-start | bytes 12582920 | tf_op jit(solution)/shard_map/ppermute | solution.py:598
  153.9 96.7 %collective-permute-start.7 = (bf16[4,512,1024]{2,1,0:T(8,128)(2,1)}, bf16[4,512,1024]{2,1,0:T(8,128)(2,1)}, u32[]{:S(2)}, u32[]{:S(2)}) collective-permute-start(bf16[4,512,1024]{2,1,0:T(8,128)(2,1)} %get-tuple-element.178.refs_0_), channel_id=1, source_target_pairs={{0,2},{1,3},{2,0},{3,1},{4,6},{5,7},{6,4},{7,5},{8,10},{9,11},{10,... | collective-permute-start | bytes 12582920 | tf_op jit(solution)/shard_map/ppermute | solution.py:598
  154.9 251.4 %collective-permute-start.6 = (bf16[4,512,1024]{2,1,0:T(8,128)(2,1)}, bf16[4,512,1024]{2,1,0:T(8,128)(2,1)}, u32[]{:S(2)}, u32[]{:S(2)}) collective-permute-start(bf16[4,512,1024]{2,1,0:T(8,128)(2,1)} %get-tuple-element.178.refs_0_), channel_id=1, source_target_pairs={{0,1},{1,0},{2,3},{3,2},{4,5},{5,4},{6,7},{7,6},{8,9},{9,8},{10,11... | collective-permute-start | bytes 12582920 | tf_op jit(solution)/shard_map/ppermute | solution.py:598
  154.9 149.0 %collective-permute-start.14 = (bf16[1024,1792]{1,0:T(8,128)(2,1)}, bf16[1024,1792]{1,0:T(8,128)(2,1)}, u32[]{:S(2)}, u32[]{:S(2)}) collective-permute-start(bf16[1024,1792]{1,0:T(8,128)(2,1)} %bitcast.16.refs_0_.refs_1_), channel_id=1, source_target_pairs={{0,8},{1,25},{2,10},{3,27},{4,12},{5,29},{6,14},{7,31},{8,0},{9,17... | collective-permute-start | bytes 11010056 | tf_op jit(solution)/shard_map/ppermute | solution.py:587
  157.2 158.6 %collective-permute-start.15 = (bf16[1024,1792]{1,0:T(8,128)(2,1)}, bf16[1024,1792]{1,0:T(8,128)(2,1)}, u32[]{:S(2)}, u32[]{:S(2)}) collective-permute-start(bf16[1024,1792]{1,0:T(8,128)(2,1)} %bitcast.17.refs_1_.refs_2_), channel_id=1, source_target_pairs={{0,8},{1,25},{2,10},{3,27},{4,12},{5,29},{6,14},{7,31},{8,0},{9,17... | collective-permute-start | bytes 11010056 | tf_op jit(solution)/shard_map/ppermute | solution.py:587
  201.2 103.2 %copy-start.18 = (s32[512,1]{0,1:T(1,128)}, s32[512,1]{0,1:T(1,128)S(1)}, u32[]{:S(2)}) copy-start(s32[512,1]{0,1:T(1,128)S(1)} %get-tuple-element.263) | copy-start | bytes 6148
  201.2 103.2 %copy-start.20 = (s32[512,1]{0,1:T(1,128)}, s32[512,1]{0,1:T(1,128)S(1)}, u32[]{:S(2)}) copy-start(s32[512,1]{0,1:T(1,128)S(1)} %get-tuple-element.262) | copy-start | bytes 6148
  201.6 52.7 %copy-start.2 = (bf16[1,1792,1024]{2,1,0:T(8,128)(2,1)S(1)}, bf16[1,1792,1024]{2,1,0:T(8,128)(2,1)}, u32[]{:S(2)}) copy-start(bf16[1,1792,1024]{2,1,0:T(8,128)(2,1)} %param.17) | copy-start | bytes 11010052
  249.1 47.4 %collective-permute-start.11 = (bf16[2,512,1024]{2,1,0:T(8,128)(2,1)}, bf16[2,512,1024]{2,1,0:T(8,128)(2,1)}, u32[]{:S(2)}, u32[]{:S(2)}) collective-permute-start(bf16[2,512,1024]{2,1,0:T(8,128)(2,1)} %slice.57), channel_id=1, source_target_pairs={{0,2},{1,3},{2,0},{3,1},{4,6},{5,7},{6,4},{7,5},{8,10},{9,11},{10,... | collective-permute-start | bytes 6291464 | tf_op jit(solution)/shard_map/ppermute | solution.py:598
  253.7 47.1 %collective-permute-start.12 = (bf16[2,512,1024]{2,1,0:T(8,128)(2,1)}, bf16[2,512,1024]{2,1,0:T(8,128)(2,1)}, u32[]{:S(2)}, u32[]{:S(2)}) collective-permute-start(bf16[2,512,1024]{2,1,0:T(8,128)(2,1)} %slice.58), channel_id=1, source_target_pairs={{0,4},{1,5},{2,6},{3,7},{4,0},{5,1},{6,2},{7,3},{8,12},{9,13},{10,... | collective-permute-start | bytes 6291464 | tf_op jit(solution)/shard_map/ppermute | solution.py:598
  296.6 109.8 %collective-permute-start.10 = (bf16[4,512,1024]{2,1,0:T(8,128)(2,1)}, bf16[4,512,1024]{2,1,0:T(8,128)(2,1)}, u32[]{:S(2)}, u32[]{:S(2)}) collective-permute-start(bf16[4,512,1024]{2,1,0:T(8,128)(2,1)} %collective-permute-done.9.refs_4_), channel_id=1, source_target_pairs={{0,1},{1,0},{2,3},{3,2},{4,5},{5,4},{6,7},{7,6},{8,9},{9,8},{10,11... | collective-permute-start | bytes 12582920 | tf_op jit(solution)/shard_map/ppermute | solution.py:598
  300.8 105.5 %collective-permute-start.8 = (bf16[4,512,1024]{2,1,0:T(8,128)(2,1)}, bf16[4,512,1024]{2,1,0:T(8,128)(2,1)}, u32[]{:S(2)}, u32[]{:S(2)}) collective-permute-start(bf16[4,512,1024]{2,1,0:T(8,128)(2,1)} %collective-permute-done.7.refs_2_), channel_id=1, source_target_pairs={{0,1},{1,0},{2,3},{3,2},{4,5},{5,4},{6,7},{7,6},{8,9},{9,8},{10,11... | collective-permute-start | bytes 12582920 | tf_op jit(solution)/shard_map/ppermute | solution.py:598
  303.9 102.5 %collective-permute-start.13 = (bf16[4,512,1024]{2,1,0:T(8,128)(2,1)}, bf16[4,512,1024]{2,1,0:T(8,128)(2,1)}, u32[]{:S(2)}, u32[]{:S(2)}) collective-permute-start(bf16[4,512,1024]{2,1,0:T(8,128)(2,1)} %constant_dynamic-update-slice_fusion.refs_6_), channel_id=1, source_target_pairs={{0,1},{1,0},{2,3},{3,2},{4,5},{5,4},{6,7},{7,6},{8,9},{9,8},{10,11... | collective-permute-start | bytes 12582920 | tf_op jit(solution)/shard_map/ppermute | solution.py:598
  315.8 81.2 %collective-permute-start.16 = (bf16[1792,1024]{1,0:T(8,128)(2,1)}, bf16[1792,1024]{1,0:T(8,128)(2,1)}, u32[]{:S(2)}, u32[]{:S(2)}) collective-permute-start(bf16[1792,1024]{1,0:T(8,128)(2,1)} %bitcast.151), channel_id=1, source_target_pairs={{0,8},{1,25},{2,10},{3,27},{4,12},{5,29},{6,14},{7,31},{8,0},{9,17... | collective-permute-start | bytes 11010056 | tf_op jit(solution)/shard_map/ppermute | solution.py:587
  408.4 192.6 %collective-permute-start.18 = (f32[1104,1024]{1,0:T(8,128)}, f32[1104,1024]{1,0:T(8,128)}, u32[]{:S(2)}, u32[]{:S(2)}) collective-permute-start(f32[1104,1024]{1,0:T(8,128)} %ffn_down.3), channel_id=1, source_target_pairs={{0,24},{1,9},{2,26},{3,11},{4,28},{5,13},{6,30},{7,15},{8,16},{9,1... | collective-permute-start | bytes 13565960 | tf_op jit(solution)/shard_map/ppermute | solution.py:587
  416.6 184.5 %collective-permute-start.17 = (f32[368,1024]{1,0:T(8,128)}, f32[368,1024]{1,0:T(8,128)}, u32[]{:S(2)}, u32[]{:S(2)}) collective-permute-start(f32[368,1024]{1,0:T(8,128)} %ffn_down.2), channel_id=1, source_target_pairs={{0,24},{1,9},{2,26},{3,11},{4,28},{5,13},{6,30},{7,15},{8,16},{9,1... | collective-permute-start | bytes 4521992 | tf_op jit(solution)/shard_map/ppermute | solution.py:587
  610.5 102.8 %all-to-all-start = ((bf16[8,224,1024]{2,1,0:T(8,128)(2,1)}), bf16[8,224,1024]{2,1,0:T(8,128)(2,1)}, u32[]{:S(2)}, u32[]{:S(2)}) async-start(bf16[8,224,1024]{2,1,0:T(8,128)(2,1)} %home_blocks.1), calls=%async_computation | async-start | bytes 7340032 | tf_op jit(solution)/shard_map/all_to_all | solution.py:712
  632.5 138.7 %collective-permute-start.20 = (f32[736,1024]{1,0:T(8,128)}, f32[736,1024]{1,0:T(8,128)}, u32[]{:S(2)}, u32[]{:S(2)}) collective-permute-start(f32[736,1024]{1,0:T(8,128)} %ffn_grad.13), channel_id=1, source_target_pairs={{0,24},{1,9},{2,26},{3,11},{4,28},{5,13},{6,30},{7,15},{8,16},{9,1... | collective-permute-start | bytes 9043976 | tf_op jit(solution)/shard_map/ppermute | solution.py:587
  652.7 113.4 %collective-permute-start.19 = (f32[736,1024]{1,0:T(8,128)}, f32[736,1024]{1,0:T(8,128)S(1)}, u32[]{:S(2)}, u32[]{:S(2)}) collective-permute-start(f32[736,1024]{1,0:T(8,128)} %ffn_grad.12), channel_id=1, source_target_pairs={{0,24},{1,9},{2,26},{3,11},{4,28},{5,13},{6,30},{7,15},{8,16},{9,1... | collective-permute-start | bytes 9043976 | tf_op jit(solution)/shard_map/ppermute | solution.py:587
  713.8 53.8 %slice-start.2 = ((s8[6029312]{0:T(1024)(128)(4,1)}), s8[4194304]{0:T(1024)(128)(4,1)S(1)}, s32[]{:S(2)}) async-start(s8[6029312]{0:T(1024)(128)(4,1)} %bitcast.167), calls=%async_computation.3 | async-start | bytes 8388608
  718.2 49.4 %slice-start.3 = ((s8[6029312]{0:T(1024)(128)(4,1)}), s8[1835008]{0:T(1024)(128)(4,1)S(1)}, s32[]{:S(2)}) async-start(s8[6029312]{0:T(1024)(128)(4,1)} %bitcast.167), calls=%async_computation.4 | async-start | bytes 3670016
  722.7 43.4 %copy-start.4 = (bf16[512,1024]{1,0:T(8,128)(2,1)S(1)}, bf16[512,1024]{1,0:T(8,128)(2,1)}, u32[]{:S(2)}) copy-start(bf16[512,1024]{1,0:T(8,128)(2,1)} %param.11) | copy-start | bytes 3145732
  (14 other events, 150.5 us)

commit v5 on v4

--- a/solution.py
+++ b/solution.py
@@ -327,7 +327,7 @@
         sum_into(dx_ref, base[0] if base else None, lambda cols: mm_nt(da_ref[...], w1[cols, :]) + mm_nt(db_ref[...], w3[cols, :]))
 
 
-def ffn_grad(c, act_a, act_b, weights, tile, first, first_act, n_tiles, kept, total=0, base=(), dx_rows=0, first_dx=0):
+def ffn_grad(c, act_a, act_b, weights, tile, first, first_act, n_tiles, kept, total=0, base=()):
     w2, *w13 = weights
     d_ff, d_model = w2.shape
     with_dx = bool(w13)
@@ -336,8 +336,8 @@
     out_specs = [at(d_ff, first)] * 2 if total else []
     out_shape = [jax.ShapeDtypeStruct((total, d_ff), BF16)] * 2 if total else []
     if with_dx:
-        out_specs.append(at(d_model, first_dx))
-        out_shape.append(jax.ShapeDtypeStruct((dx_rows or rows, d_model), F32))
+        out_specs.append(at(d_model))
+        out_shape.append(jax.ShapeDtypeStruct((rows, d_model), F32))
     n_in = 3 + len(weights) + len(base)
     return pl.pallas_call(
         functools.partial(grad_kernel, with_dx, bool(total), len(base), len(kept)),
@@ -437,7 +437,7 @@
     )(starts, near, *fars, more)
 
 
-def return_kernel(n_etp, start_ref, first_ref, near_ref, far_ref, more_ref, part_ref, slot_ref, out_ref, total_ref, sum_ref, send_ref, back_ref, z_part, col_part, col_sum, send_sem, back_sem, z_sem, col_sem):
+def return_kernel(n_etp, start_ref, near_ref, far_ref, more_ref, part_ref, slot_ref, out_ref, total_ref, sum_ref, send_ref, back_ref, z_part, col_part, col_sum, send_sem, back_sem, z_sem, col_sem):
     t = lax.axis_index("etp")
     o = lax.axis_index("ep")
     n_ep = send_ref.shape[0]
@@ -464,10 +464,8 @@
     for copy in z_copies:
         copy.start()
 
-    rows = first_ref.shape[0]
-    sum_ref[:rows, :] = first_ref[...]
-    end = rows + far_ref.shape[0]
-    sum_ref[rows:end, :] = (near_ref[...] + far_ref[...]).astype(BF16)
+    end = far_ref.shape[0]
+    sum_ref[:end, :] = (near_ref[...] + far_ref[...]).astype(BF16)
     sum_ref[end:, :] = more_ref[...]
 
     blk_rows = send_ref.shape[1]
@@ -520,21 +518,20 @@
         copy.wait_send()
 
 
-def return_rows(starts, first, near, far, more, part, slots, n_etp, n_ep, blk_rows):
+def return_rows(starts, near, far, more, part, slots, n_etp, n_ep, blk_rows):
     d_model = near.shape[1]
     out = jax.ShapeDtypeStruct((slots.shape[0], d_model), F32)
-    half = far.shape[0]
     dma = pltpu.SemaphoreType.DMA
     vmem = lambda array: rows_at(*array.shape)
     blocks = pltpu.VMEM((n_ep, blk_rows, d_model), BF16)
     return pl.pallas_call(
         functools.partial(return_kernel, n_etp),
         grid=(1,),
-        in_specs=[pl.BlockSpec(memory_space=pltpu.SMEM), vmem(first), rows_at(half, d_model, 1), vmem(far), vmem(more), vmem(part), vmem(slots)],
+        in_specs=[pl.BlockSpec(memory_space=pltpu.SMEM), vmem(near), vmem(far), vmem(more), vmem(part), vmem(slots)],
         out_specs=[vmem(out), vmem(part)],
         out_shape=[out, jax.ShapeDtypeStruct(part.shape, F32)],
         scratch_shapes=[
-            pltpu.VMEM((2 * half + more.shape[0], d_model), BF16),
+            pltpu.VMEM((near.shape[0] + more.shape[0], d_model), BF16),
             blocks,
             blocks,
             pltpu.VMEM((n_etp, *part.shape), F32),
@@ -545,10 +542,10 @@
             dma((2, n_etp)),
             dma((2, n_ep)),
         ],
-        compiler_params=pltpu.CompilerParams(collective_id=1, has_side_effects=True, vmem_limit_bytes=56 * MIB),
+        compiler_params=pltpu.CompilerParams(collective_id=1, has_side_effects=True, vmem_limit_bytes=42 * MIB),
         cost_estimate=cost(10**10, 12 * near.size),
         name="return_rows",
-    )(starts, first, near, far, more, part, slots)
+    )(starts, near, far, more, part, slots)
 
 
 def split3(value):
@@ -648,15 +645,13 @@
         act_a, act_b, inner = ffn_act(x_main, (w1, w3), tile, 8, 8, acts, n_rows)
         far_a, far_b, far_u = ffn_act(x_main, (w1p, w3p), tile, 0, 4, (), main_rows)
         *grads, dx_base = ffn_grad(c_main, act_a, act_b, (w2, w1, w3), tile, 0, 0, 4, (), n_rows)
-        y_far, dx_far = [], []
+        y_far = []
         for i, n_tiles in enumerate((1, 3)):
             y_part = ffn_down(far_u, w2p, y_base, tile, i, n_tiles)
             y_far.append(swap(y_part, ENDS_PAIRS, NEXT_PAIRS))
-        for i in range(2):
-            (dx_part,) = ffn_grad(c_main, far_a, far_b, (w2p, w1p, w3p), tile, 2 * i, 2 * i, 2, (), base=(dx_base,))
-            dx_far.append(swap(dx_part, ENDS_PAIRS, NEXT_PAIRS))
-        grads = ffn_grad(c_main, act_a, act_b, (w2, w1, w3), tile, 4, 4, 2, grads, n_rows, dx_rows=main_rows)
-        *grads, dx_base = ffn_grad(c_main, act_a, act_b, (w2, w1, w3), tile, 6, 6, 2, grads, n_rows, dx_rows=main_rows, first_dx=2)
+        (dx_part,) = ffn_grad(c_main, far_a, far_b, (w2p, w1p, w3p), tile, 0, 0, 4, (), base=(dx_base,))
+        dx_far = swap(dx_part, ENDS_PAIRS, NEXT_PAIRS)
+        *grads, dx_base = ffn_grad(c_main, act_a, act_b, (w2, w1, w3), tile, 4, 4, 4, grads, n_rows)
         y_near, dx_near = ffn_pair(x_main, c_main, y_base, dx_base, (w1p, w3p, w2p), tile, 4, 4, 0)
         d_a, d_b = ffn_grad(c_main, act_a, act_b, (w2,), tile, 8, 8, 8, grads, n_rows)
 
@@ -729,10 +724,8 @@
         d_router_part = mm_tn(d_logits, hidden_f, lax.Precision.HIGHEST)
         d_route = mm_nt(d_logits, w_router, lax.Precision.HIGHEST)
         rest = d_out_f + d_route
-        rest, first_far = lax.optimization_barrier((rest, dx_far[0]))
-        first_dx = (dx_near[: main_rows // 2] + first_far).astype(BF16)
-        dx_near, dw1, dw3, dw2, rest, first_dx, output = lax.optimization_barrier((dx_near, dw1, dw3, dw2, rest, first_dx, output))
-        dx_sum, d_router = return_rows(home_start, first_dx, dx_near, dx_far[1], dx_more, d_router_part, jnp.concatenate(slots, axis=1), etp_size, ep_size, per_expert)
+        dx_near, dw1, dw3, dw2, rest, output = lax.optimization_barrier((dx_near, dw1, dw3, dw2, rest, output))
+        dx_sum, d_router = return_rows(home_start, dx_near, dx_far, dx_more, d_router_part, jnp.concatenate(slots, axis=1), etp_size, ep_size, per_expert)
         d_hidden = (rest + dx_sum).astype(BF16)
         d_router = d_router.T
         return output, d_hidden, d_router, aux_loss, dw1[None], dw3[None], dw2[None]

time: 840 us -> 832 us (level)
    pallas_call x6 -> x4, Pallas kernels: 126 us -> 110 us  [ffn_grad(): pl.pallas_call(functools.partial(grad_kernel, with_dx, bool(total), len(b...]
    pallas_call x3, Pallas kernels: 87.4 us -> 99.8 us  [ffn_act(): pl.pallas_call(functools.partial(act_kernel, with_y, len(kept)), grid=(n_...]
    ppermute x7 -> x6, waiting for transfers between devices: 77 us -> 81.6 us  [swap(): return lax.ppermute(array, ('etp', 'ep'), pairs)]
  transfers between devices with their start and end apart: 16 -> 15, of which waited for: 6 -> 6; matrix products, arithmetic and copies ran while one was open for 18% -> 17% of each run, Pallas kernels for 37% -> 37%
where the time goes in v5:
time: 832 us; the launch traced here: 821 us
  Pallas kernels  516 us (62%)
  waiting for transfers between devices  130 us (16%)
  matrix products  118 us (14%)
  starting transfers between devices  20.2 us (2%)
  local copies, waits for them, and re-layouts  19.7 us (2%)
  other arithmetic  12.8 us (2%)
    pallas_call x1, Pallas kernels, spread_all(): pl.pallas_call(functools.partial(spread_kernel, n_etp), in_specs=[vmem, v...  149 us
    pallas_call x4, Pallas kernels, ffn_grad(): pl.pallas_call(functools.partial(grad_kernel, with_dx, bool(total), len(b...  110 us
    pallas_call x3, Pallas kernels, ffn_act(): pl.pallas_call(functools.partial(act_kernel, with_y, len(kept)), grid=(n_...  99.8 us
    dot_general x5, matrix products, mm_tn(): lax.dot_general(lhs, rhs, (((0,), (0,)), ((), ())), precision=precision,...  91 us
    ppermute x6, waiting for transfers between devices, swap(): return lax.ppermute(array, ('etp', 'ep'), pairs)  81.6 us
    pallas_call x1, Pallas kernels, return_rows(): pl.pallas_call(functools.partial(return_kernel, n_etp), grid=(1,), in_spe...  51.2 us
    ppermute x8, waiting for transfers between devices, flip(): return lax.ppermute(array, 'ep', [(o, o ^ bit) for o in range(ep_size)])  48.2 us
    pallas_call x1, Pallas kernels, ffn_pair(): pl.pallas_call(pair_kernel, grid=(n_tiles,), in_specs=[at(first), at(firs...  41.5 us
  transfers between devices with their start and end apart: 15, of which 6 were waited for; matrix products, arithmetic and copies ran while one was open for 17% of the time, Pallas kernels for 37%

profile of v5, /device:TPU:0, one launch (start us, length us, event | category | flops | bytes accessed | tf_op | source)
XLA Modules:
  0.0 821.3 jit_solution(5793608816749257269)
XLA Ops:
  4.1 148.6 %spread_all.1 = (bf16[32,520,1024]{2,1,0:T(8,128)(2,1)}, bf16[4,512,1024]{2,1,0:T(8,128)(2,1)}) custom-call(bf16[520,1024]{1,0:T(8,128)(2,1)S(1)} %maximum_maximum_fusion.h_ref, bf16[512,1024]{1,0:T(8,128)(2,1)S(1)} %copy-done), custom_call_target="tpu_custom_call" | custom-call | flops 99999997952 | bytes 34078720 | tf_op jit(solution)/shard_map/spread_all/pallas_call | solution.py:182
  159.3 15.4 %fusion.27 = f32[24,32,520]{2,0,1:T(8,128)S(1)} fusion(bf16[32,520,1024]{2,1,0:T(8,128)(2,1)} %get-tuple-element.171, bf16[1024,8]{0,1:T(8,128)(2,1)S(1)} %get-tuple-element.248, bf16[1024,8]{0,1:T(8,128)(2,1)S(1)} %get-tuple-element.249, bf16[1024,8]{0,1:T(8,128)(2,1)S(1)} %get-tuple-element.247), kind=kOutput, calls=%fused_computation.76 | convolution fusion | flops 818036736 | bytes 35725312 | tf_op jit(solution)/shard_map/dot_general | solution.py:633
  180.1 20.3 %pick_rows.6.x_ref = bf16[5888,1024]{1,0:T(8,128)(2,1)} custom-call(s32[4]{0:T(128)} %pad_add_fusion.1.planes_ref, s32[8]{0:T(128)} %iota.44.cols_ref, s32[4,8]{1,0:T(4,128)} %gather_fusion, bf16[8,4,520,1024]{3,2,1,0:T(8,128)(2,1)} %bitcast.152, s32[8,4,1,512]{3,2,1,0:T(1,128)} %reshape.394.refs_1_.refs_8_), custom_call_target="tpu_custom_call" | custom-call | flops 7784628224 | bytes 67108864 | tf_op jit(solution)/shard_map/pick_rows/pallas_call | solution.py:225
  201.6 44.4 %collective-permute-done.9.refs_4_ = bf16[4,512,1024]{2,1,0:T(8,128)(2,1)} collective-permute-done((bf16[4,512,1024]{2,1,0:T(8,128)(2,1)}, bf16[4,512,1024]{2,1,0:T(8,128)(2,1)}, u32[]{:S(2)}, u32[]{:S(2)}) %collective-permute-start.9) | collective-permute-done | bytes 4194336 | tf_op jit(solution)/shard_map/ppermute | solution.py:595
  254.3 39.6 %ffn_act.5 = (f32[5888,1792]{1,0:T(8,128)}, f32[5888,1792]{1,0:T(8,128)}, bf16[5888,1792]{1,0:T(8,128)(2,1)}, f32[2944,1024]{1,0:T(8,128)}) custom-call(bf16[5888,1024]{1,0:T(8,128)(2,1)} %pick_rows.6.x_ref, bf16[1024,1792]{1,0:T(8,128)(2,1)} %bitcast.16.refs_0_.refs_1_, bf16[1024,1792]{1,0:T(8,128)(2,1)} %bitcast.17.refs_1_.refs_2_, ...), custom_call_target="tpu_custom_call" | custom-call | flops 32413581312 | bytes 63766528 | tf_op jit(solution)/shard_map/ffn_act/pallas_call | solution.py:279
  306.0 9.8 %collective-permute-done.15.w3.refs_1_.refs_2_ = bf16[1024,1792]{1,0:T(8,128)(2,1)} collective-permute-done((bf16[1024,1792]{1,0:T(8,128)(2,1)}, bf16[1024,1792]{1,0:T(8,128)(2,1)}, u32[]{:S(2)}, u32[]{:S(2)}) %collective-permute-start.15) | collective-permute-done | bytes 3670048 | tf_op jit(solution)/shard_map/ppermute | solution.py:584
  321.0 42.3 %ffn_act.6 = (f32[5888,1792]{1,0:T(8,128)}, f32[5888,1792]{1,0:T(8,128)}, bf16[5888,1792]{1,0:T(8,128)(2,1)}) custom-call(bf16[5888,1024]{1,0:T(8,128)(2,1)} %pick_rows.6.x_ref, bf16[1024,1792]{1,0:T(8,128)(2,1)} %bitcast.16.refs_0_.refs_1_, bf16[1024,1792]{1,0:T(8,128)(2,1)} %bitcast.17.refs_1_.refs_2_, ...), custom_call_target="tpu_custom_call", output_to_operand_aliasing={{0}: (3, {}), {1}: (4, {}), {2}: (5, {})} | custom-call | flops 21609054208 | bytes 63766528 | tf_op jit(solution)/shard_map/ffn_act/pallas_call | solution.py:279
  363.3 17.9 %ffn_act.7 = (f32[1472,1792]{1,0:T(8,128)}, f32[1472,1792]{1,0:T(8,128)}, bf16[1472,1792]{1,0:T(8,128)(2,1)}) custom-call(bf16[5888,1024]{1,0:T(8,128)(2,1)} %pick_rows.6.x_ref, bf16[1024,1792]{1,0:T(8,128)(2,1)} %collective-permute-done.14.w1.refs_0_.refs_1_, bf16[1024,1792]{1,0:T(8,128)(2,1)} %collective-permute-done.15.w3.refs_1_.refs_2_), custom_call_target="tpu_custom_call" | custom-call | flops 10804527104 | bytes 37388288 | tf_op jit(solution)/shard_map/ffn_act/pallas_call | solution.py:279
  381.2 15.8 %collective-permute-done.16.w2.refs_0_ = bf16[1792,1024]{1,0:T(8,128)(2,1)} collective-permute-done((bf16[1792,1024]{1,0:T(8,128)(2,1)}, bf16[1792,1024]{1,0:T(8,128)(2,1)}, u32[]{:S(2)}, u32[]{:S(2)}) %collective-permute-start.16) | collective-permute-done | bytes 3670048 | tf_op jit(solution)/shard_map/ppermute | solution.py:584
  396.9 9.4 %ffn_down.3 = f32[1104,1024]{1,0:T(8,128)} custom-call(bf16[1472,1792]{1,0:T(8,128)(2,1)} %get-tuple-element.203.u_ref, bf16[1792,1024]{1,0:T(8,128)(2,1)} %collective-permute-done.16.w2.refs_0_, f32[2944,1024]{1,0:T(8,128)} %get-tuple-element.173.y_in), custom_call_target="tpu_custom_call" | custom-call | flops 4051697664 | bytes 12713984 | tf_op jit(solution)/shard_map/ffn_down/pallas_call | solution.py:299
  410.4 5.5 ffn_down.2
  417.2 20.5 %pick_rows.7.c_ref = bf16[5888,1024]{1,0:T(8,128)(2,1)} custom-call(s32[4]{0:T(128)} %pad_add_fusion.1.planes_ref, s32[8]{0:T(128)S(1)} %iota_xor_fusion.cols_ref, s32[4,8]{1,0:T(4,128)} %gather_fusion, bf16[4,512,1024]{2,1,0:T(8,128)(2,1)} %get-tuple-element.172.refs_0_, bf16[4,512,1024]{2,1,0:T(8,128)(2,1)} %collective-permute-done.6.refs_1_, ...), custom_call_target="tpu_custom_call" | custom-call | flops 7784628224 | bytes 67108864 | tf_op jit(solution)/shard_map/pick_rows/pallas_call | solution.py:225
  437.7 26.3 %ffn_grad.6 = (bf16[5888,1792]{1,0:T(8,128)(2,1)}, bf16[5888,1792]{1,0:T(8,128)(2,1)}, f32[1472,1024]{1,0:T(8,128)}) custom-call(bf16[5888,1024]{1,0:T(8,128)(2,1)} %pick_rows.7.c_ref, f32[5888,1792]{1,0:T(8,128)} %get-tuple-element.177.a_ref, f32[5888,1792]{1,0:T(8,128)} %get-tuple-element.178.b_ref, bf16[1792,1024]{1,0:T(8,128)(2,1)} %bitcast.156, ...), custom_call_target="tpu_custom_call" | custom-call | flops 16206790656 | bytes 42663936 | tf_op jit(solution)/shard_map/ffn_grad/pallas_call | solution.py:342
  464.0 26.3 %ffn_grad.7 = (bf16[5888,1792]{1,0:T(8,128)(2,1)}, bf16[5888,1792]{1,0:T(8,128)(2,1)}, f32[1472,1024]{1,0:T(8,128)}) custom-call(bf16[5888,1024]{1,0:T(8,128)(2,1)} %pick_rows.7.c_ref, f32[5888,1792]{1,0:T(8,128)} %get-tuple-element.177.a_ref, f32[5888,1792]{1,0:T(8,128)} %get-tuple-element.178.b_ref, ...), custom_call_target="tpu_custom_call", output_to_operand_aliasing={{0}: (6, {}), {1}: (7, {})} | custom-call | flops 16206790656 | bytes 42663936 | tf_op jit(solution)/shard_map/ffn_grad/pallas_call | solution.py:342
  490.3 41.5 %ffn_pair.1 = (f32[1472,1024]{1,0:T(8,128)}, f32[1472,1024]{1,0:T(8,128)}) custom-call(bf16[5888,1024]{1,0:T(8,128)(2,1)} %pick_rows.6.x_ref, bf16[5888,1024]{1,0:T(8,128)(2,1)} %pick_rows.7.c_ref, f32[2944,1024]{1,0:T(8,128)} %get-tuple-element.173.y_in, f32[1472,1024]{1,0:T(8,128)} %get-tuple-element.181.dx_in, ...), custom_call_target="tpu_custom_call" | custom-call | flops 32413581312 | bytes 41156608 | tf_op jit(solution)/shard_map/ffn_pair/pallas_call | solution.py:376
  531.8 30.8 %ffn_grad.8 = (bf16[5888,1792]{1,0:T(8,128)(2,1)}, bf16[5888,1792]{1,0:T(8,128)(2,1)}) custom-call(bf16[5888,1024]{1,0:T(8,128)(2,1)} %pick_rows.7.c_ref, f32[5888,1792]{1,0:T(8,128)} %get-tuple-element.177.a_ref, f32[5888,1792]{1,0:T(8,128)} %get-tuple-element.178.b_ref, ...), custom_call_target="tpu_custom_call", output_to_operand_aliasing={{0}: (4, {}), {1}: (5, {})} | custom-call | flops 10804527104 | bytes 74317824 | tf_op jit(solution)/shard_map/ffn_grad/pallas_call | solution.py:342
  562.7 30.0 %fusion.53 = f32[1024,1792]{1,0:T(8,128)} fusion(bf16[5888,1024]{1,0:T(8,128)(2,1)} %pick_rows.6.x_ref, bf16[5888,1792]{1,0:T(8,128)(2,1)} %get-tuple-element.189), kind=kOutput, calls=%fused_computation.144 | convolution fusion | flops 21609054208 | bytes 40501248 | tf_op jit(solution)/shard_map/dot_general | solution.py:31
  592.7 9.4 %home_blocks.1 = bf16[8,224,1024]{2,1,0:T(8,128)(2,1)} custom-call(s32[8]{0:T(128)} %fusion.45.start_ref, f32[1472,1024]{1,0:T(8,128)} %get-tuple-element.202.near_ref, f32[368,1024]{1,0:T(8,128)} %collective-permute-done.17.refs_0_, f32[1104,1024]{1,0:T(8,128)} %collective-permute-done.18.refs_1_, bf16[320,1024]{1,0:T(8,128)(2,1)S(1)} %copy-done.9), custom_call_target="tpu_custom_call" | custom-call | flops 851443712 | bytes 18087936 | tf_op jit(solution)/shard_map/home_blocks/pallas_call | solution.py:428
  602.1 4.5 all-to-all-start
  606.6 26.6 %ffn_grad.9 = f32[1472,1024]{1,0:T(8,128)} custom-call(bf16[5888,1024]{1,0:T(8,128)(2,1)} %pick_rows.7.c_ref, f32[1472,1792]{1,0:T(8,128)} %get-tuple-element.208.a_ref, f32[1472,1792]{1,0:T(8,128)} %get-tuple-element.209.b_ref, bf16[1792,1024]{1,0:T(8,128)(2,1)} %collective-permute-done.16.w2.refs_0_, ...), custom_call_target="tpu_custom_call" | custom-call | flops 16206790656 | bytes 42663936 | tf_op jit(solution)/shard_map/ffn_grad/pallas_call | solution.py:342
  635.7 29.5 %fusion.55 = f32[1792,1024]{1,0:T(8,128)} fusion(bf16[5888,1792]{1,0:T(8,128)(2,1)} %get-tuple-element.193, bf16[5888,1024]{1,0:T(8,128)(2,1)} %pick_rows.7.c_ref), kind=kOutput, calls=%fused_computation.146 | convolution fusion | flops 21609054208 | bytes 40501248 | tf_op jit(solution)/shard_map/dot_general | solution.py:31
  665.2 29.6 %fusion.54 = f32[1024,1792]{1,0:T(8,128)} fusion(bf16[5888,1024]{1,0:T(8,128)(2,1)} %pick_rows.6.x_ref, bf16[5888,1792]{1,0:T(8,128)(2,1)} %get-tuple-element.192), kind=kOutput, calls=%fused_computation.145 | convolution fusion | flops 21609054208 | bytes 40501248 | tf_op jit(solution)/shard_map/dot_general | solution.py:31
  710.8 56.0 %collective-permute-done.19.far_ref = f32[1472,1024]{1,0:T(8,128)} collective-permute-done((f32[1472,1024]{1,0:T(8,128)}, f32[1472,1024]{1,0:T(8,128)}, u32[]{:S(2)}, u32[]{:S(2)}) %collective-permute-start.19) | collective-permute-done | bytes 6029344 | tf_op jit(solution)/shard_map/ppermute | solution.py:584
  766.9 51.2 %return_rows.1 = (f32[512,1024]{1,0:T(8,128)S(1)}, f32[8,1024]{1,0:T(8,128)S(1)}) custom-call(s32[8]{0:T(128)S(1)} %copy-done.2, f32[1472,1024]{1,0:T(8,128)S(1)} %bitcast.151, f32[1472,1024]{1,0:T(8,128)} %collective-permute-done.19.far_ref, bf16[320,1024]{1,0:T(8,128)(2,1)} %get-tuple-element.211.more_ref, f32[8,1024]{1,0:T(8,128)S(1)} %fusion.48.part_ref, ...), custom_call_target="tpu_custom_call" | custom-call | flops 10000000000 | bytes 18087936 | tf_op jit(solution)/shard_map/return_rows/pallas_call | solution.py:527
  (147 shorter events, 67.1 us)
Async XLA Ops:
  4.1 153.1 %copy-start.13 = (s32[512,2]{0,1:T(2,128)S(1)}, s32[512,2]{0,1:T(2,128)}, u32[]{:S(2)}) copy-start(s32[512,2]{0,1:T(2,128)} %param.13) | copy-start | bytes 12292
  4.1 155.2 %copy-start.11 = (f32[1024,8]{0,1:T(8,128)S(1)}, f32[1024,8]{0,1:T(8,128)}, u32[]{:S(2)}) copy-start(f32[1024,8]{0,1:T(8,128)} %param.12) | copy-start | bytes 98308
  152.8 93.3 %collective-permute-start.9 = (bf16[4,512,1024]{2,1,0:T(8,128)(2,1)}, bf16[4,512,1024]{2,1,0:T(8,128)(2,1)}, u32[]{:S(2)}, u32[]{:S(2)}) collective-permute-start(bf16[4,512,1024]{2,1,0:T(8,128)(2,1)} %get-tuple-element.172.refs_0_), channel_id=1, source_target_pairs={{0,4},{1,5},{2,6},{3,7},{4,0},{5,1},{6,2},{7,3},{8,12},{9,13},{10,... | collective-permute-start | bytes 12582920 | tf_op jit(solution)/shard_map/ppermute | solution.py:595
  153.9 96.7 %collective-permute-start.7 = (bf16[4,512,1024]{2,1,0:T(8,128)(2,1)}, bf16[4,512,1024]{2,1,0:T(8,128)(2,1)}, u32[]{:S(2)}, u32[]{:S(2)}) collective-permute-start(bf16[4,512,1024]{2,1,0:T(8,128)(2,1)} %get-tuple-element.172.refs_0_), channel_id=1, source_target_pairs={{0,2},{1,3},{2,0},{3,1},{4,6},{5,7},{6,4},{7,5},{8,10},{9,11},{10,... | collective-permute-start | bytes 12582920 | tf_op jit(solution)/shard_map/ppermute | solution.py:595
  154.9 251.4 %collective-permute-start.6 = (bf16[4,512,1024]{2,1,0:T(8,128)(2,1)}, bf16[4,512,1024]{2,1,0:T(8,128)(2,1)}, u32[]{:S(2)}, u32[]{:S(2)}) collective-permute-start(bf16[4,512,1024]{2,1,0:T(8,128)(2,1)} %get-tuple-element.172.refs_0_), channel_id=1, source_target_pairs={{0,1},{1,0},{2,3},{3,2},{4,5},{5,4},{6,7},{7,6},{8,9},{9,8},{10,11... | collective-permute-start | bytes 12582920 | tf_op jit(solution)/shard_map/ppermute | solution.py:595
  154.9 149.0 %collective-permute-start.14 = (bf16[1024,1792]{1,0:T(8,128)(2,1)}, bf16[1024,1792]{1,0:T(8,128)(2,1)}, u32[]{:S(2)}, u32[]{:S(2)}) collective-permute-start(bf16[1024,1792]{1,0:T(8,128)(2,1)} %bitcast.16.refs_0_.refs_1_), channel_id=1, source_target_pairs={{0,8},{1,25},{2,10},{3,27},{4,12},{5,29},{6,14},{7,31},{8,0},{9,17... | collective-permute-start | bytes 11010056 | tf_op jit(solution)/shard_map/ppermute | solution.py:584
  157.2 158.6 %collective-permute-start.15 = (bf16[1024,1792]{1,0:T(8,128)(2,1)}, bf16[1024,1792]{1,0:T(8,128)(2,1)}, u32[]{:S(2)}, u32[]{:S(2)}) collective-permute-start(bf16[1024,1792]{1,0:T(8,128)(2,1)} %bitcast.17.refs_1_.refs_2_), channel_id=1, source_target_pairs={{0,8},{1,25},{2,10},{3,27},{4,12},{5,29},{6,14},{7,31},{8,0},{9,17... | collective-permute-start | bytes 11010056 | tf_op jit(solution)/shard_map/ppermute | solution.py:584
  157.2 43.2 %copy-start.16 = (s32[512,1]{0,1:T(1,128)}, s32[512,1]{0,1:T(1,128)S(1)}, u32[]{:S(2)}) copy-start(s32[512,1]{0,1:T(1,128)S(1)} %get-tuple-element.253) | copy-start | bytes 6148
  201.2 103.2 %copy-start.19 = (s32[512,1]{0,1:T(1,128)}, s32[512,1]{0,1:T(1,128)S(1)}, u32[]{:S(2)}) copy-start(s32[512,1]{0,1:T(1,128)S(1)} %get-tuple-element.251) | copy-start | bytes 6148
  201.3 103.2 %copy-start.21 = (s32[512,1]{0,1:T(1,128)}, s32[512,1]{0,1:T(1,128)S(1)}, u32[]{:S(2)}) copy-start(s32[512,1]{0,1:T(1,128)S(1)} %get-tuple-element.250) | copy-start | bytes 6148
  201.6 52.7 %copy-start.3 = (bf16[1,1792,1024]{2,1,0:T(8,128)(2,1)S(1)}, bf16[1,1792,1024]{2,1,0:T(8,128)(2,1)}, u32[]{:S(2)}) copy-start(bf16[1,1792,1024]{2,1,0:T(8,128)(2,1)} %param.17) | copy-start | bytes 11010052
  249.1 47.4 %collective-permute-start.11 = (bf16[2,512,1024]{2,1,0:T(8,128)(2,1)}, bf16[2,512,1024]{2,1,0:T(8,128)(2,1)}, u32[]{:S(2)}, u32[]{:S(2)}) collective-permute-start(bf16[2,512,1024]{2,1,0:T(8,128)(2,1)} %slice.53), channel_id=1, source_target_pairs={{0,2},{1,3},{2,0},{3,1},{4,6},{5,7},{6,4},{7,5},{8,10},{9,11},{10,... | collective-permute-start | bytes 6291464 | tf_op jit(solution)/shard_map/ppermute | solution.py:595
  253.7 47.1 %collective-permute-start.12 = (bf16[2,512,1024]{2,1,0:T(8,128)(2,1)}, bf16[2,512,1024]{2,1,0:T(8,128)(2,1)}, u32[]{:S(2)}, u32[]{:S(2)}) collective-permute-start(bf16[2,512,1024]{2,1,0:T(8,128)(2,1)} %slice.54), channel_id=1, source_target_pairs={{0,4},{1,5},{2,6},{3,7},{4,0},{5,1},{6,2},{7,3},{8,12},{9,13},{10,... | collective-permute-start | bytes 6291464 | tf_op jit(solution)/shard_map/ppermute | solution.py:595
  296.6 109.8 %collective-permute-start.10 = (bf16[4,512,1024]{2,1,0:T(8,128)(2,1)}, bf16[4,512,1024]{2,1,0:T(8,128)(2,1)}, u32[]{:S(2)}, u32[]{:S(2)}) collective-permute-start(bf16[4,512,1024]{2,1,0:T(8,128)(2,1)} %collective-permute-done.9.refs_4_), channel_id=1, source_target_pairs={{0,1},{1,0},{2,3},{3,2},{4,5},{5,4},{6,7},{7,6},{8,9},{9,8},{10,11... | collective-permute-start | bytes 12582920 | tf_op jit(solution)/shard_map/ppermute | solution.py:595
  300.8 105.5 %collective-permute-start.8 = (bf16[4,512,1024]{2,1,0:T(8,128)(2,1)}, bf16[4,512,1024]{2,1,0:T(8,128)(2,1)}, u32[]{:S(2)}, u32[]{:S(2)}) collective-permute-start(bf16[4,512,1024]{2,1,0:T(8,128)(2,1)} %collective-permute-done.7.refs_2_), channel_id=1, source_target_pairs={{0,1},{1,0},{2,3},{3,2},{4,5},{5,4},{6,7},{7,6},{8,9},{9,8},{10,11... | collective-permute-start | bytes 12582920 | tf_op jit(solution)/shard_map/ppermute | solution.py:595
  303.9 102.5 %collective-permute-start.13 = (bf16[4,512,1024]{2,1,0:T(8,128)(2,1)}, bf16[4,512,1024]{2,1,0:T(8,128)(2,1)}, u32[]{:S(2)}, u32[]{:S(2)}) collective-permute-start(bf16[4,512,1024]{2,1,0:T(8,128)(2,1)} %constant_dynamic-update-slice_fusion.refs_6_), channel_id=1, source_target_pairs={{0,1},{1,0},{2,3},{3,2},{4,5},{5,4},{6,7},{7,6},{8,9},{9,8},{10,11... | collective-permute-start | bytes 12582920 | tf_op jit(solution)/shard_map/ppermute | solution.py:595
  315.8 81.2 %collective-permute-start.16 = (bf16[1792,1024]{1,0:T(8,128)(2,1)}, bf16[1792,1024]{1,0:T(8,128)(2,1)}, u32[]{:S(2)}, u32[]{:S(2)}) collective-permute-start(bf16[1792,1024]{1,0:T(8,128)(2,1)} %bitcast.154), channel_id=1, source_target_pairs={{0,8},{1,25},{2,10},{3,27},{4,12},{5,29},{6,14},{7,31},{8,0},{9,17... | collective-permute-start | bytes 11010056 | tf_op jit(solution)/shard_map/ppermute | solution.py:584
  407.8 184.9 %collective-permute-start.18 = (f32[1104,1024]{1,0:T(8,128)}, f32[1104,1024]{1,0:T(8,128)}, u32[]{:S(2)}, u32[]{:S(2)}) collective-permute-start(f32[1104,1024]{1,0:T(8,128)} %ffn_down.3), channel_id=1, source_target_pairs={{0,24},{1,9},{2,26},{3,11},{4,28},{5,13},{6,30},{7,15},{8,16},{9,1... | collective-permute-start | bytes 13565960 | tf_op jit(solution)/shard_map/ppermute | solution.py:584
  415.9 176.8 %collective-permute-start.17 = (f32[368,1024]{1,0:T(8,128)}, f32[368,1024]{1,0:T(8,128)}, u32[]{:S(2)}, u32[]{:S(2)}) collective-permute-start(f32[368,1024]{1,0:T(8,128)} %ffn_down.2), channel_id=1, source_target_pairs={{0,24},{1,9},{2,26},{3,11},{4,28},{5,13},{6,30},{7,15},{8,16},{9,1... | collective-permute-start | bytes 4521992 | tf_op jit(solution)/shard_map/ppermute | solution.py:584
  602.1 92.8 %all-to-all-start = ((bf16[8,224,1024]{2,1,0:T(8,128)(2,1)}), bf16[8,224,1024]{2,1,0:T(8,128)(2,1)}, u32[]{:S(2)}, u32[]{:S(2)}) async-start(bf16[8,224,1024]{2,1,0:T(8,128)(2,1)} %home_blocks.1), calls=%async_computation | async-start | bytes 7340032 | tf_op jit(solution)/shard_map/all_to_all | solution.py:707
  633.2 133.7 %collective-permute-start.19 = (f32[1472,1024]{1,0:T(8,128)}, f32[1472,1024]{1,0:T(8,128)}, u32[]{:S(2)}, u32[]{:S(2)}) collective-permute-start(f32[1472,1024]{1,0:T(8,128)} %ffn_grad.9), channel_id=1, source_target_pairs={{0,24},{1,9},{2,26},{3,11},{4,28},{5,13},{6,30},{7,15},{8,16},{9,1... | collective-permute-start | bytes 18087944 | tf_op jit(solution)/shard_map/ppermute | solution.py:584
  695.5 71.4 %slice-start = ((s8[6029312]{0:T(1024)(128)(4,1)}), s8[4194304]{0:T(1024)(128)(4,1)S(1)}, s32[]{:S(2)}) async-start(s8[6029312]{0:T(1024)(128)(4,1)} %bitcast.150), calls=%async_computation.1 | async-start | bytes 8388608
  699.8 67.0 %slice-start.1 = ((s8[6029312]{0:T(1024)(128)(4,1)}), s8[1835008]{0:T(1024)(128)(4,1)S(1)}, s32[]{:S(2)}) async-start(s8[6029312]{0:T(1024)(128)(4,1)} %bitcast.150), calls=%async_computation.2 | async-start | bytes 3670016
  708.0 58.8 %copy-start.2 = (s32[8]{0:T(128)S(1)}, s32[8]{0:T(128)}, u32[]{:S(2)}) copy-start(s32[8]{0:T(128)} %fusion.45.start_ref) | copy-start | bytes 100
  (15 other events, 146.3 us)
